TPU v7x, 256 devices: a whole 4x4x8 slice. The times are simulated.
256 devices in a mesh: row: 16 (over z_lo, y), col: 16 (over z_hi, x, core).
Axes of the slice: x: 4, y: 4, z: 8 (z_hi: 2, z_lo: 4; z = z_hi * 4 + z_lo), core: 2. Of those that a mesh axis runs over, the one named last changes fastest.
Arguments:
- orbitals: float32 [2048, 28672], P(('row', 'col')), may hold values from -0.03125 to 0.03125
- applied: float32 [2048, 28672], P(('row', 'col')), may hold values from -24 to 24
Outputs:
- hamiltonian: float32 [2048, 2048], P('col', 'row')
- intersection: float32 [2048, 2048], P('col', 'row')
All inputs are finite; a program needn't handle non-finite values.
Results may differ from a plain program's by a relative error of at most 0.000098.
Values sent between devices are 32-bit elements; how exact they have to be, the bound alone decides.
No kernel may reach another device: no remote copies, remote signals or barrier semaphores. Data moves between devices by JAX's collectives and lax.ppermute only.
A program may use at most 64 MiB of HBM per device.

v0:
```python
import jax
import jax.numpy as jnp
from jax import lax
from jax.sharding import PartitionSpec as P


def sent_together(arrays, axis, dim, along):
    both = jnp.concatenate(arrays, axis=along)
    result, at, done = (lax.psum_scatter(both, axis, scatter_dimension=dim, tiled=True), 0, [])
    for a in arrays:
        done.append(lax.slice_in_dim(result, at, at + a.shape[along], axis=along))
        at += a.shape[along]
    return tuple(done)


def product(left, right):
    return lax.dot_general(
        left,
        right,
        (((1,), (1,)), ((), ())),
        precision=lax.Precision.HIGHEST,
        preferred_element_type=jnp.float32,
    )


def shards(orbitals, applied):
    mine_orb, mine_app = (
        lax.all_to_all(orbitals, "col", split_axis=1, concat_axis=0, tiled=True),
        lax.all_to_all(applied, "col", split_axis=1, concat_axis=0, tiled=True),
    )
    every_orb = lax.all_gather(mine_orb, "row", axis=0, tiled=True)
    ham_part = product(every_orb, mine_app)
    ovl_part = product(every_orb, mine_orb)
    hamiltonian, intersection = sent_together((ham_part, ovl_part), "col", 0, 1)
    return (hamiltonian, intersection)


def solution(mesh):
    placed = (P(("row", "col"), None), P(("row", "col"), None))
    return jax.shard_map(
        shards,
        mesh=mesh,
        in_specs=placed,
        out_specs=(P("col", "row"), P("col", "row")),
        check_vma=False,
    )
```

profile of v0, /device:TPU:8, one launch (start us, length us, event | category | flops | bytes accessed | tf_op | source)
XLA Modules:
  0.0 355.5 jit_solution(10867969578513426620)
XLA Ops:
  7.2 0.0 all-gather.2.cloned.1.call-start
  7.2 32.4 %all_to_all.38 = f32[8,16,1792]{2,0,1:T(8,128)} all-to-all(f32[8,16,1792]{2,0,1:T(8,128)} %bitcast.15), channel_id=1, replica_groups=mesh['row'=16,'col'=16] {'col'}, dimensions={1} | all-to-all | bytes 1835008 | tf_op jit(solution)/shard_map/all_to_all | solution.py:28
  39.6 0.0 all-gather.2.cloned.1.call-update
  39.7 3.6 %all-to-all-start.1 = ((f32[8,16,1792]{2,0,1:T(8,128)}), f32[8,16,1792]{2,0,1:T(8,128)S(1)}, u32[]{:S(2)}, u32[]{:S(2)}) async-start(f32[8,16,1792]{2,0,1:T(8,128)} %bitcast.16), calls=%async_computation.1 | async-start | bytes 1835008 | tf_op jit(solution)/shard_map/all_to_all | solution.py:29
  43.3 0.0 reduce-scatter.2.cloned.1.call-start
  43.4 173.2 %all-gather.2.cloned.1.call-done = f32[2048,1792]{1,0:T(8,128)} async-done(((f32[128,1792]{1,0:T(8,128)}), f32[2048,1792]{1,0:T(8,128)}) %all-gather.2.cloned.1.call-update) | async-done | bytes 14680080 | tf_op jit(solution)/shard_map/all_gather | solution.py:31
  216.6 18.5 %fusion.2 = f32[2048,128]{0,1:T(8,128)S(1)} fusion(f32[2048,1792]{1,0:T(8,128)} %all-gather.2.cloned.1.call-done, f32[8,16,1792]{2,0,1:T(8,128)} %all_to_all.38), kind=kOutput, calls=%fused_computation.3 | convolution fusion | flops 5637144576 | bytes 16646144 | tf_op jit(solution)/shard_map/dot_general | solution.py:17
  235.1 0.0 all-to-all-done.1
  235.2 18.3 %fusion = f32[2048,128]{0,1:T(8,128)S(1)} fusion(f32[2048,1792]{1,0:T(8,128)} %all-gather.2.cloned.1.call-done, f32[8,16,1792]{2,0,1:T(8,128)S(1)} %all-to-all-done.1), kind=kOutput, calls=%fused_computation.1 | convolution fusion | flops 5637144576 | bytes 16646144 | tf_op jit(solution)/shard_map/dot_general | solution.py:17
  253.5 1.5 pad_maximum_fusion
  255.0 0.0 reduce-scatter.2.cloned.1.call-update
  255.0 91.3 %reduce-scatter.2.cloned.1.call-done = f32[128,256]{0,1:T(8,128)} async-done(((f32[2048,256]{0,1:T(8,128)}), f32[128,256]{0,1:T(8,128)}) %reduce-scatter.2.cloned.1.call-update) | async-done | bytes 131088 | tf_op jit(solution)/shard_map/reduce_scatter | solution.py:9
  346.4 0.9 fusion.4
  347.2 0.7 copy.5
  348.0 0.7 copy.4
Async XLA Ops:
  7.2 209.5 %all-gather.2.cloned.1.call-start = ((), (), s32[]{:S(2)}) async-start(), calls=%async_computation.3 | async-start | bytes 15597568 | tf_op jit(solution)/shard_map/all_gather | solution.py:31
  39.7 195.5 %all-to-all-start.1 = ((f32[8,16,1792]{2,0,1:T(8,128)}), f32[8,16,1792]{2,0,1:T(8,128)S(1)}, u32[]{:S(2)}, u32[]{:S(2)}) async-start(f32[8,16,1792]{2,0,1:T(8,128)} %bitcast.16), calls=%async_computation.1 | async-start | bytes 1835008 | tf_op jit(solution)/shard_map/all_to_all | solution.py:29
  43.3 303.0 %reduce-scatter.2.cloned.1.call-start = ((), (), s32[]{:S(2)}) async-start(), calls=%async_computation.4 | async-start | bytes 2228224 | tf_op jit(solution)/shard_map/reduce_scatter | solution.py:9
Sparse Core Ops, SparseCore 0:
  39.8 176.7 all-gather.1
  255.1 91.1 reduce-scatter.1
where the time goes:
time: 356 us
  waiting for transfers between devices  265 us (74%)
  matrix products  36.8 us (10%)
  blocking collectives  32.4 us (9%)
  between operations  14.1 us (4%)
  starting transfers between devices  3.73 us (1%)
    all_gather x1, waiting for transfers between devices, shards(): every_orb = lax.all_gather(mine_orb, 'row', axis=0, tiled=True)  173 us
    reduce_scatter x1, waiting for transfers between devices, sent_together(): lax.psum_scatter(both, axis, scatter_dimension=dim, tiled=True)  91.3 us
    dot_general x2, matrix products, product(): lax.dot_general(left, right, (((1,), (1,)), ((), ())), precision=lax.Prec...  36.8 us
    all_to_all x1, blocking collectives, shards(): lax.all_to_all(orbitals, 'col', split_axis=1, concat_axis=0, tiled=True)  32.4 us
  transfers between devices with their start and end apart: 3, of which 2 were waited for; matrix products, arithmetic and copies ran while one was open for 5% of the time, Pallas kernels for 0%

commit v1 on v0

v1 whole, which is shorter than its diff:
```python
import jax
import jax.numpy as jnp
from jax import lax
from jax.sharding import Mesh, PartitionSpec as P

AXES = ("zlo", "y", "zhi", "x", "core")
Z = ("zlo", "zhi")
CHUNKS = 2


def z_ring(step):
    place = lambda z: (z % 4) * 2 + z // 4
    return [(place(z), place((z + step) % 8)) for z in range(8)]


def product(left, right):
    return lax.dot_general(
        left,
        right,
        (((1,), (1,)), ((), ())),
        precision=lax.Precision.HIGH,
        preferred_element_type=jnp.float32,
    )


def both_cores(mine, core):
    other = lax.ppermute(mine, "core", [(0, 1), (1, 0)])
    k = mine.shape[-1]
    mine, other = mine.reshape(4, 4, 1, 8, k), other.reshape(4, 4, 1, 8, k)
    first = core == 0
    return jnp.concatenate([jnp.where(first, mine, other), jnp.where(first, other, mine)], 2)


def body(orbitals, applied):
    core = lax.axis_index("core")
    z = lax.axis_index("zhi") * 4 + lax.axis_index("zlo")
    width = orbitals.shape[1] // CHUNKS

    def spread(a, c):
        piece = lax.slice_in_dim(a, c * width, (c + 1) * width, axis=1)
        return lax.all_to_all(piece, ("y", "x"), split_axis=1, concat_axis=0, tiled=True)

    orb = [both_cores(spread(orbitals, c), core) for c in range(CHUNKS)]
    k = width // 16
    blocks = []
    for o in orb:
        half = lax.dynamic_index_in_dim(o.reshape(2, 2, 64, k), core, axis=1, keepdims=False)
        blocks.append(half.reshape(128, k))
    app = [both_cores(spread(applied, c), core) for c in range(CHUNKS)]
    own = [
        jnp.stack([a.reshape(4, 64, k), o.reshape(4, 64, k)], 1).reshape(512, k)
        for a, o in zip(app, orb)
    ]

    held = {(0, c): blocks[c] for c in range(CHUNKS)}
    for d in range(1, 5):
        for c in range(CHUNKS):
            if d < 4 or c == 0:
                held[(d, c)] = lax.ppermute(held[(d - 1, c)], Z, z_ring(-1))
            if d < 4 or c == 1:
                got = lax.ppermute(held[((1 - d) % 8, c)], Z, z_ring(1))
                held[(-d % 8, c)] = got
    parts = []
    for d in range(8):
        parts.append(sum(product(held[(d, c)], own[c]) for c in range(CHUNKS)))
    part = jnp.stack(parts).reshape(8, 128, 4, 128)

    part = jnp.transpose(part, (2, 0, 1, 3))
    got = lax.all_to_all(part, "y", split_axis=0, concat_axis=0, tiled=True)
    part = got.sum(0)
    part = jnp.roll(part, z, axis=0)
    part = part.reshape(2, 2, 2, 2, 64, 128)
    part = jnp.transpose(part, (1, 2, 3, 0, 4, 5)).reshape(8, 2, 64, 128)
    got = lax.all_to_all(part, ("zhi", "x"), split_axis=0, concat_axis=0, tiled=True)
    tile = got.reshape(2, 4, 2, 64, 2, 64).sum(1)
    tile = jnp.transpose(tile, (3, 1, 2, 0, 4)).reshape(2, 128, 128)
    return tile[0], tile[1]


def solution(mesh):
    fine = Mesh(mesh.devices.reshape(4, 4, 2, 4, 2), AXES)
    placed = P(AXES, None)
    out = P(("zhi", "x", "core"), ("zlo", "y"))
    return jax.shard_map(
        body, mesh=fine, in_specs=(placed, placed), out_specs=(out, out), check_vma=False
    )
```

time: 356 us -> 209 us (0.59)
  waiting for transfers between devices: 265 us -> 86.5 us
  starting transfers between devices: 3.73 us -> 45.5 us
  between operations: 14.1 us -> 1.07 us
  local copies, waits for them, and re-layouts: 2.34 us -> 14.1 us
  matrix products: 36.8 us -> 27.1 us
    all_gather x1 -> x0, waiting for transfers between devices: 173 us -> none  [shards(): every_orb = lax.all_gather(mine_orb, 'row', axis=0, tiled=True)]
    reduce_scatter x1 -> x0, waiting for transfers between devices: 91.3 us -> none  [sent_together(): lax.psum_scatter(both, axis, scatter_dimension=dim, tiled=True)]
    ppermute x0 -> x18, waiting for transfers between devices: none -> 43.6 us  [the longest x7 31.8 us: body(): held[d, c] = lax.ppermute(held[d - 1, c], Z, z_ring(-1))]
    all_to_all x1 -> x4, waiting for transfers between devices: 0.01 us -> 42.8 us  [the longest x1 21.5 us: body(): got = lax.all_to_all(part, 'y', split_axis=0, concat_axis=0, tiled=True)]
    ppermute x0 -> x18, starting transfers between devices: none -> 22.3 us  [the longest x7 17.4 us: body(): held[d, c] = lax.ppermute(held[d - 1, c], Z, z_ring(-1))]
    all_to_all x1 -> x4, starting transfers between devices: 3.65 us -> 23.2 us  [the longest x3 17.3 us: spread(): lax.all_to_all(piece, ('y', 'x'), split_axis=1, concat_axis=0, tiled=True)]
    dot_general x2 -> x16, matrix products: 36.8 us -> 27.1 us  [product(): lax.dot_general(left, right, (((1,), (1,)), ((), ())), precision=lax.Prec...]
    unnamed x2 -> x29, local copies, waits for them, and re-layouts: 1.46 us -> 6.66 us
  transfers between devices with their start and end apart: 3 -> 22, of which waited for: 2 -> 14; matrix products, arithmetic and copies ran while one was open for 5% -> 15% of each run, Pallas kernels for 0% -> 0%
where the time goes in v1:
time: 209 us; the launch traced here: 208 us
  waiting for transfers between devices  86.5 us (41%)
  starting transfers between devices  45.5 us (22%)
  blocking collectives  31.8 us (15%)
  matrix products  27.1 us (13%)
  local copies, waits for them, and re-layouts  14.1 us (7%)
    ppermute x7, waiting for transfers between devices, body(): held[d, c] = lax.ppermute(held[d - 1, c], Z, z_ring(-1))  31.8 us
    dot_general x16, matrix products, product(): lax.dot_general(left, right, (((1,), (1,)), ((), ())), precision=lax.Prec...  27.1 us
    all_to_all x1, waiting for transfers between devices, body(): got = lax.all_to_all(part, 'y', split_axis=0, concat_axis=0, tiled=True)  21.5 us
    all_to_all x3, waiting for transfers between devices, spread(): lax.all_to_all(piece, ('y', 'x'), split_axis=1, concat_axis=0, tiled=True)  21.4 us
    ppermute x7, starting transfers between devices, body(): held[d, c] = lax.ppermute(held[d - 1, c], Z, z_ring(-1))  17.4 us
    all_to_all x3, starting transfers between devices, spread(): lax.all_to_all(piece, ('y', 'x'), split_axis=1, concat_axis=0, tiled=True)  17.3 us
    all_to_all x1, blocking collectives, body(): lax.all_to_all(part, ('zhi', 'x'), split_axis=0, concat_axis=0, tiled=True)  16.2 us
    all_to_all x1, blocking collectives, spread(): lax.all_to_all(piece, ('y', 'x'), split_axis=1, concat_axis=0, tiled=True)  15.6 us
  transfers between devices with their start and end apart: 22, of which 14 were waited for; matrix products, arithmetic and copies ran while one was open for 15% of the time, Pallas kernels for 0%

profile of v1, /device:TPU:8, one launch (start us, length us, event | category | flops | bytes accessed | tf_op | source)
XLA Modules:
  0.0 208.0 jit_solution(8067996328030365672)
XLA Ops:
  0.6 2.1 fusion.2
  2.7 15.6 %all_to_all.86 = f32[8,16,896]{2,0,1:T(8,128)S(1)} all-to-all(f32[8,16,896]{2,0,1:T(8,128)S(1)} %bitcast.106), channel_id=1, replica_groups=mesh['zlo'=4,'y'=4,'zhi'=2,'x'=4,'core'=2] {'y','x'}, dimensions={1} | all-to-all | bytes 917504 | tf_op jit(solution)/shard_map/all_to_all | solution.py:41
  18.3 5.9 %all-to-all-start.2 = ((f32[8,16,896]{2,0,1:T(8,128)}), f32[8,16,896]{2,0,1:T(8,128)S(1)}, u32[]{:S(2)}, u32[]{:S(2)}) async-start(f32[8,16,896]{2,0,1:T(8,128)} %bitcast.17), calls=%async_computation.2 | async-start | bytes 917504 | tf_op jit(solution)/shard_map/all_to_all | solution.py:41
  25.2 6.8 %all-to-all-done.2 = f32[8,16,896]{2,0,1:T(8,128)S(1)} async-done(((f32[8,16,896]{2,0,1:T(8,128)}), f32[8,16,896]{2,0,1:T(8,128)S(1)}, u32[]{:S(2)}, u32[]{:S(2)}) %all-to-all-start.2) | async-done | bytes 458784 | tf_op jit(solution)/shard_map/all_to_all | solution.py:41
  32.0 5.7 %all-to-all-start.3 = ((f32[8,16,896]{2,0,1:T(8,128)}), f32[8,16,896]{2,0,1:T(8,128)S(1)}, u32[]{:S(2)}, u32[]{:S(2)}) async-start(f32[8,16,896]{2,0,1:T(8,128)} %bitcast.25), calls=%async_computation.3 | async-start | bytes 917504 | tf_op jit(solution)/shard_map/all_to_all | solution.py:41
  37.7 7.5 %all-to-all-done.3 = f32[8,16,896]{2,0,1:T(8,128)S(1)} async-done(((f32[8,16,896]{2,0,1:T(8,128)}), f32[8,16,896]{2,0,1:T(8,128)S(1)}, u32[]{:S(2)}, u32[]{:S(2)}) %all-to-all-start.3) | async-done | bytes 458784 | tf_op jit(solution)/shard_map/all_to_all | solution.py:41
  45.2 5.7 %all-to-all-start.1 = ((f32[8,16,896]{2,0,1:T(8,128)}), f32[8,16,896]{2,0,1:T(8,128)S(1)}, u32[]{:S(2)}, u32[]{:S(2)}) async-start(f32[8,16,896]{2,0,1:T(8,128)} %bitcast.8), calls=%async_computation.1 | async-start | bytes 917504 | tf_op jit(solution)/shard_map/all_to_all | solution.py:41
  51.4 7.0 %all-to-all-done.1 = f32[8,16,896]{2,0,1:T(8,128)S(1)} async-done(((f32[8,16,896]{2,0,1:T(8,128)}), f32[8,16,896]{2,0,1:T(8,128)S(1)}, u32[]{:S(2)}, u32[]{:S(2)}) %all-to-all-start.1) | async-done | bytes 458784 | tf_op jit(solution)/shard_map/all_to_all | solution.py:41
  58.7 5.9 %collective-permute-start.5 = (f32[128,896]{1,0:T(8,128)S(1)}, f32[128,896]{1,0:T(8,128)}, u32[]{:S(2)}, u32[]{:S(2)}) collective-permute-start(f32[128,896]{1,0:T(8,128)S(1)} %bitcast.113), channel_id=1, source_target_pairs={{0,200},{64,0},{128,64},{192,128},{8,192},{72,8},{136,72},{200,136... | collective-permute-start | bytes 1376264 | tf_op jit(solution)/shard_map/ppermute | solution.py:59
  64.8 3.3 %collective-permute-start.4 = (f32[128,896]{1,0:T(8,128)S(1)}, f32[128,896]{1,0:T(8,128)}, u32[]{:S(2)}, u32[]{:S(2)}) collective-permute-start(f32[128,896]{1,0:T(8,128)S(1)} %bitcast.103), channel_id=1, source_target_pairs={{0,200},{64,0},{128,64},{192,128},{8,192},{72,8},{136,72},{200,136... | collective-permute-start | bytes 1376264 | tf_op jit(solution)/shard_map/ppermute | solution.py:59
  72.1 3.4 %collective-permute-done.5 = f32[128,896]{1,0:T(8,128)} collective-permute-done((f32[128,896]{1,0:T(8,128)S(1)}, f32[128,896]{1,0:T(8,128)}, u32[]{:S(2)}, u32[]{:S(2)}) %collective-permute-start.5) | collective-permute-done | bytes 458784 | tf_op jit(solution)/shard_map/ppermute | solution.py:59
  75.5 2.1 fusion.5
  77.6 7.3 %collective-permute-done.4 = f32[128,896]{1,0:T(8,128)} collective-permute-done((f32[128,896]{1,0:T(8,128)S(1)}, f32[128,896]{1,0:T(8,128)}, u32[]{:S(2)}, u32[]{:S(2)}) %collective-permute-start.4) | collective-permute-done | bytes 458784 | tf_op jit(solution)/shard_map/ppermute | solution.py:59
  84.9 2.1 convolution_add_fusion.6
  87.1 4.1 %collective-permute-start.7 = (f32[128,896]{1,0:T(8,128)}, f32[128,896]{1,0:T(8,128)}, u32[]{:S(2)}, u32[]{:S(2)}) collective-permute-start(f32[128,896]{1,0:T(8,128)} %collective-permute-done.5), channel_id=1, source_target_pairs={{0,200},{64,0},{128,64},{192,128},{8,192},{72,8},{136,72},{200,136... | collective-permute-start | bytes 1376264 | tf_op jit(solution)/shard_map/ppermute | solution.py:59
  93.2 2.1 convolution_add_fusion
  98.2 4.1 %collective-permute-done.7 = f32[128,896]{1,0:T(8,128)} collective-permute-done((f32[128,896]{1,0:T(8,128)}, f32[128,896]{1,0:T(8,128)}, u32[]{:S(2)}, u32[]{:S(2)}) %collective-permute-start.7) | collective-permute-done | bytes 458784 | tf_op jit(solution)/shard_map/ppermute | solution.py:59
  102.3 2.1 fusion.6
  104.4 6.4 %collective-permute-done.6 = f32[128,896]{1,0:T(8,128)S(1)} collective-permute-done((f32[128,896]{1,0:T(8,128)}, f32[128,896]{1,0:T(8,128)S(1)}, u32[]{:S(2)}, u32[]{:S(2)}) %collective-permute-start.6) | collective-permute-done | bytes 458784 | tf_op jit(solution)/shard_map/ppermute | solution.py:59
  112.8 3.7 %collective-permute-start.9 = (f32[128,896]{1,0:T(8,128)}, f32[128,896]{1,0:T(8,128)}, u32[]{:S(2)}, u32[]{:S(2)}) collective-permute-start(f32[128,896]{1,0:T(8,128)} %collective-permute-done.7), channel_id=1, source_target_pairs={{0,200},{64,0},{128,64},{192,128},{8,192},{72,8},{136,72},{200,136... | collective-permute-start | bytes 1376264 | tf_op jit(solution)/shard_map/ppermute | solution.py:59
  118.8 2.1 convolution_add_fusion.1
  124.2 3.5 %collective-permute-done.9 = f32[128,896]{1,0:T(8,128)} collective-permute-done((f32[128,896]{1,0:T(8,128)}, f32[128,896]{1,0:T(8,128)}, u32[]{:S(2)}, u32[]{:S(2)}) %collective-permute-start.9) | collective-permute-done | bytes 458784 | tf_op jit(solution)/shard_map/ppermute | solution.py:59
  127.7 2.1 fusion.7
  129.8 5.6 %collective-permute-done.8 = f32[128,896]{1,0:T(8,128)S(1)} collective-permute-done((f32[128,896]{1,0:T(8,128)}, f32[128,896]{1,0:T(8,128)S(1)}, u32[]{:S(2)}, u32[]{:S(2)}) %collective-permute-start.8) | collective-permute-done | bytes 458784 | tf_op jit(solution)/shard_map/ppermute | solution.py:59
  137.4 2.2 %fusion.9 = f32[128,512]{1,0:T(8,128)S(1)} fusion(f32[128,896]{1,0:T(8,128)} %collective-permute-done.13, f32[512,896]{1,0:T(8,128)S(1)} %bitcast.85), kind=kOutput, calls=%fused_computation.43 | convolution fusion | flops 352321536 | bytes 2555904 | tf_op jit(solution)/shard_map/dot_general | solution.py:17
  139.6 6.1 %collective-permute-done.17 = f32[128,896]{1,0:T(8,128)} collective-permute-done((f32[128,896]{1,0:T(8,128)}, f32[128,896]{1,0:T(8,128)}, u32[]{:S(2)}, u32[]{:S(2)}) %collective-permute-start.17) | collective-permute-done | bytes 458784 | tf_op jit(solution)/shard_map/ppermute | solution.py:61
  145.7 2.1 convolution_add_fusion.2
  148.7 4.4 %collective-permute-done.14 = f32[128,896]{1,0:T(8,128)} collective-permute-done((f32[128,896]{1,0:T(8,128)}, f32[128,896]{1,0:T(8,128)}, u32[]{:S(2)}, u32[]{:S(2)}) %collective-permute-start.14) | collective-permute-done | bytes 458784 | tf_op jit(solution)/shard_map/ppermute | solution.py:61
  153.1 2.1 fusion.8
  160.7 6.0 %all-to-all-start.4 = ((f32[4,8,128,128]{3,2,1,0:T(8,128)}), f32[4,8,128,128]{3,2,1,0:T(8,128)S(1)}, u32[]{:S(2)}, u32[]{:S(2)}) async-start(f32[4,8,128,128]{3,2,1,0:T(8,128)} %bitcast.101), calls=%async_computation.4 | async-start | bytes 4194304 | tf_op jit(solution)/shard_map/all_to_all | solution.py:69
  166.6 21.5 %all-to-all-done.4 = f32[4,8,128,128]{3,2,1,0:T(8,128)S(1)} async-done(((f32[4,8,128,128]{3,2,1,0:T(8,128)}), f32[4,8,128,128]{3,2,1,0:T(8,128)S(1)}, u32[]{:S(2)}, u32[]{:S(2)}) %all-to-all-start.4) | async-done | bytes 2097184 | tf_op jit(solution)/shard_map/all_to_all | solution.py:69
  188.4 16.2 %all_to_all.87 = f32[8,2,64,128]{3,2,1,0:T(8,128)S(1)} all-to-all(f32[8,2,64,128]{3,2,1,0:T(8,128)S(1)} %copy.48), channel_id=1, replica_groups=mesh['zlo'=4,'y'=4,'zhi'=2,'x'=4,'core'=2] {'zhi','x'}, dimensions={0} | all-to-all | bytes 1048576 | tf_op jit(solution)/shard_map/all_to_all | solution.py:74
  (93 shorter events, 30.5 us)
Async XLA Ops:
  0.6 23.5 %copy-start.8 = (f32[8,28672]{1,0:T(8,128)S(1)}, f32[8,28672]{1,0:T(8,128)}, u32[]{:S(2)}) copy-start(f32[8,28672]{1,0:T(8,128)} %param.3) | copy-start | bytes 2752516
  18.3 13.7 %all-to-all-start.2 = ((f32[8,16,896]{2,0,1:T(8,128)}), f32[8,16,896]{2,0,1:T(8,128)S(1)}, u32[]{:S(2)}, u32[]{:S(2)}) async-start(f32[8,16,896]{2,0,1:T(8,128)} %bitcast.17), calls=%async_computation.2 | async-start | bytes 917504 | tf_op jit(solution)/shard_map/all_to_all | solution.py:41
  32.0 13.2 %all-to-all-start.3 = ((f32[8,16,896]{2,0,1:T(8,128)}), f32[8,16,896]{2,0,1:T(8,128)S(1)}, u32[]{:S(2)}, u32[]{:S(2)}) async-start(f32[8,16,896]{2,0,1:T(8,128)} %bitcast.25), calls=%async_computation.3 | async-start | bytes 917504 | tf_op jit(solution)/shard_map/all_to_all | solution.py:41
  37.6 20.8 %collective-permute-start.2 = (f32[128,896]{1,0:T(8,128)S(1)}, f32[128,896]{1,0:T(8,128)S(1)}, u32[]{:S(2)}, u32[]{:S(2)}) collective-permute-start(f32[128,896]{1,0:T(8,128)S(1)} %bitcast.116), channel_id=1, source_target_pairs={{0,1},{1,0},{2,3},{3,2},{4,5},{5,4},{6,7},{7,6},{8,9},{9,8},{10,11... | collective-permute-start | bytes 1376264 | tf_op jit(solution)/shard_map/ppermute | solution.py:27
  45.2 13.3 %all-to-all-start.1 = ((f32[8,16,896]{2,0,1:T(8,128)}), f32[8,16,896]{2,0,1:T(8,128)S(1)}, u32[]{:S(2)}, u32[]{:S(2)}) async-start(f32[8,16,896]{2,0,1:T(8,128)} %bitcast.8), calls=%async_computation.1 | async-start | bytes 917504 | tf_op jit(solution)/shard_map/all_to_all | solution.py:41
  50.9 13.7 %collective-permute-start = (f32[128,896]{1,0:T(8,128)S(1)}, f32[128,896]{1,0:T(8,128)S(1)}, u32[]{:S(2)}, u32[]{:S(2)}) collective-permute-start(f32[128,896]{1,0:T(8,128)S(1)} %bitcast.109), channel_id=1, source_target_pairs={{0,1},{1,0},{2,3},{3,2},{4,5},{5,4},{6,7},{7,6},{8,9},{9,8},{10,11... | collective-permute-start | bytes 1376264 | tf_op jit(solution)/shard_map/ppermute | solution.py:27
  50.9 17.2 %collective-permute-start.3 = (f32[128,896]{1,0:T(8,128)S(1)}, f32[128,896]{1,0:T(8,128)S(1)}, u32[]{:S(2)}, u32[]{:S(2)}) collective-permute-start(f32[128,896]{1,0:T(8,128)S(1)} %bitcast.107), channel_id=1, source_target_pairs={{0,1},{1,0},{2,3},{3,2},{4,5},{5,4},{6,7},{7,6},{8,9},{9,8},{10,11... | collective-permute-start | bytes 1376264 | tf_op jit(solution)/shard_map/ppermute | solution.py:27
  58.5 9.7 %collective-permute-start.1 = (f32[128,896]{1,0:T(8,128)S(1)}, f32[128,896]{1,0:T(8,128)S(1)}, u32[]{:S(2)}, u32[]{:S(2)}) collective-permute-start(f32[128,896]{1,0:T(8,128)S(1)} %bitcast.111), channel_id=1, source_target_pairs={{0,1},{1,0},{2,3},{3,2},{4,5},{5,4},{6,7},{7,6},{8,9},{9,8},{10,11... | collective-permute-start | bytes 1376264 | tf_op jit(solution)/shard_map/ppermute | solution.py:27
  58.7 16.8 %collective-permute-start.5 = (f32[128,896]{1,0:T(8,128)S(1)}, f32[128,896]{1,0:T(8,128)}, u32[]{:S(2)}, u32[]{:S(2)}) collective-permute-start(f32[128,896]{1,0:T(8,128)S(1)} %bitcast.113), channel_id=1, source_target_pairs={{0,200},{64,0},{128,64},{192,128},{8,192},{72,8},{136,72},{200,136... | collective-permute-start | bytes 1376264 | tf_op jit(solution)/shard_map/ppermute | solution.py:59
  64.6 26.5 %collective-permute-start.11 = (f32[128,896]{1,0:T(8,128)S(1)}, f32[128,896]{1,0:T(8,128)}, u32[]{:S(2)}, u32[]{:S(2)}) collective-permute-start(f32[128,896]{1,0:T(8,128)S(1)} %bitcast.114), channel_id=1, source_target_pairs={{0,64},{64,128},{128,192},{192,8},{8,72},{72,136},{136,200},{200,0... | collective-permute-start | bytes 1376264 | tf_op jit(solution)/shard_map/ppermute | solution.py:61
  64.8 20.1 %collective-permute-start.4 = (f32[128,896]{1,0:T(8,128)S(1)}, f32[128,896]{1,0:T(8,128)}, u32[]{:S(2)}, u32[]{:S(2)}) collective-permute-start(f32[128,896]{1,0:T(8,128)S(1)} %bitcast.103), channel_id=1, source_target_pairs={{0,200},{64,0},{128,64},{192,128},{8,192},{72,8},{136,72},{200,136... | collective-permute-start | bytes 1376264 | tf_op jit(solution)/shard_map/ppermute | solution.py:59
  68.1 25.1 %collective-permute-start.15 = (f32[128,896]{1,0:T(8,128)S(1)}, f32[128,896]{1,0:T(8,128)}, u32[]{:S(2)}, u32[]{:S(2)}) collective-permute-start(f32[128,896]{1,0:T(8,128)S(1)} %bitcast.104), channel_id=1, source_target_pairs={{0,64},{64,128},{128,192},{192,8},{8,72},{72,136},{136,200},{200,0... | collective-permute-start | bytes 1376264 | tf_op jit(solution)/shard_map/ppermute | solution.py:61
  68.7 1.2 copy-start
  71.4 13.5 %copy-start.1 = (f32[4,2,64,896]{3,2,1,0:T(8,128)S(1)}, f32[4,2,64,896]{3,2,1,0:T(8,128)}, u32[]{:S(2)}) copy-start(f32[4,2,64,896]{3,2,1,0:T(8,128)} %copy-done) | copy-start | bytes 5505028
  87.1 6.1 %copy-start.2 = (f32[4,2,64,896]{3,2,1,0:T(8,128)S(1)}, f32[4,2,64,896]{3,2,1,0:T(8,128)}, u32[]{:S(2)}) copy-start(f32[4,2,64,896]{3,2,1,0:T(8,128)} %copy-done) | copy-start | bytes 5505028
  87.1 15.3 %collective-permute-start.7 = (f32[128,896]{1,0:T(8,128)}, f32[128,896]{1,0:T(8,128)}, u32[]{:S(2)}, u32[]{:S(2)}) collective-permute-start(f32[128,896]{1,0:T(8,128)} %collective-permute-done.5), channel_id=1, source_target_pairs={{0,200},{64,0},{128,64},{192,128},{8,192},{72,8},{136,72},{200,136... | collective-permute-start | bytes 1376264 | tf_op jit(solution)/shard_map/ppermute | solution.py:59
  95.4 16.2 %copy-start.3 = (f32[4,2,64,896]{3,2,1,0:T(8,128)S(1)}, f32[4,2,64,896]{3,2,1,0:T(8,128)}, u32[]{:S(2)}) copy-start(f32[4,2,64,896]{3,2,1,0:T(8,128)} %copy-done) | copy-start | bytes 5505028
  95.4 15.5 %collective-permute-start.6 = (f32[128,896]{1,0:T(8,128)}, f32[128,896]{1,0:T(8,128)S(1)}, u32[]{:S(2)}, u32[]{:S(2)}) collective-permute-start(f32[128,896]{1,0:T(8,128)} %collective-permute-done.4), channel_id=1, source_target_pairs={{0,200},{64,0},{128,64},{192,128},{8,192},{72,8},{136,72},{200,136... | collective-permute-start | bytes 1376264 | tf_op jit(solution)/shard_map/ppermute | solution.py:59
  95.6 20.8 %collective-permute-start.12 = (f32[128,896]{1,0:T(8,128)}, f32[128,896]{1,0:T(8,128)S(1)}, u32[]{:S(2)}, u32[]{:S(2)}) collective-permute-start(f32[128,896]{1,0:T(8,128)} %collective-permute-done.11), channel_id=1, source_target_pairs={{0,64},{64,128},{128,192},{192,8},{8,72},{72,136},{136,200},{200,0... | collective-permute-start | bytes 1376264 | tf_op jit(solution)/shard_map/ppermute | solution.py:61
  97.5 21.3 %collective-permute-start.16 = (f32[128,896]{1,0:T(8,128)}, f32[128,896]{1,0:T(8,128)}, u32[]{:S(2)}, u32[]{:S(2)}) collective-permute-start(f32[128,896]{1,0:T(8,128)} %collective-permute-done.15), channel_id=1, source_target_pairs={{0,64},{64,128},{128,192},{192,8},{8,72},{72,136},{136,200},{200,0... | collective-permute-start | bytes 1376264 | tf_op jit(solution)/shard_map/ppermute | solution.py:61
  112.8 6.0 %copy-start.4 = (f32[4,2,64,896]{3,2,1,0:T(8,128)S(1)}, f32[4,2,64,896]{3,2,1,0:T(8,128)}, u32[]{:S(2)}) copy-start(f32[4,2,64,896]{3,2,1,0:T(8,128)} %copy-done) | copy-start | bytes 5505028
  112.8 14.9 %collective-permute-start.9 = (f32[128,896]{1,0:T(8,128)}, f32[128,896]{1,0:T(8,128)}, u32[]{:S(2)}, u32[]{:S(2)}) collective-permute-start(f32[128,896]{1,0:T(8,128)} %collective-permute-done.7), channel_id=1, source_target_pairs={{0,200},{64,0},{128,64},{192,128},{8,192},{72,8},{136,72},{200,136... | collective-permute-start | bytes 1376264 | tf_op jit(solution)/shard_map/ppermute | solution.py:59
  121.0 15.2 %copy-start.5 = (f32[4,2,64,896]{3,2,1,0:T(8,128)S(1)}, f32[4,2,64,896]{3,2,1,0:T(8,128)}, u32[]{:S(2)}) copy-start(f32[4,2,64,896]{3,2,1,0:T(8,128)} %copy-done) | copy-start | bytes 5505028
  121.0 14.4 %collective-permute-start.8 = (f32[128,896]{1,0:T(8,128)}, f32[128,896]{1,0:T(8,128)S(1)}, u32[]{:S(2)}, u32[]{:S(2)}) collective-permute-start(f32[128,896]{1,0:T(8,128)} %copy-done.9), channel_id=1, source_target_pairs={{0,200},{64,0},{128,64},{192,128},{8,192},{72,8},{136,72},{200,136... | collective-permute-start | bytes 1376264 | tf_op jit(solution)/shard_map/ppermute | solution.py:59
  121.1 16.2 %collective-permute-start.13 = (f32[128,896]{1,0:T(8,128)S(1)}, f32[128,896]{1,0:T(8,128)}, u32[]{:S(2)}, u32[]{:S(2)}) collective-permute-start(f32[128,896]{1,0:T(8,128)S(1)} %collective-permute-done.12), channel_id=1, source_target_pairs={{0,64},{64,128},{128,192},{192,8},{8,72},{72,136},{136,200},{200,0... | collective-permute-start | bytes 1376264 | tf_op jit(solution)/shard_map/ppermute | solution.py:61
  123.1 22.6 %collective-permute-start.17 = (f32[128,896]{1,0:T(8,128)}, f32[128,896]{1,0:T(8,128)}, u32[]{:S(2)}, u32[]{:S(2)}) collective-permute-start(f32[128,896]{1,0:T(8,128)} %collective-permute-done.16), channel_id=1, source_target_pairs={{0,64},{64,128},{128,192},{192,8},{8,72},{72,136},{136,200},{200,0... | collective-permute-start | bytes 1376264 | tf_op jit(solution)/shard_map/ppermute | solution.py:61
  135.3 0.8 copy-start.10
  137.3 8.4 %copy-start.6 = (f32[4,2,64,896]{3,2,1,0:T(8,128)S(1)}, f32[4,2,64,896]{3,2,1,0:T(8,128)}, u32[]{:S(2)}) copy-start(f32[4,2,64,896]{3,2,1,0:T(8,128)} %copy-done) | copy-start | bytes 5505028
  137.3 15.8 %collective-permute-start.14 = (f32[128,896]{1,0:T(8,128)}, f32[128,896]{1,0:T(8,128)}, u32[]{:S(2)}, u32[]{:S(2)}) collective-permute-start(f32[128,896]{1,0:T(8,128)} %collective-permute-done.13), channel_id=1, source_target_pairs={{0,64},{64,128},{128,192},{192,8},{8,72},{72,136},{136,200},{200,0... | collective-permute-start | bytes 1376264 | tf_op jit(solution)/shard_map/ppermute | solution.py:61
  147.9 8.8 %copy-start.7 = (f32[4,2,64,896]{3,2,1,0:T(8,128)S(1)}, f32[4,2,64,896]{3,2,1,0:T(8,128)}, u32[]{:S(2)}) copy-start(f32[4,2,64,896]{3,2,1,0:T(8,128)} %copy-done) | copy-start | bytes 5505028
  147.9 8.8 %collective-permute-start.10 = (f32[128,896]{1,0:T(8,128)}, f32[128,896]{1,0:T(8,128)S(1)}, u32[]{:S(2)}, u32[]{:S(2)}) collective-permute-start(f32[128,896]{1,0:T(8,128)} %copy-done.10), channel_id=1, source_target_pairs={{0,200},{64,0},{128,64},{192,128},{8,192},{72,8},{136,72},{200,136... | collective-permute-start | bytes 1376264 | tf_op jit(solution)/shard_map/ppermute | solution.py:59
  160.7 27.4 %all-to-all-start.4 = ((f32[4,8,128,128]{3,2,1,0:T(8,128)}), f32[4,8,128,128]{3,2,1,0:T(8,128)S(1)}, u32[]{:S(2)}, u32[]{:S(2)}) async-start(f32[4,8,128,128]{3,2,1,0:T(8,128)} %bitcast.101), calls=%async_computation.4 | async-start | bytes 4194304 | tf_op jit(solution)/shard_map/all_to_all | solution.py:69
  (1 other events, 0.8 us)

commit v2 on v0

v2 whole, which is shorter than its diff:
```python
import jax
import jax.numpy as jnp
from jax import lax
from jax.experimental import pallas as pl
from jax.experimental.pallas import tpu as pltpu
from jax.sharding import Mesh, PartitionSpec as P


AXES = ("zlo", "y", "zhi", "x", "core")
Z = ("zlo", "zhi")
F32, BF16 = jnp.float32, jnp.bfloat16
K = 1792
NT = (((1,), (1,)), ((), ()))
VMEM = pl.BlockSpec(memory_space=pltpu.VMEM)


def z_ring(step):
    place = lambda z: (z % 4) * 2 + z // 4
    return [(place(z), place((z + step) % 8)) for z in range(8)]


def ring(n, step):
    return [(i, (i + step) % n) for i in range(n)]


def call(kernel, shapes, *args, scratch=()):
    out = [jax.ShapeDtypeStruct(s, t) for s, t in shapes]
    return pl.pallas_call(
        kernel,
        out_shape=out,
        in_specs=[VMEM] * len(args),
        out_specs=[VMEM] * len(out),
        scratch_shapes=list(scratch),
        compiler_params=pltpu.CompilerParams(vmem_limit_bytes=20 * 2**20),
    )(*args)


def own_kernel(orb, same, cross, app, app_other, hi, lo):
    y, core = lax.axis_index("y"), lax.axis_index("core")
    first = core == 0

    def step(t, carry):
        ahead, x = t // 4, lax.rem(t, 4)
        to = lax.rem(y + ahead, 4)
        src = pl.ds(pl.multiple_of(to * 32 + x * 8, 8), 8)
        part = pl.ds(pl.multiple_of((to // 2) * 32 + x * 8, 8), 8)
        theirs = jnp.where(lax.rem(to, 2) == core, same[part, :], cross[part, :])
        for h, (a, b) in enumerate(((app[src, :], app_other[src, :]), (orb[src, :], theirs))):
            v = jnp.concatenate([jnp.where(first, a, b), jnp.where(first, b, a)], 0)
            top = v.astype(BF16)
            dst = pl.ds(pl.multiple_of(ahead * 128 + h * 64 + x * 16, 16), 16)
            hi[dst, :] = top
            lo[dst, :] = (v - top.astype(F32)).astype(BF16)
        return carry

    lax.fori_loop(0, 16, step, 0)


def product_kernel(n, hi, lo, *refs):
    blocks, outs = refs[: 2 * n], refs[2 * n :]
    v = jnp.concatenate([b[...] for b in blocks], 0)
    top = v.astype(BF16)
    low = (v - top.astype(F32)).astype(BF16)
    both = jnp.concatenate([top, low], 0)
    rows = n * 128
    for half in range(2):
        cols = slice(half * 256, (half + 1) * 256)
        p = lax.dot_general(both, hi[cols, :], NT, preferred_element_type=F32)
        r = lax.dot_general(top, lo[cols, :], NT, preferred_element_type=F32)
        total = (p[:rows] + p[rows:]) + r
        outs[2 * half][...] = total[:, :128]
        outs[2 * half + 1][...] = total[:, 128:]


def products(hi, lo, pairs):
    n = len(pairs)
    flat = [b for pair in pairs for b in pair]
    shapes = [((n * 128, 128), F32)] * 4
    return call(lambda *r: product_kernel(n, *r), shapes, hi, lo, *flat)


def to_y(parts):
    sent = [lax.ppermute(parts[q], "y", ring(4, q)) for q in range(1, 4)]
    return [parts[0]] + sent


def x_kernel(picks, refs, outs, sums):
    for m, (group, at) in enumerate(picks):
        rows = pl.ds(at * 128, 128)
        four = [r[rows, :] for r in refs[4 * group : 4 * group + 4]]
        sums[m] = (four[0] + four[1]) + (four[2] + four[3])
    x, zhi, zlo = lax.axis_index("x"), lax.axis_index("zhi"), lax.axis_index("zlo")
    for ahead in range(4):
        to = lax.rem(x + ahead, 4)
        xb, yh = to // 2, lax.rem(to, 2)
        for t in range(2):
            place = lax.rem(zhi + t, 2) * 2 + xb
            m = lax.rem(place - zlo + 4, 4)
            for h in range(2):
                at = t * 64 + h * 32
                outs[ahead][at : at + 32, :] = sums[
                    m, pl.ds(pl.multiple_of(h * 64 + yh * 32, 32), 32), :
                ]


def to_x(groups, picks):
    flat = [a for g in groups for a in g]
    n = len(flat)
    body = lambda *r: x_kernel(picks, r[:n], r[n : n + 4], r[n + 4])
    scratch = [pltpu.VMEM((4, 128, 128), F32)]
    outs = call(body, [((128, 128), F32)] * 4, *flat, scratch=scratch)
    got = [outs[0]] + [lax.ppermute(outs[q], "x", ring(4, q)) for q in range(1, 4)]

    def add(a, b, c, d, keep, send):
        v = (a[...] + b[...]) + (c[...] + d[...])
        keep[...] = v[:64]
        send[...] = v[64:]

    keep, send = call(add, [((64, 128), F32)] * 2, *got)
    return keep, lax.ppermute(send, "zhi", ring(2, 1))


def tile_kernel(keep_a, recv_a, keep_b, recv_b, ham, ovl):
    x, zhi, zlo = lax.axis_index("x"), lax.axis_index("zhi"), lax.axis_index("zlo")
    core = lax.axis_index("core")
    m = lax.rem(zhi * 2 + x // 2 - zlo + 4, 4)
    d = jnp.where(m < 2, m, m - 4)
    a0 = lax.rem(zhi * 4 + zlo + d + 8, 8) // 4
    for zi in range(2):
        parts = []
        for zj in range(2):
            far = lax.rem(zhi + zj, 2)
            late = lax.rem(zi + a0 + far, 2)
            kept = jnp.where(late == 0, keep_a[...], keep_b[...])
            came = jnp.where(late == 0, recv_a[...], recv_b[...])
            parts.append(jnp.where(far == 0, kept, came))
        for out, cut in ((ham, slice(0, 64)), (ovl, slice(64, 128))):
            v = jnp.concatenate([p[:, cut] for p in parts], axis=1)
            for h in range(2):
                c = lax.rem(core + h, 2)
                for k in range(4):
                    dst = pl.ds(pl.multiple_of(zi * 64 + k * 16 + c * 8, 8), 8)
                    out[dst, :] = v[h * 32 + k * 8 : h * 32 + k * 8 + 8, :]


def after(value, *others):
    return lax.optimization_barrier((value, *others))[0]


def body(orbitals, applied):
    core, swap = lax.axis_index("core"), ring(2, 1)
    orb = lax.all_to_all(orbitals, ("y", "x"), split_axis=1, concat_axis=0, tiled=True)
    by_parity = orb.reshape(2, 2, 32, K)
    mine = lax.dynamic_index_in_dim(by_parity, core, 1, False).reshape(64, K)
    theirs = lax.dynamic_index_in_dim(by_parity, 1 - core, 1, False).reshape(64, K)
    same = lax.ppermute(theirs, "core", swap)
    cross = lax.ppermute(mine, "core", swap)
    app = lax.all_to_all(after(applied, mine), ("y", "x"), split_axis=1, concat_axis=0, tiled=True)

    held = {(0, 0): mine, (0, 1): same}

    def forward(d, h):
        if d < 4 or h == 0:
            held[(d, h)] = lax.ppermute(held[(d - 1, h)], Z, z_ring(-1))
        if d < 4 or h == 1:
            held[(-d % 8, h)] = lax.ppermute(held[((1 - d) % 8, h)], Z, z_ring(1))

    for d in range(1, 5):
        for h in range(2):
            forward(d, h)
    app_other = lax.ppermute(app, "core", swap)
    hi, lo = call(own_kernel, [((512, K), BF16)] * 2, orb, same, cross, app, app_other)
    pair = lambda d: (held[(d % 8, 0)], held[(d % 8, 1)])
    y1 = to_y(products(hi, lo, [pair(0), pair(1), pair(-1)]))
    y2 = to_y(products(hi, lo, [pair(2), pair(-2)]))
    y3 = to_y(products(hi, lo, [pair(3), pair(-3)]))
    y4 = to_y(products(hi, lo, [pair(4)]))
    keep_a, recv_a = to_x([y1, y2], [(0, 0), (0, 1), (1, 1), (0, 2)])
    keep_b, recv_b = to_x([y2, y3, y4], [(2, 0), (1, 1), (0, 0), (1, 0)])
    return call(tile_kernel, [((128, 128), F32)] * 2, keep_a, recv_a, keep_b, recv_b)


def solution(mesh):
    fine = Mesh(mesh.devices.reshape(4, 4, 2, 4, 2), AXES)
    placed = P(AXES, None)
    out = P(("zhi", "x", "core"), ("zlo", "y"))

    return jax.shard_map(
        body, mesh=fine, in_specs=(placed, placed), out_specs=(out, out), check_vma=False
    )
```

time: 356 us -> 149 us (0.42)
  waiting for transfers between devices: 265 us -> 59.1 us
  starting transfers between devices: 3.73 us -> 75.1 us
  matrix products: 36.8 us -> 0 us
  blocking collectives: 32.4 us -> 0 us
  between operations: 14.1 us -> 0.78 us
  Pallas kernels: 0 us -> 11.1 us
    all_gather x1 -> x0, waiting for transfers between devices: 173 us -> none  [shards(): every_orb = lax.all_gather(mine_orb, 'row', axis=0, tiled=True)]
    reduce_scatter x1 -> x0, waiting for transfers between devices: 91.3 us -> none  [sent_together(): lax.psum_scatter(both, axis, scatter_dimension=dim, tiled=True)]
    ppermute x0 -> x37, starting transfers between devices: none -> 61.2 us  [the longest x7 26.6 us: forward(): held[d, h] = lax.ppermute(held[d - 1, h], Z, z_ring(-1))]
    ppermute x0 -> x37, waiting for transfers between devices: none -> 45.9 us  [the longest x7 22.4 us: forward(): held[-d % 8, h] = lax.ppermute(held[(1 - d) % 8, h], Z, z_ring(1))]
    dot_general x2 -> x0, matrix products: 36.8 us -> none  [product(): lax.dot_general(left, right, (((1,), (1,)), ((), ())), precision=lax.Prec...]
    all_to_all x1 -> x0, blocking collectives: 32.4 us -> none  [shards(): lax.all_to_all(orbitals, 'col', split_axis=1, concat_axis=0, tiled=True)]
    all_to_all x1 -> x2, waiting for transfers between devices: 0.01 us -> 13.2 us  [the longest x1 13.2 us: body(): lax.all_to_all(orbitals, ('y', 'x'), split_axis=1, concat_axis=0, tiled=T...]
    pallas_call x0 -> x10, Pallas kernels: none -> 11.1 us  [call(): pl.pallas_call(kernel, out_shape=out, in_specs=[VMEM] * len(args), out_sp...]
  transfers between devices with their start and end apart: 3 -> 39, of which waited for: 2 -> 14; matrix products, arithmetic and copies ran while one was open for 5% -> 0% of each run, Pallas kernels for 0% -> 7%
where the time goes in v2:
time: 149 us
  starting transfers between devices  75.1 us (50%)
  waiting for transfers between devices  59.1 us (40%)
  Pallas kernels  11.1 us (7%)
  local copies, waits for them, and re-layouts  2.62 us (2%)
    ppermute x7, starting transfers between devices, forward(): held[d, h] = lax.ppermute(held[d - 1, h], Z, z_ring(-1))  26.6 us
    ppermute x7, waiting for transfers between devices, forward(): held[-d % 8, h] = lax.ppermute(held[(1 - d) % 8, h], Z, z_ring(1))  22.4 us
    ppermute x12, starting transfers between devices, to_y(): sent = [lax.ppermute(parts[q], 'y', ring(4, q)) for q in range(1, 4)]  17.9 us
    ppermute x7, waiting for transfers between devices, forward(): held[d, h] = lax.ppermute(held[d - 1, h], Z, z_ring(-1))  13.6 us
    all_to_all x1, waiting for transfers between devices, body(): lax.all_to_all(orbitals, ('y', 'x'), split_axis=1, concat_axis=0, tiled=T...  13.2 us
    pallas_call x10, Pallas kernels, call(): pl.pallas_call(kernel, out_shape=out, in_specs=[VMEM] * len(args), out_sp...  11.1 us
    ppermute x6, starting transfers between devices, to_x(): lax.ppermute(outs[q], 'x', ring(4, q))  9.68 us
    all_to_all x1, starting transfers between devices, body(): lax.all_to_all(orbitals, ('y', 'x'), split_axis=1, concat_axis=0, tiled=T...  7.41 us
  transfers between devices with their start and end apart: 39, of which 14 were waited for; matrix products, arithmetic and copies ran while one was open for 0% of the time, Pallas kernels for 7%

profile of v2, /device:TPU:8, one launch (start us, length us, event | category | flops | bytes accessed | tf_op | source)
XLA Modules:
  0.0 148.7 jit_solution(651195685514560423)
XLA Ops:
  0.6 7.4 %all-to-all-start = ((f32[8,16,1792]{2,0,1:T(8,128)}), f32[8,16,1792]{2,0,1:T(8,128)S(1)}, u32[]{:S(2)}, u32[]{:S(2)}) async-start(f32[8,16,1792]{2,0,1:T(8,128)} %bitcast.20), calls=%async_computation | async-start | bytes 1835008 | tf_op jit(solution)/shard_map/all_to_all | solution.py:152
  8.0 13.2 %all-to-all-done = f32[8,16,1792]{2,0,1:T(8,128)S(1)} async-done(((f32[8,16,1792]{2,0,1:T(8,128)}), f32[8,16,1792]{2,0,1:T(8,128)S(1)}, u32[]{:S(2)}, u32[]{:S(2)}) %all-to-all-start) | async-done | bytes 917536 | tf_op jit(solution)/shard_map/all_to_all | solution.py:152
  22.0 6.5 %all-to-all-start.1 = ((f32[8,16,1792]{2,0,1:T(8,128)}), f32[8,16,1792]{2,0,1:T(8,128)S(1)}, u32[]{:S(2)}, u32[]{:S(2)}) async-start(f32[8,16,1792]{2,0,1:T(8,128)} %bitcast.21), calls=%async_computation.1 | async-start | bytes 1835008 | tf_op jit(solution)/shard_map/all_to_all | solution.py:158
  28.5 5.9 %collective-permute-start.3 = (f32[64,1792]{1,0:T(8,128)S(1)}, f32[64,1792]{1,0:T(8,128)S(1)}, u32[]{:S(2)}, u32[]{:S(2)}) collective-permute-start(f32[64,1792]{1,0:T(8,128)S(1)} %bitcast.16), channel_id=1, source_target_pairs={{0,200},{64,0},{128,64},{192,128},{8,192},{72,8},{136,72},{200,136... | collective-permute-start | bytes 1376264 | tf_op jit(solution)/shard_map/ppermute | solution.py:164
  34.5 3.2 %collective-permute-start.4 = (f32[64,1792]{1,0:T(8,128)S(1)}, f32[64,1792]{1,0:T(8,128)}, u32[]{:S(2)}, u32[]{:S(2)}) collective-permute-start(f32[64,1792]{1,0:T(8,128)S(1)} %collective-permute-done.same.r_3_), channel_id=1, source_target_pairs={{0,200},{64,0},{128,64},{192,128},{8,192},{72,8},{136,72},{200,136... | collective-permute-start | bytes 1376264 | tf_op jit(solution)/shard_map/ppermute | solution.py:164
  37.7 7.6 %collective-permute-done.3.r_4_ = f32[64,1792]{1,0:T(8,128)S(1)} collective-permute-done((f32[64,1792]{1,0:T(8,128)S(1)}, f32[64,1792]{1,0:T(8,128)S(1)}, u32[]{:S(2)}, u32[]{:S(2)}) %collective-permute-start.3) | collective-permute-done | bytes 458784 | tf_op jit(solution)/shard_map/ppermute | solution.py:164
  45.3 3.7 %collective-permute-start.10 = (f32[64,1792]{1,0:T(8,128)S(1)}, f32[64,1792]{1,0:T(8,128)}, u32[]{:S(2)}, u32[]{:S(2)}) collective-permute-start(f32[64,1792]{1,0:T(8,128)S(1)} %collective-permute-done.3.r_4_), channel_id=1, source_target_pairs={{0,200},{64,0},{128,64},{192,128},{8,192},{72,8},{136,72},{200,136... | collective-permute-start | bytes 1376264 | tf_op jit(solution)/shard_map/ppermute | solution.py:164
  49.9 9.0 %collective-permute-done.5.r_6_ = f32[64,1792]{1,0:T(8,128)} collective-permute-done((f32[64,1792]{1,0:T(8,128)S(1)}, f32[64,1792]{1,0:T(8,128)}, u32[]{:S(2)}, u32[]{:S(2)}) %collective-permute-start.5) | collective-permute-done | bytes 458784 | tf_op jit(solution)/shard_map/ppermute | solution.py:166
  58.9 3.2 %collective-permute-start.11 = (f32[64,1792]{1,0:T(8,128)}, f32[64,1792]{1,0:T(8,128)S(1)}, u32[]{:S(2)}, u32[]{:S(2)}) collective-permute-start(f32[64,1792]{1,0:T(8,128)} %collective-permute-done.4.r_5_), channel_id=1, source_target_pairs={{0,200},{64,0},{128,64},{192,128},{8,192},{72,8},{136,72},{200,136... | collective-permute-start | bytes 1376264 | tf_op jit(solution)/shard_map/ppermute | solution.py:164
  62.2 2.8 %collective-permute-done.10.r_2_ = f32[64,1792]{1,0:T(8,128)} collective-permute-done((f32[64,1792]{1,0:T(8,128)S(1)}, f32[64,1792]{1,0:T(8,128)}, u32[]{:S(2)}, u32[]{:S(2)}) %collective-permute-start.10) | collective-permute-done | bytes 458784 | tf_op jit(solution)/shard_map/ppermute | solution.py:164
  64.9 3.8 %collective-permute-start.21 = (f32[64,1792]{1,0:T(8,128)}, f32[64,1792]{1,0:T(8,128)S(1)}, u32[]{:S(2)}, u32[]{:S(2)}) collective-permute-start(f32[64,1792]{1,0:T(8,128)} %collective-permute-done.10.r_2_), channel_id=1, source_target_pairs={{0,200},{64,0},{128,64},{192,128},{8,192},{72,8},{136,72},{200,136... | collective-permute-start | bytes 1376264 | tf_op jit(solution)/shard_map/ppermute | solution.py:164
  68.7 9.7 %collective-permute-done.12.r_4_ = f32[64,1792]{1,0:T(8,128)S(1)} collective-permute-done((f32[64,1792]{1,0:T(8,128)}, f32[64,1792]{1,0:T(8,128)S(1)}, u32[]{:S(2)}, u32[]{:S(2)}) %collective-permute-start.12) | collective-permute-done | bytes 458784 | tf_op jit(solution)/shard_map/ppermute | solution.py:166
  78.5 3.2 %collective-permute-start.22 = (f32[64,1792]{1,0:T(8,128)S(1)}, f32[64,1792]{1,0:T(8,128)S(1)}, u32[]{:S(2)}, u32[]{:S(2)}) collective-permute-start(f32[64,1792]{1,0:T(8,128)S(1)} %collective-permute-done.11.r_3_), channel_id=1, source_target_pairs={{0,200},{64,0},{128,64},{192,128},{8,192},{72,8},{136,72},{200,136... | collective-permute-start | bytes 1376264 | tf_op jit(solution)/shard_map/ppermute | solution.py:164
  81.7 3.0 %collective-permute-done.21.r_2_ = f32[64,1792]{1,0:T(8,128)S(1)} collective-permute-done((f32[64,1792]{1,0:T(8,128)}, f32[64,1792]{1,0:T(8,128)S(1)}, u32[]{:S(2)}, u32[]{:S(2)}) %collective-permute-start.21) | collective-permute-done | bytes 458784 | tf_op jit(solution)/shard_map/ppermute | solution.py:164
  84.7 3.6 %collective-permute-start.28 = (f32[64,1792]{1,0:T(8,128)S(1)}, f32[64,1792]{1,0:T(8,128)S(1)}, u32[]{:S(2)}, u32[]{:S(2)}) collective-permute-start(f32[64,1792]{1,0:T(8,128)S(1)} %collective-permute-done.21.r_2_), channel_id=1, source_target_pairs={{0,200},{64,0},{128,64},{192,128},{8,192},{72,8},{136,72},{200,136... | collective-permute-start | bytes 1376264 | tf_op jit(solution)/shard_map/ppermute | solution.py:164
  90.3 2.8 %shard_map.43 = (f32[256,128]{1,0:T(8,128)S(1)}, f32[256,128]{1,0:T(8,128)S(1)}, f32[256,128]{1,0:T(8,128)S(1)}, f32[256,128]{1,0:T(8,128)S(1)}) custom-call(bf16[512,1792]{1,0:T(8,128)(2,1)S(1)} %get-tuple-element.34.r_0_, bf16[512,1792]{1,0:T(8,128)(2,1)S(1)} %get-tuple-element.35.r_1_, f32[64,1792]{1,0:T(8,128)} %collective-permute-done.10.r_2_, ...), custom_call_target="tpu_custom_call" | custom-call | tf_op jit(solution)/shard_map/pallas_call | solution.py:28
  93.1 1.6 %collective-permute-start.14 = (f32[256,128]{1,0:T(8,128)S(1)}, f32[256,128]{1,0:T(8,128)S(1)}, u32[]{:S(2)}, u32[]{:S(2)}) collective-permute-start(f32[256,128]{1,0:T(8,128)S(1)} %get-tuple-element.41), channel_id=1, source_target_pairs={{0,16},{16,32},{32,48},{48,0},{1,17},{17,33},{33,49},{49,1},{2,18}... | collective-permute-start | bytes 393224 | tf_op jit(solution)/shard_map/ppermute | solution.py:83
  94.7 3.5 %collective-permute-done.23.r_4_ = f32[64,1792]{1,0:T(8,128)S(1)} collective-permute-done((f32[64,1792]{1,0:T(8,128)S(1)}, f32[64,1792]{1,0:T(8,128)S(1)}, u32[]{:S(2)}, u32[]{:S(2)}) %collective-permute-start.23) | collective-permute-done | bytes 458784 | tf_op jit(solution)/shard_map/ppermute | solution.py:166
  98.1 2.1 %collective-permute-start.15 = (f32[256,128]{1,0:T(8,128)S(1)}, f32[256,128]{1,0:T(8,128)S(1)}, u32[]{:S(2)}, u32[]{:S(2)}) collective-permute-start(f32[256,128]{1,0:T(8,128)S(1)} %get-tuple-element.42), channel_id=1, source_target_pairs={{0,32},{16,48},{32,0},{48,16},{1,33},{17,49},{33,1},{49,17},{2,34}... | collective-permute-start | bytes 393224 | tf_op jit(solution)/shard_map/ppermute | solution.py:83
  101.7 1.6 %shard_map.46 = (f32[256,128]{1,0:T(8,128)S(1)}, f32[256,128]{1,0:T(8,128)S(1)}, f32[256,128]{1,0:T(8,128)S(1)}, f32[256,128]{1,0:T(8,128)S(1)}) custom-call(bf16[512,1792]{1,0:T(8,128)(2,1)S(1)} %get-tuple-element.34.r_0_, bf16[512,1792]{1,0:T(8,128)(2,1)S(1)} %get-tuple-element.35.r_1_, f32[64,1792]{1,0:T(8,128)S(1)} %collective-permute-done.21.r_2_, ...), custom_call_target="tpu_custom_call" | custom-call | tf_op jit(solution)/shard_map/pallas_call | solution.py:28
  105.0 3.6 %shard_map.42 = (f32[384,128]{1,0:T(8,128)S(1)}, f32[384,128]{1,0:T(8,128)S(1)}, f32[384,128]{1,0:T(8,128)S(1)}, f32[384,128]{1,0:T(8,128)S(1)}) custom-call(bf16[512,1792]{1,0:T(8,128)(2,1)S(1)} %get-tuple-element.34.r_0_, bf16[512,1792]{1,0:T(8,128)(2,1)S(1)} %get-tuple-element.35.r_1_, f32[64,1792]{1,0:T(8,128)S(1)} %bitcast.19, ...), custom_call_target="tpu_custom_call" | custom-call | tf_op jit(solution)/shard_map/pallas_call | solution.py:28
  111.3 1.6 %collective-permute-start.9 = (f32[384,128]{1,0:T(8,128)S(1)}, f32[384,128]{1,0:T(8,128)S(1)}, u32[]{:S(2)}, u32[]{:S(2)}) collective-permute-start(f32[384,128]{1,0:T(8,128)S(1)} %get-tuple-element.39), channel_id=1, source_target_pairs={{0,48},{16,0},{32,16},{48,32},{1,49},{17,1},{33,17},{49,33},{2,50}... | collective-permute-start | bytes 589832 | tf_op jit(solution)/shard_map/ppermute | solution.py:83
  113.7 1.7 %collective-permute-start.27 = (f32[256,128]{1,0:T(8,128)S(1)}, f32[256,128]{1,0:T(8,128)S(1)}, u32[]{:S(2)}, u32[]{:S(2)}) collective-permute-start(f32[256,128]{1,0:T(8,128)S(1)} %get-tuple-element.53), channel_id=1, source_target_pairs={{0,48},{16,0},{32,16},{48,32},{1,49},{17,1},{33,17},{49,33},{2,50}... | collective-permute-start | bytes 393224 | tf_op jit(solution)/shard_map/ppermute | solution.py:83
  117.6 1.6 %collective-permute-done.8.r_2_ = f32[384,128]{1,0:T(8,128)S(1)} collective-permute-done((f32[384,128]{1,0:T(8,128)S(1)}, f32[384,128]{1,0:T(8,128)S(1)}, u32[]{:S(2)}, u32[]{:S(2)}) %collective-permute-start.8) | collective-permute-done | bytes 196640 | tf_op jit(solution)/shard_map/ppermute | solution.py:83
  119.2 2.0 %collective-permute-start.31 = (f32[128,128]{1,0:T(8,128)S(1)}, f32[128,128]{1,0:T(8,128)S(1)}, u32[]{:S(2)}, u32[]{:S(2)}) collective-permute-start(f32[128,128]{1,0:T(8,128)S(1)} %get-tuple-element.56), channel_id=1, source_target_pairs={{0,32},{16,48},{32,0},{48,16},{1,33},{17,49},{33,1},{49,17},{2,34}... | collective-permute-start | bytes 196616 | tf_op jit(solution)/shard_map/ppermute | solution.py:83
  122.8 1.5 %collective-permute-start.32 = (f32[128,128]{1,0:T(8,128)S(1)}, f32[128,128]{1,0:T(8,128)S(1)}, u32[]{:S(2)}, u32[]{:S(2)}) collective-permute-start(f32[128,128]{1,0:T(8,128)S(1)} %get-tuple-element.57), channel_id=1, source_target_pairs={{0,48},{16,0},{32,16},{48,32},{1,49},{17,1},{33,17},{49,33},{2,50}... | collective-permute-start | bytes 196616 | tf_op jit(solution)/shard_map/ppermute | solution.py:83
  124.4 1.9 %collective-permute-done.26.r_6_ = f32[256,128]{1,0:T(8,128)S(1)} collective-permute-done((f32[256,128]{1,0:T(8,128)S(1)}, f32[256,128]{1,0:T(8,128)S(1)}, u32[]{:S(2)}, u32[]{:S(2)}) %collective-permute-start.26) | collective-permute-done | bytes 131104 | tf_op jit(solution)/shard_map/ppermute | solution.py:83
  127.8 2.9 %collective-permute-start.18 = (f32[128,128]{1,0:T(8,128)S(1)}, f32[128,128]{1,0:T(8,128)S(1)}, u32[]{:S(2)}, u32[]{:S(2)}) collective-permute-start(f32[128,128]{1,0:T(8,128)S(1)} %get-tuple-element.46), channel_id=1, source_target_pairs={{0,4},{2,6},{4,0},{6,2},{1,5},{3,7},{5,1},{7,3},{8,12},{10,14},{12... | collective-permute-start | bytes 196616 | tf_op jit(solution)/shard_map/ppermute | solution.py:112
  133.6 2.5 %collective-permute-start.35 = (f32[128,128]{1,0:T(8,128)S(1)}, f32[128,128]{1,0:T(8,128)S(1)}, u32[]{:S(2)}, u32[]{:S(2)}) collective-permute-start(f32[128,128]{1,0:T(8,128)S(1)} %get-tuple-element.61), channel_id=1, source_target_pairs={{0,6},{2,0},{4,2},{6,4},{1,7},{3,1},{5,3},{7,5},{8,14},{10,8},{12,... | collective-permute-start | bytes 196616 | tf_op jit(solution)/shard_map/ppermute | solution.py:112
  136.1 3.9 %collective-permute-start.20 = (f32[64,128]{1,0:T(8,128)S(1)}, f32[64,128]{1,0:T(8,128)S(1)}, u32[]{:S(2)}, u32[]{:S(2)}) collective-permute-start(f32[64,128]{1,0:T(8,128)S(1)} %get-tuple-element.49), channel_id=1, source_target_pairs={{0,8},{8,0},{1,9},{9,1},{2,10},{10,2},{3,11},{11,3},{4,12},{12,4},... | collective-permute-start | bytes 98312 | tf_op jit(solution)/shard_map/ppermute | solution.py:120
  140.1 3.0 %collective-permute-start.36 = (f32[64,128]{1,0:T(8,128)S(1)}, f32[64,128]{1,0:T(8,128)S(1)}, u32[]{:S(2)}, u32[]{:S(2)}) collective-permute-start(f32[64,128]{1,0:T(8,128)S(1)} %get-tuple-element.63), channel_id=1, source_target_pairs={{0,8},{8,0},{1,9},{9,1},{2,10},{10,2},{3,11},{11,3},{4,12},{12,4},... | collective-permute-start | bytes 98312 | tf_op jit(solution)/shard_map/ppermute | solution.py:120
  144.0 3.9 %collective-permute-done.36.recv_b = f32[64,128]{1,0:T(8,128)S(1)} collective-permute-done((f32[64,128]{1,0:T(8,128)S(1)}, f32[64,128]{1,0:T(8,128)S(1)}, u32[]{:S(2)}, u32[]{:S(2)}) %collective-permute-start.36) | collective-permute-done | bytes 32800 | tf_op jit(solution)/shard_map/ppermute | solution.py:120
  (61 shorter events, 20.4 us)
Async XLA Ops:
  0.6 20.6 %all-to-all-start = ((f32[8,16,1792]{2,0,1:T(8,128)}), f32[8,16,1792]{2,0,1:T(8,128)S(1)}, u32[]{:S(2)}, u32[]{:S(2)}) async-start(f32[8,16,1792]{2,0,1:T(8,128)} %bitcast.20), calls=%async_computation | async-start | bytes 1835008 | tf_op jit(solution)/shard_map/all_to_all | solution.py:152
  22.0 12.3 %collective-permute-start = (f32[64,1792]{1,0:T(8,128)}, f32[64,1792]{1,0:T(8,128)S(1)}, u32[]{:S(2)}, u32[]{:S(2)}) collective-permute-start(f32[64,1792]{1,0:T(8,128)} %bitcast.4), channel_id=1, source_target_pairs={{0,1},{1,0},{2,3},{3,2},{4,5},{5,4},{6,7},{7,6},{8,9},{9,8},{10,11... | collective-permute-start | bytes 1376264 | tf_op jit(solution)/shard_map/ppermute | solution.py:156
  22.0 27.8 %all-to-all-start.1 = ((f32[8,16,1792]{2,0,1:T(8,128)}), f32[8,16,1792]{2,0,1:T(8,128)S(1)}, u32[]{:S(2)}, u32[]{:S(2)}) async-start(f32[8,16,1792]{2,0,1:T(8,128)} %bitcast.21), calls=%async_computation.1 | async-start | bytes 1835008 | tf_op jit(solution)/shard_map/all_to_all | solution.py:158
  28.5 16.8 %collective-permute-start.3 = (f32[64,1792]{1,0:T(8,128)S(1)}, f32[64,1792]{1,0:T(8,128)S(1)}, u32[]{:S(2)}, u32[]{:S(2)}) collective-permute-start(f32[64,1792]{1,0:T(8,128)S(1)} %bitcast.16), channel_id=1, source_target_pairs={{0,200},{64,0},{128,64},{192,128},{8,192},{72,8},{136,72},{200,136... | collective-permute-start | bytes 1376264 | tf_op jit(solution)/shard_map/ppermute | solution.py:164
  34.4 14.7 %collective-permute-start.6 = (f32[64,1792]{1,0:T(8,128)S(1)}, f32[64,1792]{1,0:T(8,128)}, u32[]{:S(2)}, u32[]{:S(2)}) collective-permute-start(f32[64,1792]{1,0:T(8,128)S(1)} %collective-permute-done.same.r_3_), channel_id=1, source_target_pairs={{0,64},{64,128},{128,192},{192,8},{8,72},{72,136},{136,200},{200,0... | collective-permute-start | bytes 1376264 | tf_op jit(solution)/shard_map/ppermute | solution.py:166
  34.4 14.7 %collective-permute-start.1 = (f32[64,1792]{1,0:T(8,128)S(1)}, f32[64,1792]{1,0:T(8,128)S(1)}, u32[]{:S(2)}, u32[]{:S(2)}) collective-permute-start(f32[64,1792]{1,0:T(8,128)S(1)} %bitcast.17), channel_id=1, source_target_pairs={{0,1},{1,0},{2,3},{3,2},{4,5},{5,4},{6,7},{7,6},{8,9},{9,8},{10,11... | collective-permute-start | bytes 1376264 | tf_op jit(solution)/shard_map/ppermute | solution.py:157
  34.4 24.5 %collective-permute-start.5 = (f32[64,1792]{1,0:T(8,128)S(1)}, f32[64,1792]{1,0:T(8,128)}, u32[]{:S(2)}, u32[]{:S(2)}) collective-permute-start(f32[64,1792]{1,0:T(8,128)S(1)} %bitcast.18), channel_id=1, source_target_pairs={{0,64},{64,128},{128,192},{192,8},{8,72},{72,136},{136,200},{200,0... | collective-permute-start | bytes 1376264 | tf_op jit(solution)/shard_map/ppermute | solution.py:166
  34.5 24.4 %collective-permute-start.4 = (f32[64,1792]{1,0:T(8,128)S(1)}, f32[64,1792]{1,0:T(8,128)}, u32[]{:S(2)}, u32[]{:S(2)}) collective-permute-start(f32[64,1792]{1,0:T(8,128)S(1)} %collective-permute-done.same.r_3_), channel_id=1, source_target_pairs={{0,200},{64,0},{128,64},{192,128},{8,192},{72,8},{136,72},{200,136... | collective-permute-start | bytes 1376264 | tf_op jit(solution)/shard_map/ppermute | solution.py:164
  45.3 19.7 %collective-permute-start.10 = (f32[64,1792]{1,0:T(8,128)S(1)}, f32[64,1792]{1,0:T(8,128)}, u32[]{:S(2)}, u32[]{:S(2)}) collective-permute-start(f32[64,1792]{1,0:T(8,128)S(1)} %collective-permute-done.3.r_4_), channel_id=1, source_target_pairs={{0,200},{64,0},{128,64},{192,128},{8,192},{72,8},{136,72},{200,136... | collective-permute-start | bytes 1376264 | tf_op jit(solution)/shard_map/ppermute | solution.py:164
  49.1 19.7 %collective-permute-start.13 = (f32[64,1792]{1,0:T(8,128)}, f32[64,1792]{1,0:T(8,128)}, u32[]{:S(2)}, u32[]{:S(2)}) collective-permute-start(f32[64,1792]{1,0:T(8,128)} %collective-permute-done.6.r_7_), channel_id=1, source_target_pairs={{0,64},{64,128},{128,192},{192,8},{8,72},{72,136},{136,200},{200,0... | collective-permute-start | bytes 1376264 | tf_op jit(solution)/shard_map/ppermute | solution.py:166
  49.9 38.4 %collective-permute-start.2 = (f32[128,1792]{1,0:T(8,128)S(1)}, f32[128,1792]{1,0:T(8,128)S(1)}, u32[]{:S(2)}, u32[]{:S(2)}) collective-permute-start(f32[128,1792]{1,0:T(8,128)S(1)} %bitcast.14), channel_id=1, source_target_pairs={{0,1},{1,0},{2,3},{3,2},{4,5},{5,4},{6,7},{7,6},{8,9},{9,8},{10,11... | collective-permute-start | bytes 2752520 | tf_op jit(solution)/shard_map/ppermute | solution.py:171
  58.9 19.6 %collective-permute-start.12 = (f32[64,1792]{1,0:T(8,128)}, f32[64,1792]{1,0:T(8,128)S(1)}, u32[]{:S(2)}, u32[]{:S(2)}) collective-permute-start(f32[64,1792]{1,0:T(8,128)} %collective-permute-done.5.r_6_), channel_id=1, source_target_pairs={{0,64},{64,128},{128,192},{192,8},{8,72},{72,136},{136,200},{200,0... | collective-permute-start | bytes 1376264 | tf_op jit(solution)/shard_map/ppermute | solution.py:166
  58.9 19.6 %collective-permute-start.11 = (f32[64,1792]{1,0:T(8,128)}, f32[64,1792]{1,0:T(8,128)S(1)}, u32[]{:S(2)}, u32[]{:S(2)}) collective-permute-start(f32[64,1792]{1,0:T(8,128)} %collective-permute-done.4.r_5_), channel_id=1, source_target_pairs={{0,200},{64,0},{128,64},{192,128},{8,192},{72,8},{136,72},{200,136... | collective-permute-start | bytes 1376264 | tf_op jit(solution)/shard_map/ppermute | solution.py:164
  64.9 19.8 %collective-permute-start.21 = (f32[64,1792]{1,0:T(8,128)}, f32[64,1792]{1,0:T(8,128)S(1)}, u32[]{:S(2)}, u32[]{:S(2)}) collective-permute-start(f32[64,1792]{1,0:T(8,128)} %collective-permute-done.10.r_2_), channel_id=1, source_target_pairs={{0,200},{64,0},{128,64},{192,128},{8,192},{72,8},{136,72},{200,136... | collective-permute-start | bytes 1376264 | tf_op jit(solution)/shard_map/ppermute | solution.py:164
  68.7 19.6 %collective-permute-start.24 = (f32[64,1792]{1,0:T(8,128)}, f32[64,1792]{1,0:T(8,128)S(1)}, u32[]{:S(2)}, u32[]{:S(2)}) collective-permute-start(f32[64,1792]{1,0:T(8,128)} %collective-permute-done.13.r_5_), channel_id=1, source_target_pairs={{0,64},{64,128},{128,192},{192,8},{8,72},{72,136},{136,200},{200,0... | collective-permute-start | bytes 1376264 | tf_op jit(solution)/shard_map/ppermute | solution.py:166
  78.5 19.7 %collective-permute-start.23 = (f32[64,1792]{1,0:T(8,128)S(1)}, f32[64,1792]{1,0:T(8,128)S(1)}, u32[]{:S(2)}, u32[]{:S(2)}) collective-permute-start(f32[64,1792]{1,0:T(8,128)S(1)} %collective-permute-done.12.r_4_), channel_id=1, source_target_pairs={{0,64},{64,128},{128,192},{192,8},{8,72},{72,136},{136,200},{200,0... | collective-permute-start | bytes 1376264 | tf_op jit(solution)/shard_map/ppermute | solution.py:166
  78.5 21.8 %collective-permute-start.22 = (f32[64,1792]{1,0:T(8,128)S(1)}, f32[64,1792]{1,0:T(8,128)S(1)}, u32[]{:S(2)}, u32[]{:S(2)}) collective-permute-start(f32[64,1792]{1,0:T(8,128)S(1)} %collective-permute-done.11.r_3_), channel_id=1, source_target_pairs={{0,200},{64,0},{128,64},{192,128},{8,192},{72,8},{136,72},{200,136... | collective-permute-start | bytes 1376264 | tf_op jit(solution)/shard_map/ppermute | solution.py:164
  84.7 18.8 %collective-permute-start.28 = (f32[64,1792]{1,0:T(8,128)S(1)}, f32[64,1792]{1,0:T(8,128)S(1)}, u32[]{:S(2)}, u32[]{:S(2)}) collective-permute-start(f32[64,1792]{1,0:T(8,128)S(1)} %collective-permute-done.21.r_2_), channel_id=1, source_target_pairs={{0,200},{64,0},{128,64},{192,128},{8,192},{72,8},{136,72},{200,136... | collective-permute-start | bytes 1376264 | tf_op jit(solution)/shard_map/ppermute | solution.py:164
  88.3 25.4 %collective-permute-start.29 = (f32[64,1792]{1,0:T(8,128)S(1)}, f32[64,1792]{1,0:T(8,128)S(1)}, u32[]{:S(2)}, u32[]{:S(2)}) collective-permute-start(f32[64,1792]{1,0:T(8,128)S(1)} %collective-permute-done.24.r_5_), channel_id=1, source_target_pairs={{0,64},{64,128},{128,192},{192,8},{8,72},{72,136},{136,200},{200,0... | collective-permute-start | bytes 1376264 | tf_op jit(solution)/shard_map/ppermute | solution.py:166
  93.1 15.5 %collective-permute-start.14 = (f32[256,128]{1,0:T(8,128)S(1)}, f32[256,128]{1,0:T(8,128)S(1)}, u32[]{:S(2)}, u32[]{:S(2)}) collective-permute-start(f32[256,128]{1,0:T(8,128)S(1)} %get-tuple-element.41), channel_id=1, source_target_pairs={{0,16},{16,32},{32,48},{48,0},{1,17},{17,33},{33,49},{49,1},{2,18}... | collective-permute-start | bytes 393224 | tf_op jit(solution)/shard_map/ppermute | solution.py:83
  98.1 11.8 %collective-permute-start.15 = (f32[256,128]{1,0:T(8,128)S(1)}, f32[256,128]{1,0:T(8,128)S(1)}, u32[]{:S(2)}, u32[]{:S(2)}) collective-permute-start(f32[256,128]{1,0:T(8,128)S(1)} %get-tuple-element.42), channel_id=1, source_target_pairs={{0,32},{16,48},{32,0},{48,16},{1,33},{17,49},{33,1},{49,17},{2,34}... | collective-permute-start | bytes 393224 | tf_op jit(solution)/shard_map/ppermute | solution.py:83
  100.3 11.1 %collective-permute-start.16 = (f32[256,128]{1,0:T(8,128)S(1)}, f32[256,128]{1,0:T(8,128)S(1)}, u32[]{:S(2)}, u32[]{:S(2)}) collective-permute-start(f32[256,128]{1,0:T(8,128)S(1)} %get-tuple-element.43), channel_id=1, source_target_pairs={{0,48},{16,0},{32,16},{48,32},{1,49},{17,1},{33,17},{49,33},{2,50}... | collective-permute-start | bytes 393224 | tf_op jit(solution)/shard_map/ppermute | solution.py:83
  103.5 9.4 %collective-permute-start.25 = (f32[256,128]{1,0:T(8,128)S(1)}, f32[256,128]{1,0:T(8,128)S(1)}, u32[]{:S(2)}, u32[]{:S(2)}) collective-permute-start(f32[256,128]{1,0:T(8,128)S(1)} %get-tuple-element.51), channel_id=1, source_target_pairs={{0,16},{16,32},{32,48},{48,0},{1,17},{17,33},{33,49},{49,1},{2,18}... | collective-permute-start | bytes 393224 | tf_op jit(solution)/shard_map/ppermute | solution.py:83
  109.9 9.3 %collective-permute-start.8 = (f32[384,128]{1,0:T(8,128)S(1)}, f32[384,128]{1,0:T(8,128)S(1)}, u32[]{:S(2)}, u32[]{:S(2)}) collective-permute-start(f32[384,128]{1,0:T(8,128)S(1)} %get-tuple-element.38), channel_id=1, source_target_pairs={{0,32},{16,48},{32,0},{48,16},{1,33},{17,49},{33,1},{49,17},{2,34}... | collective-permute-start | bytes 589832 | tf_op jit(solution)/shard_map/ppermute | solution.py:83
  111.3 11.4 %collective-permute-start.9 = (f32[384,128]{1,0:T(8,128)S(1)}, f32[384,128]{1,0:T(8,128)S(1)}, u32[]{:S(2)}, u32[]{:S(2)}) collective-permute-start(f32[384,128]{1,0:T(8,128)S(1)} %get-tuple-element.39), channel_id=1, source_target_pairs={{0,48},{16,0},{32,16},{48,32},{1,49},{17,1},{33,17},{49,33},{2,50}... | collective-permute-start | bytes 589832 | tf_op jit(solution)/shard_map/ppermute | solution.py:83
  113.0 13.4 %collective-permute-start.26 = (f32[256,128]{1,0:T(8,128)S(1)}, f32[256,128]{1,0:T(8,128)S(1)}, u32[]{:S(2)}, u32[]{:S(2)}) collective-permute-start(f32[256,128]{1,0:T(8,128)S(1)} %get-tuple-element.52), channel_id=1, source_target_pairs={{0,32},{16,48},{32,0},{48,16},{1,33},{17,49},{33,1},{49,17},{2,34}... | collective-permute-start | bytes 393224 | tf_op jit(solution)/shard_map/ppermute | solution.py:83
  113.7 14.1 %collective-permute-start.27 = (f32[256,128]{1,0:T(8,128)S(1)}, f32[256,128]{1,0:T(8,128)S(1)}, u32[]{:S(2)}, u32[]{:S(2)}) collective-permute-start(f32[256,128]{1,0:T(8,128)S(1)} %get-tuple-element.53), channel_id=1, source_target_pairs={{0,48},{16,0},{32,16},{48,32},{1,49},{17,1},{33,17},{49,33},{2,50}... | collective-permute-start | bytes 393224 | tf_op jit(solution)/shard_map/ppermute | solution.py:83
  116.6 14.0 %collective-permute-start.30 = (f32[128,128]{1,0:T(8,128)S(1)}, f32[128,128]{1,0:T(8,128)S(1)}, u32[]{:S(2)}, u32[]{:S(2)}) collective-permute-start(f32[128,128]{1,0:T(8,128)S(1)} %get-tuple-element.55), channel_id=1, source_target_pairs={{0,16},{16,32},{32,48},{48,0},{1,17},{17,33},{33,49},{49,1},{2,18}... | collective-permute-start | bytes 196616 | tf_op jit(solution)/shard_map/ppermute | solution.py:83
  119.2 12.7 %collective-permute-start.31 = (f32[128,128]{1,0:T(8,128)S(1)}, f32[128,128]{1,0:T(8,128)S(1)}, u32[]{:S(2)}, u32[]{:S(2)}) collective-permute-start(f32[128,128]{1,0:T(8,128)S(1)} %get-tuple-element.56), channel_id=1, source_target_pairs={{0,32},{16,48},{32,0},{48,16},{1,33},{17,49},{33,1},{49,17},{2,34}... | collective-permute-start | bytes 196616 | tf_op jit(solution)/shard_map/ppermute | solution.py:83
  122.8 9.2 %collective-permute-start.32 = (f32[128,128]{1,0:T(8,128)S(1)}, f32[128,128]{1,0:T(8,128)S(1)}, u32[]{:S(2)}, u32[]{:S(2)}) collective-permute-start(f32[128,128]{1,0:T(8,128)S(1)} %get-tuple-element.57), channel_id=1, source_target_pairs={{0,48},{16,0},{32,16},{48,32},{1,49},{17,1},{33,17},{49,33},{2,50}... | collective-permute-start | bytes 196616 | tf_op jit(solution)/shard_map/ppermute | solution.py:83
  127.8 8.3 %collective-permute-start.18 = (f32[128,128]{1,0:T(8,128)S(1)}, f32[128,128]{1,0:T(8,128)S(1)}, u32[]{:S(2)}, u32[]{:S(2)}) collective-permute-start(f32[128,128]{1,0:T(8,128)S(1)} %get-tuple-element.46), channel_id=1, source_target_pairs={{0,4},{2,6},{4,0},{6,2},{1,5},{3,7},{5,1},{7,3},{8,12},{10,14},{12... | collective-permute-start | bytes 196616 | tf_op jit(solution)/shard_map/ppermute | solution.py:112
  132.0 8.0 %collective-permute-start.33 = (f32[128,128]{1,0:T(8,128)S(1)}, f32[128,128]{1,0:T(8,128)S(1)}, u32[]{:S(2)}, u32[]{:S(2)}) collective-permute-start(f32[128,128]{1,0:T(8,128)S(1)} %get-tuple-element.59), channel_id=1, source_target_pairs={{0,2},{2,4},{4,6},{6,0},{1,3},{3,5},{5,7},{7,1},{8,10},{10,12},{12... | collective-permute-start | bytes 196616 | tf_op jit(solution)/shard_map/ppermute | solution.py:112
  (9 other events, 51.9 us)

commit v3 on v2

--- a/solution.py
+++ b/solution.py
@@ -56,27 +56,52 @@
     lax.fori_loop(0, 16, step, 0)
 
 
-def product_kernel(n, hi, lo, *refs):
-    blocks, outs = refs[: 2 * n], refs[2 * n :]
+def product(blocks, hi, lo):
     v = jnp.concatenate([b[...] for b in blocks], 0)
     top = v.astype(BF16)
     low = (v - top.astype(F32)).astype(BF16)
     both = jnp.concatenate([top, low], 0)
-    rows = n * 128
+    rows, parts = v.shape[0], []
     for half in range(2):
         cols = slice(half * 256, (half + 1) * 256)
         p = lax.dot_general(both, hi[cols, :], NT, preferred_element_type=F32)
         r = lax.dot_general(top, lo[cols, :], NT, preferred_element_type=F32)
         total = (p[:rows] + p[rows:]) + r
-        outs[2 * half][...] = total[:, :128]
-        outs[2 * half + 1][...] = total[:, 128:]
-
-
-def products(hi, lo, pairs):
-    n = len(pairs)
-    flat = [b for pair in pairs for b in pair]
-    shapes = [((n * 128, 128), F32)] * 4
-    return call(lambda *r: product_kernel(n, *r), shapes, hi, lo, *flat)
+        parts += [total[:, :128], total[:, 128:]]
+    return parts
+
+
+def products(hi, lo, blocks, groups=1):
+    rows = sum(b.shape[0] for b in blocks) // groups
+
+    def kernel(hi, lo, *refs):
+        n = len(blocks)
+        for q, part in enumerate(product(refs[:n], hi, lo)):
+            for g in range(groups):
+                refs[n + 4 * g + q][...] = part[g * rows : (g + 1) * rows]
+
+    outs = call(kernel, [((rows, 128), F32)] * (4 * groups), hi, lo, *blocks)
+    return [outs[4 * g : 4 * g + 4] for g in range(groups)]
+
+
+def last_products(hi, lo, blocks, three):
+
+    def kernel(hi, lo, *refs):
+        n = len(blocks)
+        out = refs[-1]
+        y, zlo = lax.axis_index("y"), lax.axis_index("zlo")
+        four = product(refs[:n], hi, lo)
+        for d, parts in ((3, [r[...] for r in refs[n : n + 4]]), (4, four)):
+            xb = lax.rem(zlo + d, 2)
+            for q in range(4):
+                to = lax.rem(y + q, 4) * 4 + xb * 2
+                for yh in range(2):
+                    for h in range(2):
+                        at = pl.multiple_of((to + yh) * 64 + h * 32, 32)
+                        src = h * 64 + yh * 32
+                        out[pl.ds(at, 32), :] = parts[q][src : src + 32]
+
+    return call(kernel, [((1024, 128), F32)], hi, lo, *blocks, *three)[0]
 
 
 def to_y(parts):
@@ -109,14 +134,50 @@
     body = lambda *r: x_kernel(picks, r[:n], r[n : n + 4], r[n + 4])
     scratch = [pltpu.VMEM((4, 128, 128), F32)]
     outs = call(body, [((128, 128), F32)] * 4, *flat, scratch=scratch)
-    got = [outs[0]] + [lax.ppermute(outs[q], "x", ring(4, q)) for q in range(1, 4)]
-
-    def add(a, b, c, d, keep, send):
-        v = (a[...] + b[...]) + (c[...] + d[...])
-        keep[...] = v[:64]
-        send[...] = v[64:]
-
-    keep, send = call(add, [((64, 128), F32)] * 2, *got)
+    return [outs[0]] + [lax.ppermute(outs[q], "x", ring(4, q)) for q in range(1, 4)]
+
+
+def to_x_pair(even, odd, at):
+
+    def kernel(*refs):
+        sums, outs = refs[-1], refs[8:12]
+        for parity, four, row in ((0, refs[:4], at), (1, refs[4:8], 0)):
+            rows = pl.ds(row * 128, 128)
+            v = [r[rows, :] for r in four]
+            sums[parity] = (v[0] + v[1]) + (v[2] + v[3])
+        x, zlo = lax.axis_index("x"), lax.axis_index("zlo")
+        for ahead in range(4):
+            to = lax.rem(x + ahead, 4)
+            which, yh = lax.rem(to // 2 + zlo, 2), lax.rem(to, 2)
+            for h in range(2):
+                src = pl.ds(pl.multiple_of(h * 64 + yh * 32, 32), 32)
+                outs[ahead][h * 32 : h * 32 + 32, :] = sums[which, src, :]
+
+    scratch = [pltpu.VMEM((2, 128, 128), F32)]
+    outs = call(kernel, [((64, 128), F32)] * 4, *even, *odd, scratch=scratch)
+    return [outs[0]] + [lax.ppermute(outs[q], "x", ring(4, q)) for q in range(1, 4)]
+
+
+def add_early(a, b, c, d, keep, send):
+    v = (a[...] + b[...]) + (c[...] + d[...])
+    keep[...] = v[:64]
+    send[...] = v[64:]
+
+
+def add_late(a, b, c, d, many, keep, send):
+    early = (a[...] + b[...]) + (c[...] + d[...])
+    v = [many[i * 64 : (i + 1) * 64, :] for i in range(16)]
+    while len(v) > 1:
+        v = [p + q for p, q in zip(v[::2], v[1::2])]
+    x, zhi, zlo = lax.axis_index("x"), lax.axis_index("zhi"), lax.axis_index("zlo")
+    ahead = jnp.where(lax.rem(x // 2 + zlo, 2) == 0, 2, 5)
+    home = lax.rem(zlo + ahead, 4) // 2 == zhi
+    keep[...] = jnp.where(home, early, v[0])
+    send[...] = jnp.where(home, v[0], early)
+
+
+def to_owner(kernel, *args):
+    keep, send = call(kernel, [((64, 128), F32)] * 2, *args)
     return keep, lax.ppermute(send, "zhi", ring(2, 1))
 
 
@@ -159,24 +220,35 @@
 
     held = {(0, 0): mine, (0, 1): same}
 
+    last = []
+
     def forward(d, h):
-        if d < 4 or h == 0:
-            held[(d, h)] = lax.ppermute(held[(d - 1, h)], Z, z_ring(-1))
-        if d < 4 or h == 1:
-            held[(-d % 8, h)] = lax.ppermute(held[((1 - d) % 8, h)], Z, z_ring(1))
+        ahead, behind = held[(d - 1, h)], held[((1 - d) % 8, h)]
+        if d == 4:
+            ahead, behind = ahead[:32], behind[32:]
+        ahead = lax.ppermute(ahead, Z, z_ring(-1))
+        behind = lax.ppermute(behind, Z, z_ring(1))
+        if d == 4:
+            last.extend((ahead, behind))
+        else:
+            held[(d, h)], held[(-d % 8, h)] = ahead, behind
 
     for d in range(1, 5):
         for h in range(2):
             forward(d, h)
     app_other = lax.ppermute(app, "core", swap)
     hi, lo = call(own_kernel, [((512, K), BF16)] * 2, orb, same, cross, app, app_other)
-    pair = lambda d: (held[(d % 8, 0)], held[(d % 8, 1)])
-    y1 = to_y(products(hi, lo, [pair(0), pair(1), pair(-1)]))
-    y2 = to_y(products(hi, lo, [pair(2), pair(-2)]))
-    y3 = to_y(products(hi, lo, [pair(3), pair(-3)]))
-    y4 = to_y(products(hi, lo, [pair(4)]))
-    keep_a, recv_a = to_x([y1, y2], [(0, 0), (0, 1), (1, 1), (0, 2)])
-    keep_b, recv_b = to_x([y2, y3, y4], [(2, 0), (1, 1), (0, 0), (1, 0)])
+    blocks = lambda *ds: [held[(d % 8, h)] for d in ds for h in range(2)]
+    y1 = to_y(products(hi, lo, blocks(0, 1, -1))[0])
+    y2 = to_y(products(hi, lo, blocks(2, -2))[0])
+    three, behind = products(hi, lo, blocks(3, -3), 2)
+    y3 = to_y(behind)
+    late = last_products(hi, lo, last, three)
+    late = lax.all_to_all(late, ("y", "x"), split_axis=0, concat_axis=0, tiled=True)
+    xa = to_x([y1, y2], [(0, 0), (0, 1), (1, 1), (0, 2)])
+    xb = to_x_pair(y2, y3, 0)
+    keep_a, recv_a = to_owner(add_early, *xa)
+    keep_b, recv_b = to_owner(add_late, *xb, late)
     return call(tile_kernel, [((128, 128), F32)] * 2, keep_a, recv_a, keep_b, recv_b)
 
 

time: 149 us -> 169 us (1.13)
  waiting for transfers between devices: 59.1 us -> 75.8 us
  local copies, waits for them, and re-layouts: 2.62 us -> 4.39 us
    ppermute x16 -> x21, waiting for transfers between devices: 40.8 us -> 52.4 us  [the longest x8 45.2 us: forward(): behind = lax.ppermute(behind, Z, z_ring(1))]
    all_to_all x0 -> x1, starting transfers between devices: none -> 7.26 us  [body(): lax.all_to_all(late, ('y', 'x'), split_axis=0, concat_axis=0, tiled=True)]
    ppermute x12 -> x9, starting transfers between devices: 17.9 us -> 11.5 us  [to_y(): sent = [lax.ppermute(parts[q], 'y', ring(4, q)) for q in range(1, 4)]]
    ppermute x12 -> x9, waiting for transfers between devices: 5.07 us -> 10.2 us  [to_y(): sent = [lax.ppermute(parts[q], 'y', ring(4, q)) for q in range(1, 4)]]
    ppermute x6 -> x3, starting transfers between devices: 9.68 us -> 5.69 us  [to_x(): lax.ppermute(outs[q], 'x', ring(4, q))]
    ppermute x16 -> x21, starting transfers between devices: 33.6 us -> 35.5 us  [the longest x8 22.8 us: forward(): ahead = lax.ppermute(ahead, Z, z_ring(-1))]
    unnamed x4 -> x22, local copies, waits for them, and re-layouts: 1.78 us -> 3.49 us
  transfers between devices with their start and end apart: 39 -> 39, of which waited for: 14 -> 15; matrix products, arithmetic and copies ran while one was open for 0% -> 0% of each run, Pallas kernels for 7% -> 6%
where the time goes in v3:
time: 169 us; the launch traced here: 167 us
  waiting for transfers between devices  75.8 us (45%)
  starting transfers between devices  73.9 us (44%)
  Pallas kernels  12.3 us (7%)
  local copies, waits for them, and re-layouts  4.39 us (3%)
    ppermute x8, waiting for transfers between devices, forward(): behind = lax.ppermute(behind, Z, z_ring(1))  45.2 us
    ppermute x8, starting transfers between devices, forward(): ahead = lax.ppermute(ahead, Z, z_ring(-1))  22.8 us
    all_to_all x1, waiting for transfers between devices, body(): lax.all_to_all(orbitals, ('y', 'x'), split_axis=1, concat_axis=0, tiled=T...  13.2 us
    pallas_call x10, Pallas kernels, call(): pl.pallas_call(kernel, out_shape=out, in_specs=[VMEM] * len(args), out_sp...  12.3 us
    ppermute x9, starting transfers between devices, to_y(): sent = [lax.ppermute(parts[q], 'y', ring(4, q)) for q in range(1, 4)]  11.5 us
    ppermute x9, waiting for transfers between devices, to_y(): sent = [lax.ppermute(parts[q], 'y', ring(4, q)) for q in range(1, 4)]  10.2 us
    all_to_all x1, starting transfers between devices, body(): lax.all_to_all(orbitals, ('y', 'x'), split_axis=1, concat_axis=0, tiled=T...  7.41 us
    all_to_all x1, starting transfers between devices, body(): lax.all_to_all(late, ('y', 'x'), split_axis=0, concat_axis=0, tiled=True)  7.26 us
  transfers between devices with their start and end apart: 39, of which 15 were waited for; matrix products, arithmetic and copies ran while one was open for 0% of the time, Pallas kernels for 6%

profile of v3, /device:TPU:8, one launch (start us, length us, event | category | flops | bytes accessed | tf_op | source)
XLA Modules:
  0.0 167.2 jit_solution(17477117037970943123)
XLA Ops:
  0.6 7.4 %all-to-all-start = ((f32[8,16,1792]{2,0,1:T(8,128)}), f32[8,16,1792]{2,0,1:T(8,128)S(1)}, u32[]{:S(2)}, u32[]{:S(2)}) async-start(f32[8,16,1792]{2,0,1:T(8,128)} %bitcast.23), calls=%async_computation | async-start | bytes 1835008 | tf_op jit(solution)/shard_map/all_to_all | solution.py:213
  8.0 13.2 %all-to-all-done = f32[8,16,1792]{2,0,1:T(8,128)S(1)} async-done(((f32[8,16,1792]{2,0,1:T(8,128)}), f32[8,16,1792]{2,0,1:T(8,128)S(1)}, u32[]{:S(2)}, u32[]{:S(2)}) %all-to-all-start) | async-done | bytes 917536 | tf_op jit(solution)/shard_map/all_to_all | solution.py:213
  22.0 5.9 %collective-permute-start.3 = (f32[64,1792]{1,0:T(8,128)S(1)}, f32[64,1792]{1,0:T(8,128)S(1)}, u32[]{:S(2)}, u32[]{:S(2)}) collective-permute-start(f32[64,1792]{1,0:T(8,128)S(1)} %bitcast.19), channel_id=1, source_target_pairs={{0,200},{64,0},{128,64},{192,128},{8,192},{72,8},{136,72},{200,136... | collective-permute-start | bytes 1376264 | tf_op jit(solution)/shard_map/ppermute | solution.py:229
  27.9 6.5 %all-to-all-start.1 = ((f32[8,16,1792]{2,0,1:T(8,128)}), f32[8,16,1792]{2,0,1:T(8,128)S(1)}, u32[]{:S(2)}, u32[]{:S(2)}) async-start(f32[8,16,1792]{2,0,1:T(8,128)} %bitcast.24), calls=%async_computation.1 | async-start | bytes 1835008 | tf_op jit(solution)/shard_map/all_to_all | solution.py:219
  34.4 3.2 %collective-permute-start.4 = (f32[64,1792]{1,0:T(8,128)S(1)}, f32[64,1792]{1,0:T(8,128)}, u32[]{:S(2)}, u32[]{:S(2)}) collective-permute-start(f32[64,1792]{1,0:T(8,128)S(1)} %collective-permute-done.same.refs_1_), channel_id=1, source_target_pairs={{0,200},{64,0},{128,64},{192,128},{8,192},{72,8},{136,72},{200,136... | collective-permute-start | bytes 1376264 | tf_op jit(solution)/shard_map/ppermute | solution.py:229
  38.8 3.7 %collective-permute-start.10 = (f32[64,1792]{1,0:T(8,128)S(1)}, f32[64,1792]{1,0:T(8,128)}, u32[]{:S(2)}, u32[]{:S(2)}) collective-permute-start(f32[64,1792]{1,0:T(8,128)S(1)} %collective-permute-done.3.refs_2_), channel_id=1, source_target_pairs={{0,200},{64,0},{128,64},{192,128},{8,192},{72,8},{136,72},{200,136... | collective-permute-start | bytes 1376264 | tf_op jit(solution)/shard_map/ppermute | solution.py:229
  43.3 5.8 %collective-permute-done.5.refs_4_ = f32[64,1792]{1,0:T(8,128)} collective-permute-done((f32[64,1792]{1,0:T(8,128)S(1)}, f32[64,1792]{1,0:T(8,128)}, u32[]{:S(2)}, u32[]{:S(2)}) %collective-permute-start.5) | collective-permute-done | bytes 458784 | tf_op jit(solution)/shard_map/ppermute | solution.py:230
  49.1 3.4 %collective-permute-start.11 = (f32[64,1792]{1,0:T(8,128)}, f32[64,1792]{1,0:T(8,128)}, u32[]{:S(2)}, u32[]{:S(2)}) collective-permute-start(f32[64,1792]{1,0:T(8,128)} %collective-permute-done.4.refs_3_), channel_id=1, source_target_pairs={{0,200},{64,0},{128,64},{192,128},{8,192},{72,8},{136,72},{200,136... | collective-permute-start | bytes 1376264 | tf_op jit(solution)/shard_map/ppermute | solution.py:229
  52.4 6.5 %collective-permute-done.6.refs_5_ = f32[64,1792]{1,0:T(8,128)} collective-permute-done((f32[64,1792]{1,0:T(8,128)S(1)}, f32[64,1792]{1,0:T(8,128)}, u32[]{:S(2)}, u32[]{:S(2)}) %collective-permute-start.6) | collective-permute-done | bytes 458784 | tf_op jit(solution)/shard_map/ppermute | solution.py:230
  58.9 3.4 %collective-permute-start.21 = (f32[64,1792]{1,0:T(8,128)}, f32[64,1792]{1,0:T(8,128)S(1)}, u32[]{:S(2)}, u32[]{:S(2)}) collective-permute-start(f32[64,1792]{1,0:T(8,128)} %collective-permute-done.10.refs_0_), channel_id=1, source_target_pairs={{0,200},{64,0},{128,64},{192,128},{8,192},{72,8},{136,72},{200,136... | collective-permute-start | bytes 1376264 | tf_op jit(solution)/shard_map/ppermute | solution.py:229
  62.3 6.5 %collective-permute-done.12.refs_2_ = f32[64,1792]{1,0:T(8,128)} collective-permute-done((f32[64,1792]{1,0:T(8,128)}, f32[64,1792]{1,0:T(8,128)}, u32[]{:S(2)}, u32[]{:S(2)}) %collective-permute-start.12) | collective-permute-done | bytes 458784 | tf_op jit(solution)/shard_map/ppermute | solution.py:230
  68.7 3.4 %collective-permute-start.22 = (f32[64,1792]{1,0:T(8,128)}, f32[64,1792]{1,0:T(8,128)S(1)}, u32[]{:S(2)}, u32[]{:S(2)}) collective-permute-start(f32[64,1792]{1,0:T(8,128)} %collective-permute-done.11.refs_1_), channel_id=1, source_target_pairs={{0,200},{64,0},{128,64},{192,128},{8,192},{72,8},{136,72},{200,136... | collective-permute-start | bytes 1376264 | tf_op jit(solution)/shard_map/ppermute | solution.py:229
  72.1 6.5 %collective-permute-done.13.refs_3_ = f32[64,1792]{1,0:T(8,128)} collective-permute-done((f32[64,1792]{1,0:T(8,128)}, f32[64,1792]{1,0:T(8,128)}, u32[]{:S(2)}, u32[]{:S(2)}) %collective-permute-start.13) | collective-permute-done | bytes 458784 | tf_op jit(solution)/shard_map/ppermute | solution.py:230
  78.7 9.6 %collective-permute-done.23.refs_2_ = f32[64,1792]{1,0:T(8,128)S(1)} collective-permute-done((f32[64,1792]{1,0:T(8,128)}, f32[64,1792]{1,0:T(8,128)S(1)}, u32[]{:S(2)}, u32[]{:S(2)}) %collective-permute-start.23) | collective-permute-done | bytes 458784 | tf_op jit(solution)/shard_map/ppermute | solution.py:230
  88.3 2.1 %collective-permute-start.32 = (f32[32,1792]{1,0:T(8,128)S(1)}, f32[32,1792]{1,0:T(8,128)S(1)}, u32[]{:S(2)}, u32[]{:S(2)}) collective-permute-start(f32[32,1792]{1,0:T(8,128)S(1)} %slice.17), channel_id=1, source_target_pairs={{0,64},{64,128},{128,192},{192,8},{8,72},{72,136},{136,200},{200,0... | collective-permute-start | bytes 688136 | tf_op jit(solution)/shard_map/ppermute | solution.py:230
  90.5 7.7 %collective-permute-done.24.refs_3_ = f32[64,1792]{1,0:T(8,128)S(1)} collective-permute-done((f32[64,1792]{1,0:T(8,128)}, f32[64,1792]{1,0:T(8,128)S(1)}, u32[]{:S(2)}, u32[]{:S(2)}) %collective-permute-start.24) | collective-permute-done | bytes 458784 | tf_op jit(solution)/shard_map/ppermute | solution.py:230
  98.2 2.1 %collective-permute-start.34 = (f32[32,1792]{1,0:T(8,128)S(1)}, f32[32,1792]{1,0:T(8,128)S(1)}, u32[]{:S(2)}, u32[]{:S(2)}) collective-permute-start(f32[32,1792]{1,0:T(8,128)S(1)} %slice.19), channel_id=1, source_target_pairs={{0,64},{64,128},{128,192},{192,8},{8,72},{72,136},{136,200},{200,0... | collective-permute-start | bytes 688136 | tf_op jit(solution)/shard_map/ppermute | solution.py:230
  104.2 2.8 %collective-permute-done.34.refs_3_ = f32[32,1792]{1,0:T(8,128)S(1)} collective-permute-done((f32[32,1792]{1,0:T(8,128)S(1)}, f32[32,1792]{1,0:T(8,128)S(1)}, u32[]{:S(2)}, u32[]{:S(2)}) %collective-permute-start.34) | collective-permute-done | bytes 229408 | tf_op jit(solution)/shard_map/ppermute | solution.py:230
  106.9 2.0 %shard_map.48 = f32[1024,128]{1,0:T(8,128)} custom-call(bf16[512,1792]{1,0:T(8,128)(2,1)S(1)} %get-tuple-element.34.hi, bf16[512,1792]{1,0:T(8,128)(2,1)S(1)} %get-tuple-element.35.lo, f32[32,1792]{1,0:T(8,128)S(1)} %collective-permute-done.31.refs_0_, f32[32,1792]{1,0:T(8,128)S(1)} %collective-permute-done.32.refs_1_, ...), custom_call_target="tpu_custom_call" | custom-call | tf_op jit(solution)/shard_map/pallas_call | solution.py:28
  108.9 7.3 %all-to-all-start.2 = ((f32[16,64,128]{2,1,0:T(8,128)}), f32[16,64,128]{2,1,0:T(8,128)S(1)}, u32[]{:S(2)}, u32[]{:S(2)}) async-start(f32[16,64,128]{2,1,0:T(8,128)} %bitcast.11), calls=%async_computation.2 | async-start | bytes 1048576 | tf_op jit(solution)/shard_map/all_to_all | solution.py:247
  117.7 3.2 %shard_map.43 = (f32[256,128]{1,0:T(8,128)S(1)}, f32[256,128]{1,0:T(8,128)S(1)}, f32[256,128]{1,0:T(8,128)S(1)}, f32[256,128]{1,0:T(8,128)S(1)}) custom-call(bf16[512,1792]{1,0:T(8,128)(2,1)S(1)} %get-tuple-element.34.hi, bf16[512,1792]{1,0:T(8,128)(2,1)S(1)} %copy-done.1, f32[64,1792]{1,0:T(8,128)} %collective-permute-done.10.refs_0_, ...), custom_call_target="tpu_custom_call" | custom-call | tf_op jit(solution)/shard_map/pallas_call | solution.py:28
  122.5 3.6 %shard_map.42 = (f32[384,128]{1,0:T(8,128)S(1)}, f32[384,128]{1,0:T(8,128)S(1)}, f32[384,128]{1,0:T(8,128)S(1)}, f32[384,128]{1,0:T(8,128)S(1)}) custom-call(bf16[512,1792]{1,0:T(8,128)(2,1)S(1)} %get-tuple-element.34.hi, bf16[512,1792]{1,0:T(8,128)(2,1)S(1)} %copy-done.2, f32[64,1792]{1,0:T(8,128)S(1)} %bitcast.22, ...), custom_call_target="tpu_custom_call" | custom-call | tf_op jit(solution)/shard_map/pallas_call | solution.py:28
  129.5 1.6 collective-permute-start.15
  131.1 1.8 %collective-permute-start.16 = (f32[256,128]{1,0:T(8,128)S(1)}, f32[256,128]{1,0:T(8,128)S(1)}, u32[]{:S(2)}, u32[]{:S(2)}) collective-permute-start(f32[256,128]{1,0:T(8,128)S(1)} %get-tuple-element.43), channel_id=1, source_target_pairs={{0,48},{16,0},{32,16},{48,32},{1,49},{17,1},{33,17},{49,33},{2,50}... | collective-permute-start | bytes 393224 | tf_op jit(solution)/shard_map/ppermute | solution.py:108
  132.9 9.3 %collective-permute-done.15.r_6_.refs_2_ = f32[256,128]{1,0:T(8,128)S(1)} collective-permute-done((f32[256,128]{1,0:T(8,128)S(1)}, f32[256,128]{1,0:T(8,128)S(1)}, u32[]{:S(2)}, u32[]{:S(2)}) %collective-permute-start.15) | collective-permute-done | bytes 131104 | tf_op jit(solution)/shard_map/ppermute | solution.py:108
  143.1 1.8 %collective-permute-start.26 = (f32[128,128]{1,0:T(8,128)S(1)}, f32[128,128]{1,0:T(8,128)S(1)}, u32[]{:S(2)}, u32[]{:S(2)}) collective-permute-start(f32[128,128]{1,0:T(8,128)S(1)} %get-tuple-element.52), channel_id=1, source_target_pairs={{0,32},{16,48},{32,0},{48,16},{1,33},{17,49},{33,1},{49,17},{2,34}... | collective-permute-start | bytes 196616 | tf_op jit(solution)/shard_map/ppermute | solution.py:108
  147.9 2.7 %collective-permute-start.18 = (f32[128,128]{1,0:T(8,128)S(1)}, f32[128,128]{1,0:T(8,128)S(1)}, u32[]{:S(2)}, u32[]{:S(2)}) collective-permute-start(f32[128,128]{1,0:T(8,128)S(1)} %get-tuple-element.46), channel_id=1, source_target_pairs={{0,4},{2,6},{4,0},{6,2},{1,5},{3,7},{5,1},{7,3},{8,12},{10,14},{12... | collective-permute-start | bytes 196616 | tf_op jit(solution)/shard_map/ppermute | solution.py:137
  153.9 1.6 collective-permute-start.30
  155.5 1.9 %collective-permute-start.20 = (f32[64,128]{1,0:T(8,128)S(1)}, f32[64,128]{1,0:T(8,128)S(1)}, u32[]{:S(2)}, u32[]{:S(2)}) collective-permute-start(f32[64,128]{1,0:T(8,128)S(1)} %get-tuple-element.49), channel_id=1, source_target_pairs={{0,8},{8,0},{1,9},{9,1},{2,10},{10,2},{3,11},{11,3},{4,12},{12,4},... | collective-permute-start | bytes 98312 | tf_op jit(solution)/shard_map/ppermute | solution.py:181
  158.6 3.2 %collective-permute-start.35 = (f32[64,128]{1,0:T(8,128)S(1)}, f32[64,128]{1,0:T(8,128)S(1)}, u32[]{:S(2)}, u32[]{:S(2)}) collective-permute-start(f32[64,128]{1,0:T(8,128)S(1)} %get-tuple-element.63), channel_id=1, source_target_pairs={{0,8},{8,0},{1,9},{9,1},{2,10},{10,2},{3,11},{11,3},{4,12},{12,4},... | collective-permute-start | bytes 98312 | tf_op jit(solution)/shard_map/ppermute | solution.py:181
  161.7 1.8 %collective-permute-done.20.recv_a = f32[64,128]{1,0:T(8,128)S(1)} collective-permute-done((f32[64,128]{1,0:T(8,128)S(1)}, f32[64,128]{1,0:T(8,128)S(1)}, u32[]{:S(2)}, u32[]{:S(2)}) %collective-permute-start.20) | collective-permute-done | bytes 32800 | tf_op jit(solution)/shard_map/ppermute | solution.py:181
  163.5 3.0 %collective-permute-done.35.recv_b = f32[64,128]{1,0:T(8,128)S(1)} collective-permute-done((f32[64,128]{1,0:T(8,128)S(1)}, f32[64,128]{1,0:T(8,128)S(1)}, u32[]{:S(2)}, u32[]{:S(2)}) %collective-permute-start.35) | collective-permute-done | bytes 32800 | tf_op jit(solution)/shard_map/ppermute | solution.py:181
  (83 shorter events, 22.4 us)
Async XLA Ops:
  0.6 20.6 %all-to-all-start = ((f32[8,16,1792]{2,0,1:T(8,128)}), f32[8,16,1792]{2,0,1:T(8,128)S(1)}, u32[]{:S(2)}, u32[]{:S(2)}) async-start(f32[8,16,1792]{2,0,1:T(8,128)} %bitcast.23), calls=%async_computation | async-start | bytes 1835008 | tf_op jit(solution)/shard_map/all_to_all | solution.py:213
  22.0 12.3 %collective-permute-start = (f32[64,1792]{1,0:T(8,128)}, f32[64,1792]{1,0:T(8,128)S(1)}, u32[]{:S(2)}, u32[]{:S(2)}) collective-permute-start(f32[64,1792]{1,0:T(8,128)} %bitcast.4), channel_id=1, source_target_pairs={{0,1},{1,0},{2,3},{3,2},{4,5},{5,4},{6,7},{7,6},{8,9},{9,8},{10,11... | collective-permute-start | bytes 1376264 | tf_op jit(solution)/shard_map/ppermute | solution.py:217
  22.0 16.8 %collective-permute-start.3 = (f32[64,1792]{1,0:T(8,128)S(1)}, f32[64,1792]{1,0:T(8,128)S(1)}, u32[]{:S(2)}, u32[]{:S(2)}) collective-permute-start(f32[64,1792]{1,0:T(8,128)S(1)} %bitcast.19), channel_id=1, source_target_pairs={{0,200},{64,0},{128,64},{192,128},{8,192},{72,8},{136,72},{200,136... | collective-permute-start | bytes 1376264 | tf_op jit(solution)/shard_map/ppermute | solution.py:229
  27.9 34.4 %all-to-all-start.1 = ((f32[8,16,1792]{2,0,1:T(8,128)}), f32[8,16,1792]{2,0,1:T(8,128)S(1)}, u32[]{:S(2)}, u32[]{:S(2)}) async-start(f32[8,16,1792]{2,0,1:T(8,128)} %bitcast.24), calls=%async_computation.1 | async-start | bytes 1835008 | tf_op jit(solution)/shard_map/all_to_all | solution.py:219
  34.4 14.7 %collective-permute-start.5 = (f32[64,1792]{1,0:T(8,128)S(1)}, f32[64,1792]{1,0:T(8,128)}, u32[]{:S(2)}, u32[]{:S(2)}) collective-permute-start(f32[64,1792]{1,0:T(8,128)S(1)} %bitcast.20), channel_id=1, source_target_pairs={{0,64},{64,128},{128,192},{192,8},{8,72},{72,136},{136,200},{200,0... | collective-permute-start | bytes 1376264 | tf_op jit(solution)/shard_map/ppermute | solution.py:230
  34.4 14.7 %collective-permute-start.4 = (f32[64,1792]{1,0:T(8,128)S(1)}, f32[64,1792]{1,0:T(8,128)}, u32[]{:S(2)}, u32[]{:S(2)}) collective-permute-start(f32[64,1792]{1,0:T(8,128)S(1)} %collective-permute-done.same.refs_1_), channel_id=1, source_target_pairs={{0,200},{64,0},{128,64},{192,128},{8,192},{72,8},{136,72},{200,136... | collective-permute-start | bytes 1376264 | tf_op jit(solution)/shard_map/ppermute | solution.py:229
  37.6 21.3 %collective-permute-start.6 = (f32[64,1792]{1,0:T(8,128)S(1)}, f32[64,1792]{1,0:T(8,128)}, u32[]{:S(2)}, u32[]{:S(2)}) collective-permute-start(f32[64,1792]{1,0:T(8,128)S(1)} %collective-permute-done.same.refs_1_), channel_id=1, source_target_pairs={{0,64},{64,128},{128,192},{192,8},{8,72},{72,136},{136,200},{200,0... | collective-permute-start | bytes 1376264 | tf_op jit(solution)/shard_map/ppermute | solution.py:230
  38.8 20.1 %collective-permute-start.10 = (f32[64,1792]{1,0:T(8,128)S(1)}, f32[64,1792]{1,0:T(8,128)}, u32[]{:S(2)}, u32[]{:S(2)}) collective-permute-start(f32[64,1792]{1,0:T(8,128)S(1)} %collective-permute-done.3.refs_2_), channel_id=1, source_target_pairs={{0,200},{64,0},{128,64},{192,128},{8,192},{72,8},{136,72},{200,136... | collective-permute-start | bytes 1376264 | tf_op jit(solution)/shard_map/ppermute | solution.py:229
  49.1 19.7 %collective-permute-start.12 = (f32[64,1792]{1,0:T(8,128)}, f32[64,1792]{1,0:T(8,128)}, u32[]{:S(2)}, u32[]{:S(2)}) collective-permute-start(f32[64,1792]{1,0:T(8,128)} %collective-permute-done.5.refs_4_), channel_id=1, source_target_pairs={{0,64},{64,128},{128,192},{192,8},{8,72},{72,136},{136,200},{200,0... | collective-permute-start | bytes 1376264 | tf_op jit(solution)/shard_map/ppermute | solution.py:230
  49.1 19.7 %collective-permute-start.11 = (f32[64,1792]{1,0:T(8,128)}, f32[64,1792]{1,0:T(8,128)}, u32[]{:S(2)}, u32[]{:S(2)}) collective-permute-start(f32[64,1792]{1,0:T(8,128)} %collective-permute-done.4.refs_3_), channel_id=1, source_target_pairs={{0,200},{64,0},{128,64},{192,128},{8,192},{72,8},{136,72},{200,136... | collective-permute-start | bytes 1376264 | tf_op jit(solution)/shard_map/ppermute | solution.py:229
  58.9 19.7 %collective-permute-start.13 = (f32[64,1792]{1,0:T(8,128)}, f32[64,1792]{1,0:T(8,128)}, u32[]{:S(2)}, u32[]{:S(2)}) collective-permute-start(f32[64,1792]{1,0:T(8,128)} %collective-permute-done.6.refs_5_), channel_id=1, source_target_pairs={{0,64},{64,128},{128,192},{192,8},{8,72},{72,136},{136,200},{200,0... | collective-permute-start | bytes 1376264 | tf_op jit(solution)/shard_map/ppermute | solution.py:230
  58.9 19.7 %collective-permute-start.21 = (f32[64,1792]{1,0:T(8,128)}, f32[64,1792]{1,0:T(8,128)S(1)}, u32[]{:S(2)}, u32[]{:S(2)}) collective-permute-start(f32[64,1792]{1,0:T(8,128)} %collective-permute-done.10.refs_0_), channel_id=1, source_target_pairs={{0,200},{64,0},{128,64},{192,128},{8,192},{72,8},{136,72},{200,136... | collective-permute-start | bytes 1376264 | tf_op jit(solution)/shard_map/ppermute | solution.py:229
  62.3 38.0 %collective-permute-start.2 = (f32[128,1792]{1,0:T(8,128)S(1)}, f32[128,1792]{1,0:T(8,128)S(1)}, u32[]{:S(2)}, u32[]{:S(2)}) collective-permute-start(f32[128,1792]{1,0:T(8,128)S(1)} %bitcast.16), channel_id=1, source_target_pairs={{0,1},{1,0},{2,3},{3,2},{4,5},{5,4},{6,7},{7,6},{8,9},{9,8},{10,11... | collective-permute-start | bytes 2752520 | tf_op jit(solution)/shard_map/ppermute | solution.py:239
  68.7 19.6 %collective-permute-start.23 = (f32[64,1792]{1,0:T(8,128)}, f32[64,1792]{1,0:T(8,128)S(1)}, u32[]{:S(2)}, u32[]{:S(2)}) collective-permute-start(f32[64,1792]{1,0:T(8,128)} %collective-permute-done.12.refs_2_), channel_id=1, source_target_pairs={{0,64},{64,128},{128,192},{192,8},{8,72},{72,136},{136,200},{200,0... | collective-permute-start | bytes 1376264 | tf_op jit(solution)/shard_map/ppermute | solution.py:230
  68.7 19.6 %collective-permute-start.22 = (f32[64,1792]{1,0:T(8,128)}, f32[64,1792]{1,0:T(8,128)S(1)}, u32[]{:S(2)}, u32[]{:S(2)}) collective-permute-start(f32[64,1792]{1,0:T(8,128)} %collective-permute-done.11.refs_1_), channel_id=1, source_target_pairs={{0,200},{64,0},{128,64},{192,128},{8,192},{72,8},{136,72},{200,136... | collective-permute-start | bytes 1376264 | tf_op jit(solution)/shard_map/ppermute | solution.py:229
  78.6 19.6 %collective-permute-start.24 = (f32[64,1792]{1,0:T(8,128)}, f32[64,1792]{1,0:T(8,128)S(1)}, u32[]{:S(2)}, u32[]{:S(2)}) collective-permute-start(f32[64,1792]{1,0:T(8,128)} %collective-permute-done.13.refs_3_), channel_id=1, source_target_pairs={{0,64},{64,128},{128,192},{192,8},{8,72},{72,136},{136,200},{200,0... | collective-permute-start | bytes 1376264 | tf_op jit(solution)/shard_map/ppermute | solution.py:230
  78.6 19.6 %collective-permute-start.1 = (f32[64,1792]{1,0:T(8,128)S(1)}, f32[64,1792]{1,0:T(8,128)S(1)}, u32[]{:S(2)}, u32[]{:S(2)}) collective-permute-start(f32[64,1792]{1,0:T(8,128)S(1)} %bitcast.21), channel_id=1, source_target_pairs={{0,1},{1,0},{2,3},{3,2},{4,5},{5,4},{6,7},{7,6},{8,9},{9,8},{10,11... | collective-permute-start | bytes 1376264 | tf_op jit(solution)/shard_map/ppermute | solution.py:218
  88.3 15.8 %collective-permute-start.31 = (f32[32,1792]{1,0:T(8,128)S(1)}, f32[32,1792]{1,0:T(8,128)S(1)}, u32[]{:S(2)}, u32[]{:S(2)}) collective-permute-start(f32[32,1792]{1,0:T(8,128)S(1)} %slice.16), channel_id=1, source_target_pairs={{0,200},{64,0},{128,64},{192,128},{8,192},{72,8},{136,72},{200,136... | collective-permute-start | bytes 688136 | tf_op jit(solution)/shard_map/ppermute | solution.py:229
  88.3 15.8 %collective-permute-start.32 = (f32[32,1792]{1,0:T(8,128)S(1)}, f32[32,1792]{1,0:T(8,128)S(1)}, u32[]{:S(2)}, u32[]{:S(2)}) collective-permute-start(f32[32,1792]{1,0:T(8,128)S(1)} %slice.17), channel_id=1, source_target_pairs={{0,64},{64,128},{128,192},{192,8},{8,72},{72,136},{136,200},{200,0... | collective-permute-start | bytes 688136 | tf_op jit(solution)/shard_map/ppermute | solution.py:230
  98.2 8.8 %collective-permute-start.34 = (f32[32,1792]{1,0:T(8,128)S(1)}, f32[32,1792]{1,0:T(8,128)S(1)}, u32[]{:S(2)}, u32[]{:S(2)}) collective-permute-start(f32[32,1792]{1,0:T(8,128)S(1)} %slice.19), channel_id=1, source_target_pairs={{0,64},{64,128},{128,192},{192,8},{8,72},{72,136},{136,200},{200,0... | collective-permute-start | bytes 688136 | tf_op jit(solution)/shard_map/ppermute | solution.py:230
  108.9 49.6 %all-to-all-start.2 = ((f32[16,64,128]{2,1,0:T(8,128)}), f32[16,64,128]{2,1,0:T(8,128)S(1)}, u32[]{:S(2)}, u32[]{:S(2)}) async-start(f32[16,64,128]{2,1,0:T(8,128)} %bitcast.11), calls=%async_computation.2 | async-start | bytes 1048576 | tf_op jit(solution)/shard_map/all_to_all | solution.py:247
  120.9 10.2 %collective-permute-start.14 = (f32[256,128]{1,0:T(8,128)S(1)}, f32[256,128]{1,0:T(8,128)S(1)}, u32[]{:S(2)}, u32[]{:S(2)}) collective-permute-start(f32[256,128]{1,0:T(8,128)S(1)} %get-tuple-element.41), channel_id=1, source_target_pairs={{0,16},{16,32},{32,48},{48,0},{1,17},{17,33},{33,49},{49,1},{2,18}... | collective-permute-start | bytes 393224 | tf_op jit(solution)/shard_map/ppermute | solution.py:108
  126.1 18.8 %collective-permute-start.7 = (f32[384,128]{1,0:T(8,128)S(1)}, f32[384,128]{1,0:T(8,128)S(1)}, u32[]{:S(2)}, u32[]{:S(2)}) collective-permute-start(f32[384,128]{1,0:T(8,128)S(1)} %get-tuple-element.37), channel_id=1, source_target_pairs={{0,16},{16,32},{32,48},{48,0},{1,17},{17,33},{33,49},{49,1},{2,18}... | collective-permute-start | bytes 589832 | tf_op jit(solution)/shard_map/ppermute | solution.py:108
  127.3 18.9 %collective-permute-start.8 = (f32[384,128]{1,0:T(8,128)S(1)}, f32[384,128]{1,0:T(8,128)S(1)}, u32[]{:S(2)}, u32[]{:S(2)}) collective-permute-start(f32[384,128]{1,0:T(8,128)S(1)} %get-tuple-element.38), channel_id=1, source_target_pairs={{0,32},{16,48},{32,0},{48,16},{1,33},{17,49},{33,1},{49,17},{2,34}... | collective-permute-start | bytes 589832 | tf_op jit(solution)/shard_map/ppermute | solution.py:108
  128.8 17.5 %collective-permute-start.9 = (f32[384,128]{1,0:T(8,128)S(1)}, f32[384,128]{1,0:T(8,128)S(1)}, u32[]{:S(2)}, u32[]{:S(2)}) collective-permute-start(f32[384,128]{1,0:T(8,128)S(1)} %get-tuple-element.39), channel_id=1, source_target_pairs={{0,48},{16,0},{32,16},{48,32},{1,49},{17,1},{33,17},{49,33},{2,50}... | collective-permute-start | bytes 589832 | tf_op jit(solution)/shard_map/ppermute | solution.py:108
  129.5 12.7 %collective-permute-start.15 = (f32[256,128]{1,0:T(8,128)S(1)}, f32[256,128]{1,0:T(8,128)S(1)}, u32[]{:S(2)}, u32[]{:S(2)}) collective-permute-start(f32[256,128]{1,0:T(8,128)S(1)} %get-tuple-element.42), channel_id=1, source_target_pairs={{0,32},{16,48},{32,0},{48,16},{1,33},{17,49},{33,1},{49,17},{2,34}... | collective-permute-start | bytes 393224 | tf_op jit(solution)/shard_map/ppermute | solution.py:108
  131.1 12.0 %collective-permute-start.16 = (f32[256,128]{1,0:T(8,128)S(1)}, f32[256,128]{1,0:T(8,128)S(1)}, u32[]{:S(2)}, u32[]{:S(2)}) collective-permute-start(f32[256,128]{1,0:T(8,128)S(1)} %get-tuple-element.43), channel_id=1, source_target_pairs={{0,48},{16,0},{32,16},{48,32},{1,49},{17,1},{33,17},{49,33},{2,50}... | collective-permute-start | bytes 393224 | tf_op jit(solution)/shard_map/ppermute | solution.py:108
  142.2 8.3 %collective-permute-start.25 = (f32[128,128]{1,0:T(8,128)S(1)}, f32[128,128]{1,0:T(8,128)S(1)}, u32[]{:S(2)}, u32[]{:S(2)}) collective-permute-start(f32[128,128]{1,0:T(8,128)S(1)} %get-tuple-element.51), channel_id=1, source_target_pairs={{0,16},{16,32},{32,48},{48,0},{1,17},{17,33},{33,49},{49,1},{2,18}... | collective-permute-start | bytes 196616 | tf_op jit(solution)/shard_map/ppermute | solution.py:108
  143.1 8.9 %collective-permute-start.26 = (f32[128,128]{1,0:T(8,128)S(1)}, f32[128,128]{1,0:T(8,128)S(1)}, u32[]{:S(2)}, u32[]{:S(2)}) collective-permute-start(f32[128,128]{1,0:T(8,128)S(1)} %get-tuple-element.52), channel_id=1, source_target_pairs={{0,32},{16,48},{32,0},{48,16},{1,33},{17,49},{33,1},{49,17},{2,34}... | collective-permute-start | bytes 196616 | tf_op jit(solution)/shard_map/ppermute | solution.py:108
  147.9 7.6 %collective-permute-start.18 = (f32[128,128]{1,0:T(8,128)S(1)}, f32[128,128]{1,0:T(8,128)S(1)}, u32[]{:S(2)}, u32[]{:S(2)}) collective-permute-start(f32[128,128]{1,0:T(8,128)S(1)} %get-tuple-element.46), channel_id=1, source_target_pairs={{0,4},{2,6},{4,0},{6,2},{1,5},{3,7},{5,1},{7,3},{8,12},{10,14},{12... | collective-permute-start | bytes 196616 | tf_op jit(solution)/shard_map/ppermute | solution.py:137
  155.5 8.0 %collective-permute-start.20 = (f32[64,128]{1,0:T(8,128)S(1)}, f32[64,128]{1,0:T(8,128)S(1)}, u32[]{:S(2)}, u32[]{:S(2)}) collective-permute-start(f32[64,128]{1,0:T(8,128)S(1)} %get-tuple-element.49), channel_id=1, source_target_pairs={{0,8},{8,0},{1,9},{9,1},{2,10},{10,2},{3,11},{11,3},{4,12},{12,4},... | collective-permute-start | bytes 98312 | tf_op jit(solution)/shard_map/ppermute | solution.py:181
  158.6 7.9 %collective-permute-start.35 = (f32[64,128]{1,0:T(8,128)S(1)}, f32[64,128]{1,0:T(8,128)S(1)}, u32[]{:S(2)}, u32[]{:S(2)}) collective-permute-start(f32[64,128]{1,0:T(8,128)S(1)} %get-tuple-element.63), channel_id=1, source_target_pairs={{0,8},{8,0},{1,9},{9,1},{2,10},{10,2},{3,11},{11,3},{4,12},{12,4},... | collective-permute-start | bytes 98312 | tf_op jit(solution)/shard_map/ppermute | solution.py:181
  (18 other events, 200.0 us)

commit v4 on v3

--- a/solution.py
+++ b/solution.py
@@ -213,19 +213,21 @@
     orb = lax.all_to_all(orbitals, ("y", "x"), split_axis=1, concat_axis=0, tiled=True)
     by_parity = orb.reshape(2, 2, 32, K)
     mine = lax.dynamic_index_in_dim(by_parity, core, 1, False).reshape(64, K)
-    theirs = lax.dynamic_index_in_dim(by_parity, 1 - core, 1, False).reshape(64, K)
+    rest = after(by_parity, mine)
+    theirs = lax.dynamic_index_in_dim(rest, 1 - core, 1, False).reshape(64, K)
     same = lax.ppermute(theirs, "core", swap)
     cross = lax.ppermute(mine, "core", swap)
     app = lax.all_to_all(after(applied, mine), ("y", "x"), split_axis=1, concat_axis=0, tiled=True)
 
     held = {(0, 0): mine, (0, 1): same}
 
-    last = []
+    last, cuts = [], []
 
     def forward(d, h):
         ahead, behind = held[(d - 1, h)], held[((1 - d) % 8, h)]
         if d == 4:
             ahead, behind = ahead[:32], behind[32:]
+            cuts.extend((ahead, behind))
         ahead = lax.ppermute(ahead, Z, z_ring(-1))
         behind = lax.ppermute(behind, Z, z_ring(1))
         if d == 4:
@@ -245,6 +247,7 @@
     y3 = to_y(behind)
     late = last_products(hi, lo, last, three)
     late = lax.all_to_all(late, ("y", "x"), split_axis=0, concat_axis=0, tiled=True)
+    y1[0] = after(y1[0], *cuts[:2])
     xa = to_x([y1, y2], [(0, 0), (0, 1), (1, 1), (0, 2)])
     xb = to_x_pair(y2, y3, 0)
     keep_a, recv_a = to_owner(add_early, *xa)

time: 169 us -> 169 us (level)
    unnamed x22 -> x24, local copies, waits for them, and re-layouts: 3.49 us -> 4.51 us
where the time goes in v4:
time: 169 us; the launch traced here: 167 us
  waiting for transfers between devices  74.8 us (44%)
  starting transfers between devices  73.9 us (44%)
  Pallas kernels  12.3 us (7%)
  local copies, waits for them, and re-layouts  5.42 us (3%)
    ppermute x8, waiting for transfers between devices, forward(): behind = lax.ppermute(behind, Z, z_ring(1))  44.2 us
    ppermute x8, starting transfers between devices, forward(): ahead = lax.ppermute(ahead, Z, z_ring(-1))  22.8 us
    all_to_all x1, waiting for transfers between devices, body(): lax.all_to_all(orbitals, ('y', 'x'), split_axis=1, concat_axis=0, tiled=T...  13.2 us
    pallas_call x10, Pallas kernels, call(): pl.pallas_call(kernel, out_shape=out, in_specs=[VMEM] * len(args), out_sp...  12.3 us
    ppermute x9, starting transfers between devices, to_y(): sent = [lax.ppermute(parts[q], 'y', ring(4, q)) for q in range(1, 4)]  11.5 us
    ppermute x9, waiting for transfers between devices, to_y(): sent = [lax.ppermute(parts[q], 'y', ring(4, q)) for q in range(1, 4)]  10.2 us
    all_to_all x1, starting transfers between devices, body(): lax.all_to_all(orbitals, ('y', 'x'), split_axis=1, concat_axis=0, tiled=T...  7.41 us
    all_to_all x1, starting transfers between devices, body(): lax.all_to_all(late, ('y', 'x'), split_axis=0, concat_axis=0, tiled=True)  7.26 us
  transfers between devices with their start and end apart: 39, of which 15 were waited for; matrix products, arithmetic and copies ran while one was open for 0% of the time, Pallas kernels for 6%

profile of v4, /device:TPU:8, one launch (start us, length us, event | category | flops | bytes accessed | tf_op | source)
XLA Modules:
  0.0 167.3 jit_solution(14247845501706313104)
XLA Ops:
  0.6 7.4 %all-to-all-start = ((f32[8,16,1792]{2,0,1:T(8,128)}), f32[8,16,1792]{2,0,1:T(8,128)S(1)}, u32[]{:S(2)}, u32[]{:S(2)}) async-start(f32[8,16,1792]{2,0,1:T(8,128)} %bitcast.24), calls=%async_computation | async-start | bytes 1835008 | tf_op jit(solution)/shard_map/all_to_all | solution.py:213
  8.0 13.2 %all-to-all-done = f32[8,16,1792]{2,0,1:T(8,128)S(1)} async-done(((f32[8,16,1792]{2,0,1:T(8,128)}), f32[8,16,1792]{2,0,1:T(8,128)S(1)}, u32[]{:S(2)}, u32[]{:S(2)}) %all-to-all-start) | async-done | bytes 917536 | tf_op jit(solution)/shard_map/all_to_all | solution.py:213
  22.1 5.9 %collective-permute-start.3 = (f32[64,1792]{1,0:T(8,128)S(1)}, f32[64,1792]{1,0:T(8,128)S(1)}, u32[]{:S(2)}, u32[]{:S(2)}) collective-permute-start(f32[64,1792]{1,0:T(8,128)S(1)} %bitcast.20), channel_id=1, source_target_pairs={{0,200},{64,0},{128,64},{192,128},{8,192},{72,8},{136,72},{200,136... | collective-permute-start | bytes 1376264 | tf_op jit(solution)/shard_map/ppermute | solution.py:231
  27.9 6.5 %all-to-all-start.1 = ((f32[8,16,1792]{2,0,1:T(8,128)}), f32[8,16,1792]{2,0,1:T(8,128)S(1)}, u32[]{:S(2)}, u32[]{:S(2)}) async-start(f32[8,16,1792]{2,0,1:T(8,128)} %bitcast.25), calls=%async_computation.1 | async-start | bytes 1835008 | tf_op jit(solution)/shard_map/all_to_all | solution.py:220
  34.4 3.2 %collective-permute-start.4 = (f32[64,1792]{1,0:T(8,128)S(1)}, f32[64,1792]{1,0:T(8,128)}, u32[]{:S(2)}, u32[]{:S(2)}) collective-permute-start(f32[64,1792]{1,0:T(8,128)S(1)} %collective-permute-done.same.refs_1_), channel_id=1, source_target_pairs={{0,200},{64,0},{128,64},{192,128},{8,192},{72,8},{136,72},{200,136... | collective-permute-start | bytes 1376264 | tf_op jit(solution)/shard_map/ppermute | solution.py:231
  38.8 3.7 %collective-permute-start.7 = (f32[64,1792]{1,0:T(8,128)S(1)}, f32[64,1792]{1,0:T(8,128)}, u32[]{:S(2)}, u32[]{:S(2)}) collective-permute-start(f32[64,1792]{1,0:T(8,128)S(1)} %collective-permute-done.3.refs_2_), channel_id=1, source_target_pairs={{0,200},{64,0},{128,64},{192,128},{8,192},{72,8},{136,72},{200,136... | collective-permute-start | bytes 1376264 | tf_op jit(solution)/shard_map/ppermute | solution.py:231
  43.3 5.8 %collective-permute-done.5.refs_4_ = f32[64,1792]{1,0:T(8,128)} collective-permute-done((f32[64,1792]{1,0:T(8,128)S(1)}, f32[64,1792]{1,0:T(8,128)}, u32[]{:S(2)}, u32[]{:S(2)}) %collective-permute-start.5) | collective-permute-done | bytes 458784 | tf_op jit(solution)/shard_map/ppermute | solution.py:232
  49.1 3.4 %collective-permute-start.14 = (f32[64,1792]{1,0:T(8,128)}, f32[64,1792]{1,0:T(8,128)}, u32[]{:S(2)}, u32[]{:S(2)}) collective-permute-start(f32[64,1792]{1,0:T(8,128)} %collective-permute-done.4.refs_3_), channel_id=1, source_target_pairs={{0,200},{64,0},{128,64},{192,128},{8,192},{72,8},{136,72},{200,136... | collective-permute-start | bytes 1376264 | tf_op jit(solution)/shard_map/ppermute | solution.py:231
  52.5 6.5 %collective-permute-done.6.refs_5_ = f32[64,1792]{1,0:T(8,128)} collective-permute-done((f32[64,1792]{1,0:T(8,128)S(1)}, f32[64,1792]{1,0:T(8,128)}, u32[]{:S(2)}, u32[]{:S(2)}) %collective-permute-start.6) | collective-permute-done | bytes 458784 | tf_op jit(solution)/shard_map/ppermute | solution.py:232
  58.9 3.4 %collective-permute-start.8 = (f32[64,1792]{1,0:T(8,128)}, f32[64,1792]{1,0:T(8,128)S(1)}, u32[]{:S(2)}, u32[]{:S(2)}) collective-permute-start(f32[64,1792]{1,0:T(8,128)} %collective-permute-done.7.refs_0_), channel_id=1, source_target_pairs={{0,200},{64,0},{128,64},{192,128},{8,192},{72,8},{136,72},{200,136... | collective-permute-start | bytes 1376264 | tf_op jit(solution)/shard_map/ppermute | solution.py:231
  62.3 6.5 %collective-permute-done.9.refs_2_ = f32[64,1792]{1,0:T(8,128)} collective-permute-done((f32[64,1792]{1,0:T(8,128)}, f32[64,1792]{1,0:T(8,128)}, u32[]{:S(2)}, u32[]{:S(2)}) %collective-permute-start.9) | collective-permute-done | bytes 458784 | tf_op jit(solution)/shard_map/ppermute | solution.py:232
  68.8 3.4 %collective-permute-start.23 = (f32[64,1792]{1,0:T(8,128)}, f32[64,1792]{1,0:T(8,128)S(1)}, u32[]{:S(2)}, u32[]{:S(2)}) collective-permute-start(f32[64,1792]{1,0:T(8,128)} %collective-permute-done.14.refs_1_), channel_id=1, source_target_pairs={{0,200},{64,0},{128,64},{192,128},{8,192},{72,8},{136,72},{200,136... | collective-permute-start | bytes 1376264 | tf_op jit(solution)/shard_map/ppermute | solution.py:231
  72.1 6.5 %collective-permute-done.15.refs_3_ = f32[64,1792]{1,0:T(8,128)} collective-permute-done((f32[64,1792]{1,0:T(8,128)}, f32[64,1792]{1,0:T(8,128)}, u32[]{:S(2)}, u32[]{:S(2)}) %collective-permute-start.15) | collective-permute-done | bytes 458784 | tf_op jit(solution)/shard_map/ppermute | solution.py:232
  78.7 9.6 %collective-permute-done.10.refs_2_ = f32[64,1792]{1,0:T(8,128)S(1)} collective-permute-done((f32[64,1792]{1,0:T(8,128)}, f32[64,1792]{1,0:T(8,128)S(1)}, u32[]{:S(2)}, u32[]{:S(2)}) %collective-permute-start.10) | collective-permute-done | bytes 458784 | tf_op jit(solution)/shard_map/ppermute | solution.py:232
  88.3 2.1 %collective-permute-start.32 = (f32[32,1792]{1,0:T(8,128)S(1)}, f32[32,1792]{1,0:T(8,128)S(1)}, u32[]{:S(2)}, u32[]{:S(2)}) collective-permute-start(f32[32,1792]{1,0:T(8,128)S(1)} %slice.17), channel_id=1, source_target_pairs={{0,64},{64,128},{128,192},{192,8},{8,72},{72,136},{136,200},{200,0... | collective-permute-start | bytes 688136 | tf_op jit(solution)/shard_map/ppermute | solution.py:232
  90.5 7.7 %collective-permute-done.24.refs_3_ = f32[64,1792]{1,0:T(8,128)S(1)} collective-permute-done((f32[64,1792]{1,0:T(8,128)}, f32[64,1792]{1,0:T(8,128)S(1)}, u32[]{:S(2)}, u32[]{:S(2)}) %collective-permute-start.24) | collective-permute-done | bytes 458784 | tf_op jit(solution)/shard_map/ppermute | solution.py:232
  98.2 2.1 %collective-permute-start.34 = (f32[32,1792]{1,0:T(8,128)S(1)}, f32[32,1792]{1,0:T(8,128)S(1)}, u32[]{:S(2)}, u32[]{:S(2)}) collective-permute-start(f32[32,1792]{1,0:T(8,128)S(1)} %slice.19), channel_id=1, source_target_pairs={{0,64},{64,128},{128,192},{192,8},{8,72},{72,136},{136,200},{200,0... | collective-permute-start | bytes 688136 | tf_op jit(solution)/shard_map/ppermute | solution.py:232
  103.5 1.6 shard_map.46
  105.2 1.8 %collective-permute-done.34.refs_3_ = f32[32,1792]{1,0:T(8,128)S(1)} collective-permute-done((f32[32,1792]{1,0:T(8,128)S(1)}, f32[32,1792]{1,0:T(8,128)S(1)}, u32[]{:S(2)}, u32[]{:S(2)}) %collective-permute-start.34) | collective-permute-done | bytes 229408 | tf_op jit(solution)/shard_map/ppermute | solution.py:232
  107.0 2.0 %shard_map.48 = f32[1024,128]{1,0:T(8,128)} custom-call(bf16[512,1792]{1,0:T(8,128)(2,1)S(1)} %get-tuple-element.37.hi, bf16[512,1792]{1,0:T(8,128)(2,1)S(1)} %get-tuple-element.38.lo, f32[32,1792]{1,0:T(8,128)S(1)} %collective-permute-done.31.refs_0_, f32[32,1792]{1,0:T(8,128)S(1)} %collective-permute-done.32.refs_1_, ...), custom_call_target="tpu_custom_call" | custom-call | tf_op jit(solution)/shard_map/pallas_call | solution.py:28
  109.0 7.3 %all-to-all-start.2 = ((f32[16,64,128]{2,1,0:T(8,128)}), f32[16,64,128]{2,1,0:T(8,128)S(1)}, u32[]{:S(2)}, u32[]{:S(2)}) async-start(f32[16,64,128]{2,1,0:T(8,128)} %bitcast.11), calls=%async_computation.2 | async-start | bytes 1048576 | tf_op jit(solution)/shard_map/all_to_all | solution.py:249
  117.7 3.2 %shard_map.43 = (f32[256,128]{1,0:T(8,128)S(1)}, f32[256,128]{1,0:T(8,128)S(1)}, f32[256,128]{1,0:T(8,128)S(1)}, f32[256,128]{1,0:T(8,128)S(1)}) custom-call(bf16[512,1792]{1,0:T(8,128)(2,1)S(1)} %get-tuple-element.37.hi, bf16[512,1792]{1,0:T(8,128)(2,1)S(1)} %copy-done.1, f32[64,1792]{1,0:T(8,128)} %collective-permute-done.7.refs_0_, ...), custom_call_target="tpu_custom_call" | custom-call | tf_op jit(solution)/shard_map/pallas_call | solution.py:28
  122.5 3.6 %shard_map.42 = (f32[384,128]{1,0:T(8,128)S(1)}, f32[384,128]{1,0:T(8,128)S(1)}, f32[384,128]{1,0:T(8,128)S(1)}, f32[384,128]{1,0:T(8,128)S(1)}) custom-call(bf16[512,1792]{1,0:T(8,128)(2,1)S(1)} %get-tuple-element.37.hi, bf16[512,1792]{1,0:T(8,128)(2,1)S(1)} %copy-done.2, f32[64,1792]{1,0:T(8,128)S(1)} %bitcast.23, f32[64,1792]{1,0:T(8,128)S(1)} %copy-done.7, ...), custom_call_target="tpu_custom_call" | custom-call | tf_op jit(solution)/shard_map/pallas_call | solution.py:28
  131.1 1.8 %collective-permute-start.18 = (f32[256,128]{1,0:T(8,128)S(1)}, f32[256,128]{1,0:T(8,128)S(1)}, u32[]{:S(2)}, u32[]{:S(2)}) collective-permute-start(f32[256,128]{1,0:T(8,128)S(1)} %get-tuple-element.47), channel_id=1, source_target_pairs={{0,48},{16,0},{32,16},{48,32},{1,49},{17,1},{33,17},{49,33},{2,50}... | collective-permute-start | bytes 393224 | tf_op jit(solution)/shard_map/ppermute | solution.py:108
  132.9 9.3 %collective-permute-done.17.r_6_.refs_2_ = f32[256,128]{1,0:T(8,128)S(1)} collective-permute-done((f32[256,128]{1,0:T(8,128)S(1)}, f32[256,128]{1,0:T(8,128)S(1)}, u32[]{:S(2)}, u32[]{:S(2)}) %collective-permute-start.17) | collective-permute-done | bytes 131104 | tf_op jit(solution)/shard_map/ppermute | solution.py:108
  143.1 1.8 %collective-permute-start.26 = (f32[128,128]{1,0:T(8,128)S(1)}, f32[128,128]{1,0:T(8,128)S(1)}, u32[]{:S(2)}, u32[]{:S(2)}) collective-permute-start(f32[128,128]{1,0:T(8,128)S(1)} %get-tuple-element.56), channel_id=1, source_target_pairs={{0,32},{16,48},{32,0},{48,16},{1,33},{17,49},{33,1},{49,17},{2,34}... | collective-permute-start | bytes 196616 | tf_op jit(solution)/shard_map/ppermute | solution.py:108
  147.9 2.7 %collective-permute-start.20 = (f32[128,128]{1,0:T(8,128)S(1)}, f32[128,128]{1,0:T(8,128)S(1)}, u32[]{:S(2)}, u32[]{:S(2)}) collective-permute-start(f32[128,128]{1,0:T(8,128)S(1)} %get-tuple-element.50), channel_id=1, source_target_pairs={{0,4},{2,6},{4,0},{6,2},{1,5},{3,7},{5,1},{7,3},{8,12},{10,14},{12... | collective-permute-start | bytes 196616 | tf_op jit(solution)/shard_map/ppermute | solution.py:137
  153.9 1.6 collective-permute-start.30
  155.5 1.9 %collective-permute-start.22 = (f32[64,128]{1,0:T(8,128)S(1)}, f32[64,128]{1,0:T(8,128)S(1)}, u32[]{:S(2)}, u32[]{:S(2)}) collective-permute-start(f32[64,128]{1,0:T(8,128)S(1)} %get-tuple-element.53), channel_id=1, source_target_pairs={{0,8},{8,0},{1,9},{9,1},{2,10},{10,2},{3,11},{11,3},{4,12},{12,4},... | collective-permute-start | bytes 98312 | tf_op jit(solution)/shard_map/ppermute | solution.py:181
  158.6 3.2 %collective-permute-start.35 = (f32[64,128]{1,0:T(8,128)S(1)}, f32[64,128]{1,0:T(8,128)S(1)}, u32[]{:S(2)}, u32[]{:S(2)}) collective-permute-start(f32[64,128]{1,0:T(8,128)S(1)} %get-tuple-element.67), channel_id=1, source_target_pairs={{0,8},{8,0},{1,9},{9,1},{2,10},{10,2},{3,11},{11,3},{4,12},{12,4},... | collective-permute-start | bytes 98312 | tf_op jit(solution)/shard_map/ppermute | solution.py:181
  161.7 1.8 %collective-permute-done.22.recv_a = f32[64,128]{1,0:T(8,128)S(1)} collective-permute-done((f32[64,128]{1,0:T(8,128)S(1)}, f32[64,128]{1,0:T(8,128)S(1)}, u32[]{:S(2)}, u32[]{:S(2)}) %collective-permute-start.22) | collective-permute-done | bytes 32800 | tf_op jit(solution)/shard_map/ppermute | solution.py:181
  163.5 3.0 %collective-permute-done.35.recv_b = f32[64,128]{1,0:T(8,128)S(1)} collective-permute-done((f32[64,128]{1,0:T(8,128)S(1)}, f32[64,128]{1,0:T(8,128)S(1)}, u32[]{:S(2)}, u32[]{:S(2)}) %collective-permute-start.35) | collective-permute-done | bytes 32800 | tf_op jit(solution)/shard_map/ppermute | solution.py:181
  (86 shorter events, 23.4 us)
Async XLA Ops:
  0.6 20.6 %all-to-all-start = ((f32[8,16,1792]{2,0,1:T(8,128)}), f32[8,16,1792]{2,0,1:T(8,128)S(1)}, u32[]{:S(2)}, u32[]{:S(2)}) async-start(f32[8,16,1792]{2,0,1:T(8,128)} %bitcast.24), calls=%async_computation | async-start | bytes 1835008 | tf_op jit(solution)/shard_map/all_to_all | solution.py:213
  22.1 12.3 %collective-permute-start = (f32[64,1792]{1,0:T(8,128)}, f32[64,1792]{1,0:T(8,128)S(1)}, u32[]{:S(2)}, u32[]{:S(2)}) collective-permute-start(f32[64,1792]{1,0:T(8,128)} %bitcast.6), channel_id=1, source_target_pairs={{0,1},{1,0},{2,3},{3,2},{4,5},{5,4},{6,7},{7,6},{8,9},{9,8},{10,11... | collective-permute-start | bytes 1376264 | tf_op jit(solution)/shard_map/ppermute | solution.py:218
  22.1 16.8 %collective-permute-start.3 = (f32[64,1792]{1,0:T(8,128)S(1)}, f32[64,1792]{1,0:T(8,128)S(1)}, u32[]{:S(2)}, u32[]{:S(2)}) collective-permute-start(f32[64,1792]{1,0:T(8,128)S(1)} %bitcast.20), channel_id=1, source_target_pairs={{0,200},{64,0},{128,64},{192,128},{8,192},{72,8},{136,72},{200,136... | collective-permute-start | bytes 1376264 | tf_op jit(solution)/shard_map/ppermute | solution.py:231
  27.9 34.4 %all-to-all-start.1 = ((f32[8,16,1792]{2,0,1:T(8,128)}), f32[8,16,1792]{2,0,1:T(8,128)S(1)}, u32[]{:S(2)}, u32[]{:S(2)}) async-start(f32[8,16,1792]{2,0,1:T(8,128)} %bitcast.25), calls=%async_computation.1 | async-start | bytes 1835008 | tf_op jit(solution)/shard_map/all_to_all | solution.py:220
  34.4 14.7 %collective-permute-start.5 = (f32[64,1792]{1,0:T(8,128)S(1)}, f32[64,1792]{1,0:T(8,128)}, u32[]{:S(2)}, u32[]{:S(2)}) collective-permute-start(f32[64,1792]{1,0:T(8,128)S(1)} %bitcast.21), channel_id=1, source_target_pairs={{0,64},{64,128},{128,192},{192,8},{8,72},{72,136},{136,200},{200,0... | collective-permute-start | bytes 1376264 | tf_op jit(solution)/shard_map/ppermute | solution.py:232
  34.4 14.7 %collective-permute-start.4 = (f32[64,1792]{1,0:T(8,128)S(1)}, f32[64,1792]{1,0:T(8,128)}, u32[]{:S(2)}, u32[]{:S(2)}) collective-permute-start(f32[64,1792]{1,0:T(8,128)S(1)} %collective-permute-done.same.refs_1_), channel_id=1, source_target_pairs={{0,200},{64,0},{128,64},{192,128},{8,192},{72,8},{136,72},{200,136... | collective-permute-start | bytes 1376264 | tf_op jit(solution)/shard_map/ppermute | solution.py:231
  37.6 21.3 %collective-permute-start.6 = (f32[64,1792]{1,0:T(8,128)S(1)}, f32[64,1792]{1,0:T(8,128)}, u32[]{:S(2)}, u32[]{:S(2)}) collective-permute-start(f32[64,1792]{1,0:T(8,128)S(1)} %collective-permute-done.same.refs_1_), channel_id=1, source_target_pairs={{0,64},{64,128},{128,192},{192,8},{8,72},{72,136},{136,200},{200,0... | collective-permute-start | bytes 1376264 | tf_op jit(solution)/shard_map/ppermute | solution.py:232
  38.8 20.1 %collective-permute-start.7 = (f32[64,1792]{1,0:T(8,128)S(1)}, f32[64,1792]{1,0:T(8,128)}, u32[]{:S(2)}, u32[]{:S(2)}) collective-permute-start(f32[64,1792]{1,0:T(8,128)S(1)} %collective-permute-done.3.refs_2_), channel_id=1, source_target_pairs={{0,200},{64,0},{128,64},{192,128},{8,192},{72,8},{136,72},{200,136... | collective-permute-start | bytes 1376264 | tf_op jit(solution)/shard_map/ppermute | solution.py:231
  49.1 19.7 %collective-permute-start.9 = (f32[64,1792]{1,0:T(8,128)}, f32[64,1792]{1,0:T(8,128)}, u32[]{:S(2)}, u32[]{:S(2)}) collective-permute-start(f32[64,1792]{1,0:T(8,128)} %collective-permute-done.5.refs_4_), channel_id=1, source_target_pairs={{0,64},{64,128},{128,192},{192,8},{8,72},{72,136},{136,200},{200,0... | collective-permute-start | bytes 1376264 | tf_op jit(solution)/shard_map/ppermute | solution.py:232
  49.1 19.7 %collective-permute-start.14 = (f32[64,1792]{1,0:T(8,128)}, f32[64,1792]{1,0:T(8,128)}, u32[]{:S(2)}, u32[]{:S(2)}) collective-permute-start(f32[64,1792]{1,0:T(8,128)} %collective-permute-done.4.refs_3_), channel_id=1, source_target_pairs={{0,200},{64,0},{128,64},{192,128},{8,192},{72,8},{136,72},{200,136... | collective-permute-start | bytes 1376264 | tf_op jit(solution)/shard_map/ppermute | solution.py:231
  58.9 19.7 %collective-permute-start.15 = (f32[64,1792]{1,0:T(8,128)}, f32[64,1792]{1,0:T(8,128)}, u32[]{:S(2)}, u32[]{:S(2)}) collective-permute-start(f32[64,1792]{1,0:T(8,128)} %collective-permute-done.6.refs_5_), channel_id=1, source_target_pairs={{0,64},{64,128},{128,192},{192,8},{8,72},{72,136},{136,200},{200,0... | collective-permute-start | bytes 1376264 | tf_op jit(solution)/shard_map/ppermute | solution.py:232
  58.9 19.7 %collective-permute-start.8 = (f32[64,1792]{1,0:T(8,128)}, f32[64,1792]{1,0:T(8,128)S(1)}, u32[]{:S(2)}, u32[]{:S(2)}) collective-permute-start(f32[64,1792]{1,0:T(8,128)} %collective-permute-done.7.refs_0_), channel_id=1, source_target_pairs={{0,200},{64,0},{128,64},{192,128},{8,192},{72,8},{136,72},{200,136... | collective-permute-start | bytes 1376264 | tf_op jit(solution)/shard_map/ppermute | solution.py:231
  62.3 38.0 %collective-permute-start.2 = (f32[128,1792]{1,0:T(8,128)S(1)}, f32[128,1792]{1,0:T(8,128)S(1)}, u32[]{:S(2)}, u32[]{:S(2)}) collective-permute-start(f32[128,1792]{1,0:T(8,128)S(1)} %bitcast.17), channel_id=1, source_target_pairs={{0,1},{1,0},{2,3},{3,2},{4,5},{5,4},{6,7},{7,6},{8,9},{9,8},{10,11... | collective-permute-start | bytes 2752520 | tf_op jit(solution)/shard_map/ppermute | solution.py:241
  68.8 19.6 %collective-permute-start.10 = (f32[64,1792]{1,0:T(8,128)}, f32[64,1792]{1,0:T(8,128)S(1)}, u32[]{:S(2)}, u32[]{:S(2)}) collective-permute-start(f32[64,1792]{1,0:T(8,128)} %collective-permute-done.9.refs_2_), channel_id=1, source_target_pairs={{0,64},{64,128},{128,192},{192,8},{8,72},{72,136},{136,200},{200,0... | collective-permute-start | bytes 1376264 | tf_op jit(solution)/shard_map/ppermute | solution.py:232
  68.8 19.6 %collective-permute-start.23 = (f32[64,1792]{1,0:T(8,128)}, f32[64,1792]{1,0:T(8,128)S(1)}, u32[]{:S(2)}, u32[]{:S(2)}) collective-permute-start(f32[64,1792]{1,0:T(8,128)} %collective-permute-done.14.refs_1_), channel_id=1, source_target_pairs={{0,200},{64,0},{128,64},{192,128},{8,192},{72,8},{136,72},{200,136... | collective-permute-start | bytes 1376264 | tf_op jit(solution)/shard_map/ppermute | solution.py:231
  78.6 19.6 %collective-permute-start.24 = (f32[64,1792]{1,0:T(8,128)}, f32[64,1792]{1,0:T(8,128)S(1)}, u32[]{:S(2)}, u32[]{:S(2)}) collective-permute-start(f32[64,1792]{1,0:T(8,128)} %collective-permute-done.15.refs_3_), channel_id=1, source_target_pairs={{0,64},{64,128},{128,192},{192,8},{8,72},{72,136},{136,200},{200,0... | collective-permute-start | bytes 1376264 | tf_op jit(solution)/shard_map/ppermute | solution.py:232
  78.6 19.6 %collective-permute-start.1 = (f32[64,1792]{1,0:T(8,128)S(1)}, f32[64,1792]{1,0:T(8,128)S(1)}, u32[]{:S(2)}, u32[]{:S(2)}) collective-permute-start(f32[64,1792]{1,0:T(8,128)S(1)} %bitcast.22), channel_id=1, source_target_pairs={{0,1},{1,0},{2,3},{3,2},{4,5},{5,4},{6,7},{7,6},{8,9},{9,8},{10,11... | collective-permute-start | bytes 1376264 | tf_op jit(solution)/shard_map/ppermute | solution.py:219
  88.3 16.8 %collective-permute-start.31 = (f32[32,1792]{1,0:T(8,128)S(1)}, f32[32,1792]{1,0:T(8,128)S(1)}, u32[]{:S(2)}, u32[]{:S(2)}) collective-permute-start(f32[32,1792]{1,0:T(8,128)S(1)} %slice.16), channel_id=1, source_target_pairs={{0,200},{64,0},{128,64},{192,128},{8,192},{72,8},{136,72},{200,136... | collective-permute-start | bytes 688136 | tf_op jit(solution)/shard_map/ppermute | solution.py:231
  88.3 16.8 %collective-permute-start.32 = (f32[32,1792]{1,0:T(8,128)S(1)}, f32[32,1792]{1,0:T(8,128)S(1)}, u32[]{:S(2)}, u32[]{:S(2)}) collective-permute-start(f32[32,1792]{1,0:T(8,128)S(1)} %slice.17), channel_id=1, source_target_pairs={{0,64},{64,128},{128,192},{192,8},{8,72},{72,136},{136,200},{200,0... | collective-permute-start | bytes 688136 | tf_op jit(solution)/shard_map/ppermute | solution.py:232
  98.2 8.8 %collective-permute-start.34 = (f32[32,1792]{1,0:T(8,128)S(1)}, f32[32,1792]{1,0:T(8,128)S(1)}, u32[]{:S(2)}, u32[]{:S(2)}) collective-permute-start(f32[32,1792]{1,0:T(8,128)S(1)} %slice.19), channel_id=1, source_target_pairs={{0,64},{64,128},{128,192},{192,8},{8,72},{72,136},{136,200},{200,0... | collective-permute-start | bytes 688136 | tf_op jit(solution)/shard_map/ppermute | solution.py:232
  109.0 49.6 %all-to-all-start.2 = ((f32[16,64,128]{2,1,0:T(8,128)}), f32[16,64,128]{2,1,0:T(8,128)S(1)}, u32[]{:S(2)}, u32[]{:S(2)}) async-start(f32[16,64,128]{2,1,0:T(8,128)} %bitcast.11), calls=%async_computation.2 | async-start | bytes 1048576 | tf_op jit(solution)/shard_map/all_to_all | solution.py:249
  120.9 10.2 %collective-permute-start.16 = (f32[256,128]{1,0:T(8,128)S(1)}, f32[256,128]{1,0:T(8,128)S(1)}, u32[]{:S(2)}, u32[]{:S(2)}) collective-permute-start(f32[256,128]{1,0:T(8,128)S(1)} %get-tuple-element.45), channel_id=1, source_target_pairs={{0,16},{16,32},{32,48},{48,0},{1,17},{17,33},{33,49},{49,1},{2,18}... | collective-permute-start | bytes 393224 | tf_op jit(solution)/shard_map/ppermute | solution.py:108
  126.1 18.8 %collective-permute-start.11 = (f32[384,128]{1,0:T(8,128)S(1)}, f32[384,128]{1,0:T(8,128)S(1)}, u32[]{:S(2)}, u32[]{:S(2)}) collective-permute-start(f32[384,128]{1,0:T(8,128)S(1)} %get-tuple-element.41), channel_id=1, source_target_pairs={{0,16},{16,32},{32,48},{48,0},{1,17},{17,33},{33,49},{49,1},{2,18}... | collective-permute-start | bytes 589832 | tf_op jit(solution)/shard_map/ppermute | solution.py:108
  127.4 18.9 %collective-permute-start.12 = (f32[384,128]{1,0:T(8,128)S(1)}, f32[384,128]{1,0:T(8,128)S(1)}, u32[]{:S(2)}, u32[]{:S(2)}) collective-permute-start(f32[384,128]{1,0:T(8,128)S(1)} %get-tuple-element.42), channel_id=1, source_target_pairs={{0,32},{16,48},{32,0},{48,16},{1,33},{17,49},{33,1},{49,17},{2,34}... | collective-permute-start | bytes 589832 | tf_op jit(solution)/shard_map/ppermute | solution.py:108
  128.8 17.5 %collective-permute-start.13 = (f32[384,128]{1,0:T(8,128)S(1)}, f32[384,128]{1,0:T(8,128)S(1)}, u32[]{:S(2)}, u32[]{:S(2)}) collective-permute-start(f32[384,128]{1,0:T(8,128)S(1)} %get-tuple-element.43), channel_id=1, source_target_pairs={{0,48},{16,0},{32,16},{48,32},{1,49},{17,1},{33,17},{49,33},{2,50}... | collective-permute-start | bytes 589832 | tf_op jit(solution)/shard_map/ppermute | solution.py:108
  129.5 12.7 %collective-permute-start.17 = (f32[256,128]{1,0:T(8,128)S(1)}, f32[256,128]{1,0:T(8,128)S(1)}, u32[]{:S(2)}, u32[]{:S(2)}) collective-permute-start(f32[256,128]{1,0:T(8,128)S(1)} %get-tuple-element.46), channel_id=1, source_target_pairs={{0,32},{16,48},{32,0},{48,16},{1,33},{17,49},{33,1},{49,17},{2,34}... | collective-permute-start | bytes 393224 | tf_op jit(solution)/shard_map/ppermute | solution.py:108
  131.1 12.0 %collective-permute-start.18 = (f32[256,128]{1,0:T(8,128)S(1)}, f32[256,128]{1,0:T(8,128)S(1)}, u32[]{:S(2)}, u32[]{:S(2)}) collective-permute-start(f32[256,128]{1,0:T(8,128)S(1)} %get-tuple-element.47), channel_id=1, source_target_pairs={{0,48},{16,0},{32,16},{48,32},{1,49},{17,1},{33,17},{49,33},{2,50}... | collective-permute-start | bytes 393224 | tf_op jit(solution)/shard_map/ppermute | solution.py:108
  142.2 8.3 %collective-permute-start.25 = (f32[128,128]{1,0:T(8,128)S(1)}, f32[128,128]{1,0:T(8,128)S(1)}, u32[]{:S(2)}, u32[]{:S(2)}) collective-permute-start(f32[128,128]{1,0:T(8,128)S(1)} %get-tuple-element.55), channel_id=1, source_target_pairs={{0,16},{16,32},{32,48},{48,0},{1,17},{17,33},{33,49},{49,1},{2,18}... | collective-permute-start | bytes 196616 | tf_op jit(solution)/shard_map/ppermute | solution.py:108
  143.1 8.9 %collective-permute-start.26 = (f32[128,128]{1,0:T(8,128)S(1)}, f32[128,128]{1,0:T(8,128)S(1)}, u32[]{:S(2)}, u32[]{:S(2)}) collective-permute-start(f32[128,128]{1,0:T(8,128)S(1)} %get-tuple-element.56), channel_id=1, source_target_pairs={{0,32},{16,48},{32,0},{48,16},{1,33},{17,49},{33,1},{49,17},{2,34}... | collective-permute-start | bytes 196616 | tf_op jit(solution)/shard_map/ppermute | solution.py:108
  147.9 7.6 %collective-permute-start.20 = (f32[128,128]{1,0:T(8,128)S(1)}, f32[128,128]{1,0:T(8,128)S(1)}, u32[]{:S(2)}, u32[]{:S(2)}) collective-permute-start(f32[128,128]{1,0:T(8,128)S(1)} %get-tuple-element.50), channel_id=1, source_target_pairs={{0,4},{2,6},{4,0},{6,2},{1,5},{3,7},{5,1},{7,3},{8,12},{10,14},{12... | collective-permute-start | bytes 196616 | tf_op jit(solution)/shard_map/ppermute | solution.py:137
  155.5 8.0 %collective-permute-start.22 = (f32[64,128]{1,0:T(8,128)S(1)}, f32[64,128]{1,0:T(8,128)S(1)}, u32[]{:S(2)}, u32[]{:S(2)}) collective-permute-start(f32[64,128]{1,0:T(8,128)S(1)} %get-tuple-element.53), channel_id=1, source_target_pairs={{0,8},{8,0},{1,9},{9,1},{2,10},{10,2},{3,11},{11,3},{4,12},{12,4},... | collective-permute-start | bytes 98312 | tf_op jit(solution)/shard_map/ppermute | solution.py:181
  158.6 7.9 %collective-permute-start.35 = (f32[64,128]{1,0:T(8,128)S(1)}, f32[64,128]{1,0:T(8,128)S(1)}, u32[]{:S(2)}, u32[]{:S(2)}) collective-permute-start(f32[64,128]{1,0:T(8,128)S(1)} %get-tuple-element.67), channel_id=1, source_target_pairs={{0,8},{8,0},{1,9},{9,1},{2,10},{10,2},{3,11},{11,3},{4,12},{12,4},... | collective-permute-start | bytes 98312 | tf_op jit(solution)/shard_map/ppermute | solution.py:181
  (19 other events, 190.8 us)

commit v5 on v2

--- a/solution.py
+++ b/solution.py
@@ -56,27 +56,32 @@
     lax.fori_loop(0, 16, step, 0)
 
 
-def product_kernel(n, hi, lo, *refs):
-    blocks, outs = refs[: 2 * n], refs[2 * n :]
+def product(blocks, hi, lo):
     v = jnp.concatenate([b[...] for b in blocks], 0)
     top = v.astype(BF16)
     low = (v - top.astype(F32)).astype(BF16)
     both = jnp.concatenate([top, low], 0)
-    rows = n * 128
+    rows, parts = v.shape[0], []
     for half in range(2):
         cols = slice(half * 256, (half + 1) * 256)
         p = lax.dot_general(both, hi[cols, :], NT, preferred_element_type=F32)
         r = lax.dot_general(top, lo[cols, :], NT, preferred_element_type=F32)
         total = (p[:rows] + p[rows:]) + r
-        outs[2 * half][...] = total[:, :128]
-        outs[2 * half + 1][...] = total[:, 128:]
-
-
-def products(hi, lo, pairs):
-    n = len(pairs)
-    flat = [b for pair in pairs for b in pair]
-    shapes = [((n * 128, 128), F32)] * 4
-    return call(lambda *r: product_kernel(n, *r), shapes, hi, lo, *flat)
+        parts += [total[:, :128], total[:, 128:]]
+    return parts
+
+
+def products(hi, lo, blocks, groups=1):
+    rows = sum(b.shape[0] for b in blocks) // groups
+
+    def kernel(hi, lo, *refs):
+        n = len(blocks)
+        for q, part in enumerate(product(refs[:n], hi, lo)):
+            for g in range(groups):
+                refs[n + 4 * g + q][...] = part[g * rows : (g + 1) * rows]
+
+    outs = call(kernel, [((rows, 128), F32)] * (4 * groups), hi, lo, *blocks)
+    return [outs[4 * g : 4 * g + 4] for g in range(groups)]
 
 
 def to_y(parts):
@@ -152,29 +157,39 @@
     orb = lax.all_to_all(orbitals, ("y", "x"), split_axis=1, concat_axis=0, tiled=True)
     by_parity = orb.reshape(2, 2, 32, K)
     mine = lax.dynamic_index_in_dim(by_parity, core, 1, False).reshape(64, K)
-    theirs = lax.dynamic_index_in_dim(by_parity, 1 - core, 1, False).reshape(64, K)
+    rest = after(by_parity, mine)
+    theirs = lax.dynamic_index_in_dim(rest, 1 - core, 1, False).reshape(64, K)
     same = lax.ppermute(theirs, "core", swap)
     cross = lax.ppermute(mine, "core", swap)
     app = lax.all_to_all(after(applied, mine), ("y", "x"), split_axis=1, concat_axis=0, tiled=True)
 
     held = {(0, 0): mine, (0, 1): same}
 
+    last, cuts = [], []
+
     def forward(d, h):
-        if d < 4 or h == 0:
-            held[(d, h)] = lax.ppermute(held[(d - 1, h)], Z, z_ring(-1))
-        if d < 4 or h == 1:
-            held[(-d % 8, h)] = lax.ppermute(held[((1 - d) % 8, h)], Z, z_ring(1))
+        ahead, behind = held[(d - 1, h)], held[((1 - d) % 8, h)]
+        if d == 4:
+            ahead, behind = ahead[:32], behind[32:]
+            cuts.extend((ahead, behind))
+        ahead = lax.ppermute(ahead, Z, z_ring(-1))
+        behind = lax.ppermute(behind, Z, z_ring(1))
+        if d == 4:
+            last.extend((ahead, behind))
+        else:
+            held[(d, h)], held[(-d % 8, h)] = ahead, behind
 
     for d in range(1, 5):
         for h in range(2):
             forward(d, h)
     app_other = lax.ppermute(app, "core", swap)
     hi, lo = call(own_kernel, [((512, K), BF16)] * 2, orb, same, cross, app, app_other)
-    pair = lambda d: (held[(d % 8, 0)], held[(d % 8, 1)])
-    y1 = to_y(products(hi, lo, [pair(0), pair(1), pair(-1)]))
-    y2 = to_y(products(hi, lo, [pair(2), pair(-2)]))
-    y3 = to_y(products(hi, lo, [pair(3), pair(-3)]))
-    y4 = to_y(products(hi, lo, [pair(4)]))
+    blocks = lambda *ds: [held[(d % 8, h)] for d in ds for h in range(2)]
+    y1 = to_y(products(hi, lo, blocks(0, 1, -1))[0])
+    y2 = to_y(products(hi, lo, blocks(2, -2))[0])
+    y3 = to_y(products(hi, lo, blocks(3, -3))[0])
+    y4 = to_y(products(hi, lo, last)[0])
+    y1[0] = after(y1[0], *cuts[:2])
     keep_a, recv_a = to_x([y1, y2], [(0, 0), (0, 1), (1, 1), (0, 2)])
     keep_b, recv_b = to_x([y2, y3, y4], [(2, 0), (1, 1), (0, 0), (1, 0)])
     return call(tile_kernel, [((128, 128), F32)] * 2, keep_a, recv_a, keep_b, recv_b)

time: 149 us -> 148 us (level)
  local copies, waits for them, and re-layouts: 2.62 us -> 0.9 us
    ppermute x14 -> x16, waiting for transfers between devices: 35.9 us -> 38.3 us  [the longest x8 19.4 us: forward(): behind = lax.ppermute(behind, Z, z_ring(1))]
    ppermute x12, waiting for transfers between devices: 5.07 us -> 2.94 us  [to_y(): sent = [lax.ppermute(parts[q], 'y', ring(4, q)) for q in range(1, 4)]]
    ppermute x2, starting transfers between devices: 6.9 us -> 5.07 us  [to_x(): return (keep, lax.ppermute(send, 'zhi', ring(2, 1)))]
    ppermute x14 -> x16, starting transfers between devices: 26.7 us -> 27 us  [the longest x8 22.1 us: forward(): ahead = lax.ppermute(ahead, Z, z_ring(-1))]
  transfers between devices with their start and end apart: 39 -> 41, of which waited for: 14 -> 16; matrix products, arithmetic and copies ran while one was open for 0% -> 0% of each run, Pallas kernels for 7% -> 7%
where the time goes in v5:
time: 148 us; the launch traced here: 147 us
  starting transfers between devices  73.8 us (50%)
  waiting for transfers between devices  60.2 us (41%)
  Pallas kernels  11.1 us (8%)
    ppermute x8, starting transfers between devices, forward(): ahead = lax.ppermute(ahead, Z, z_ring(-1))  22.1 us
    ppermute x8, waiting for transfers between devices, forward(): behind = lax.ppermute(behind, Z, z_ring(1))  19.4 us
    ppermute x8, waiting for transfers between devices, forward(): ahead = lax.ppermute(ahead, Z, z_ring(-1))  18.8 us
    ppermute x12, starting transfers between devices, to_y(): sent = [lax.ppermute(parts[q], 'y', ring(4, q)) for q in range(1, 4)]  17.5 us
    all_to_all x1, waiting for transfers between devices, body(): lax.all_to_all(orbitals, ('y', 'x'), split_axis=1, concat_axis=0, tiled=T...  13.2 us
    pallas_call x10, Pallas kernels, call(): pl.pallas_call(kernel, out_shape=out, in_specs=[VMEM] * len(args), out_sp...  11.1 us
    ppermute x6, starting transfers between devices, to_x(): lax.ppermute(outs[q], 'x', ring(4, q))  10.2 us
    all_to_all x1, starting transfers between devices, body(): lax.all_to_all(orbitals, ('y', 'x'), split_axis=1, concat_axis=0, tiled=T...  7.41 us
  transfers between devices with their start and end apart: 41, of which 16 were waited for; matrix products, arithmetic and copies ran while one was open for 0% of the time, Pallas kernels for 7%

profile of v5, /device:TPU:8, one launch (start us, length us, event | category | flops | bytes accessed | tf_op | source)
XLA Modules:
  0.0 146.8 jit_solution(8738031557260078244)
XLA Ops:
  0.6 7.4 %all-to-all-start = ((f32[8,16,1792]{2,0,1:T(8,128)}), f32[8,16,1792]{2,0,1:T(8,128)S(1)}, u32[]{:S(2)}, u32[]{:S(2)}) async-start(f32[8,16,1792]{2,0,1:T(8,128)} %bitcast.21), calls=%async_computation | async-start | bytes 1835008 | tf_op jit(solution)/shard_map/all_to_all | solution.py:157
  8.0 13.2 %all-to-all-done = f32[8,16,1792]{2,0,1:T(8,128)S(1)} async-done(((f32[8,16,1792]{2,0,1:T(8,128)}), f32[8,16,1792]{2,0,1:T(8,128)S(1)}, u32[]{:S(2)}, u32[]{:S(2)}) %all-to-all-start) | async-done | bytes 917536 | tf_op jit(solution)/shard_map/all_to_all | solution.py:157
  21.2 5.9 %collective-permute-start.3 = (f32[64,1792]{1,0:T(8,128)S(1)}, f32[64,1792]{1,0:T(8,128)S(1)}, u32[]{:S(2)}, u32[]{:S(2)}) collective-permute-start(f32[64,1792]{1,0:T(8,128)S(1)} %bitcast.17), channel_id=1, source_target_pairs={{0,200},{64,0},{128,64},{192,128},{8,192},{72,8},{136,72},{200,136... | collective-permute-start | bytes 1376264 | tf_op jit(solution)/shard_map/ppermute | solution.py:175
  27.2 6.5 %all-to-all-start.1 = ((f32[8,16,1792]{2,0,1:T(8,128)}), f32[8,16,1792]{2,0,1:T(8,128)S(1)}, u32[]{:S(2)}, u32[]{:S(2)}) async-start(f32[8,16,1792]{2,0,1:T(8,128)} %bitcast.22), calls=%async_computation.1 | async-start | bytes 1835008 | tf_op jit(solution)/shard_map/all_to_all | solution.py:164
  33.9 2.0 %collective-permute-done.3.refs_2_ = f32[64,1792]{1,0:T(8,128)S(1)} collective-permute-done((f32[64,1792]{1,0:T(8,128)S(1)}, f32[64,1792]{1,0:T(8,128)S(1)}, u32[]{:S(2)}, u32[]{:S(2)}) %collective-permute-start.3) | collective-permute-done | bytes 458784 | tf_op jit(solution)/shard_map/ppermute | solution.py:175
  35.9 3.7 %collective-permute-start.7 = (f32[64,1792]{1,0:T(8,128)S(1)}, f32[64,1792]{1,0:T(8,128)}, u32[]{:S(2)}, u32[]{:S(2)}) collective-permute-start(f32[64,1792]{1,0:T(8,128)S(1)} %collective-permute-done.3.refs_2_), channel_id=1, source_target_pairs={{0,200},{64,0},{128,64},{192,128},{8,192},{72,8},{136,72},{200,136... | collective-permute-start | bytes 1376264 | tf_op jit(solution)/shard_map/ppermute | solution.py:175
  40.4 2.0 %collective-permute-start.6 = (f32[64,1792]{1,0:T(8,128)S(1)}, f32[64,1792]{1,0:T(8,128)}, u32[]{:S(2)}, u32[]{:S(2)}) collective-permute-start(f32[64,1792]{1,0:T(8,128)S(1)} %collective-permute-done.same.refs_1_), channel_id=1, source_target_pairs={{0,64},{64,128},{128,192},{192,8},{8,72},{72,136},{136,200},{200,0... | collective-permute-start | bytes 1376264 | tf_op jit(solution)/shard_map/ppermute | solution.py:176
  42.4 6.2 %collective-permute-done.5.refs_4_ = f32[64,1792]{1,0:T(8,128)} collective-permute-done((f32[64,1792]{1,0:T(8,128)S(1)}, f32[64,1792]{1,0:T(8,128)}, u32[]{:S(2)}, u32[]{:S(2)}) %collective-permute-start.5) | collective-permute-done | bytes 458784 | tf_op jit(solution)/shard_map/ppermute | solution.py:176
  48.6 1.9 %collective-permute-done.7.refs_0_ = f32[64,1792]{1,0:T(8,128)} collective-permute-done((f32[64,1792]{1,0:T(8,128)S(1)}, f32[64,1792]{1,0:T(8,128)}, u32[]{:S(2)}, u32[]{:S(2)}) %collective-permute-start.7) | collective-permute-done | bytes 458784 | tf_op jit(solution)/shard_map/ppermute | solution.py:175
  50.5 3.8 %collective-permute-start.8 = (f32[64,1792]{1,0:T(8,128)}, f32[64,1792]{1,0:T(8,128)S(1)}, u32[]{:S(2)}, u32[]{:S(2)}) collective-permute-start(f32[64,1792]{1,0:T(8,128)} %collective-permute-done.7.refs_0_), channel_id=1, source_target_pairs={{0,200},{64,0},{128,64},{192,128},{8,192},{72,8},{136,72},{200,136... | collective-permute-start | bytes 1376264 | tf_op jit(solution)/shard_map/ppermute | solution.py:175
  54.3 6.0 %collective-permute-done.4.refs_3_ = f32[64,1792]{1,0:T(8,128)} collective-permute-done((f32[64,1792]{1,0:T(8,128)S(1)}, f32[64,1792]{1,0:T(8,128)}, u32[]{:S(2)}, u32[]{:S(2)}) %collective-permute-start.4) | collective-permute-done | bytes 458784 | tf_op jit(solution)/shard_map/ppermute | solution.py:175
  60.3 3.8 %collective-permute-start.14 = (f32[64,1792]{1,0:T(8,128)}, f32[64,1792]{1,0:T(8,128)S(1)}, u32[]{:S(2)}, u32[]{:S(2)}) collective-permute-start(f32[64,1792]{1,0:T(8,128)} %collective-permute-done.4.refs_3_), channel_id=1, source_target_pairs={{0,200},{64,0},{128,64},{192,128},{8,192},{72,8},{136,72},{200,136... | collective-permute-start | bytes 1376264 | tf_op jit(solution)/shard_map/ppermute | solution.py:175
  64.1 4.1 %collective-permute-done.9.refs_2_ = f32[64,1792]{1,0:T(8,128)} collective-permute-done((f32[64,1792]{1,0:T(8,128)}, f32[64,1792]{1,0:T(8,128)}, u32[]{:S(2)}, u32[]{:S(2)}) %collective-permute-start.9) | collective-permute-done | bytes 458784 | tf_op jit(solution)/shard_map/ppermute | solution.py:176
  68.2 2.0 %collective-permute-done.8.refs_0_ = f32[64,1792]{1,0:T(8,128)S(1)} collective-permute-done((f32[64,1792]{1,0:T(8,128)}, f32[64,1792]{1,0:T(8,128)S(1)}, u32[]{:S(2)}, u32[]{:S(2)}) %collective-permute-start.8) | collective-permute-done | bytes 458784 | tf_op jit(solution)/shard_map/ppermute | solution.py:175
  70.3 6.8 %collective-permute-done.14.refs_1_ = f32[64,1792]{1,0:T(8,128)S(1)} collective-permute-done((f32[64,1792]{1,0:T(8,128)}, f32[64,1792]{1,0:T(8,128)S(1)}, u32[]{:S(2)}, u32[]{:S(2)}) %collective-permute-start.14) | collective-permute-done | bytes 458784 | tf_op jit(solution)/shard_map/ppermute | solution.py:175
  77.0 3.6 %collective-permute-start.23 = (f32[64,1792]{1,0:T(8,128)S(1)}, f32[64,1792]{1,0:T(8,128)S(1)}, u32[]{:S(2)}, u32[]{:S(2)}) collective-permute-start(f32[64,1792]{1,0:T(8,128)S(1)} %collective-permute-done.14.refs_1_), channel_id=1, source_target_pairs={{0,200},{64,0},{128,64},{192,128},{8,192},{72,8},{136,72},{200,136... | collective-permute-start | bytes 1376264 | tf_op jit(solution)/shard_map/ppermute | solution.py:175
  80.7 8.1 %collective-permute-done.10.refs_2_ = f32[64,1792]{1,0:T(8,128)S(1)} collective-permute-done((f32[64,1792]{1,0:T(8,128)}, f32[64,1792]{1,0:T(8,128)S(1)}, u32[]{:S(2)}, u32[]{:S(2)}) %collective-permute-start.10) | collective-permute-done | bytes 458784 | tf_op jit(solution)/shard_map/ppermute | solution.py:176
  88.8 2.1 %collective-permute-start.29 = (f32[32,1792]{1,0:T(8,128)S(1)}, f32[32,1792]{1,0:T(8,128)S(1)}, u32[]{:S(2)}, u32[]{:S(2)}) collective-permute-start(f32[32,1792]{1,0:T(8,128)S(1)} %slice.17), channel_id=1, source_target_pairs={{0,64},{64,128},{128,192},{192,8},{8,72},{72,136},{136,200},{200,0... | collective-permute-start | bytes 688136 | tf_op jit(solution)/shard_map/ppermute | solution.py:176
  91.9 2.8 %shard_map.43 = (f32[256,128]{1,0:T(8,128)S(1)}, f32[256,128]{1,0:T(8,128)S(1)}, f32[256,128]{1,0:T(8,128)S(1)}, f32[256,128]{1,0:T(8,128)S(1)}) custom-call(bf16[512,1792]{1,0:T(8,128)(2,1)S(1)} %get-tuple-element.37.hi, bf16[512,1792]{1,0:T(8,128)(2,1)S(1)} %get-tuple-element.38.lo, f32[64,1792]{1,0:T(8,128)} %collective-permute-done.7.refs_0_, ...), custom_call_target="tpu_custom_call" | custom-call | tf_op jit(solution)/shard_map/pallas_call | solution.py:28
  98.6 2.1 %collective-permute-start.17 = (f32[256,128]{1,0:T(8,128)S(1)}, f32[256,128]{1,0:T(8,128)S(1)}, u32[]{:S(2)}, u32[]{:S(2)}) collective-permute-start(f32[256,128]{1,0:T(8,128)S(1)} %get-tuple-element.46), channel_id=1, source_target_pairs={{0,32},{16,48},{32,0},{48,16},{1,33},{17,49},{33,1},{49,17},{2,34}... | collective-permute-start | bytes 393224 | tf_op jit(solution)/shard_map/ppermute | solution.py:88
  105.1 3.6 %shard_map.42 = (f32[384,128]{1,0:T(8,128)S(1)}, f32[384,128]{1,0:T(8,128)S(1)}, f32[384,128]{1,0:T(8,128)S(1)}, f32[384,128]{1,0:T(8,128)S(1)}) custom-call(bf16[512,1792]{1,0:T(8,128)(2,1)S(1)} %get-tuple-element.37.hi, bf16[512,1792]{1,0:T(8,128)(2,1)S(1)} %get-tuple-element.38.lo, f32[64,1792]{1,0:T(8,128)S(1)} %bitcast.20, ...), custom_call_target="tpu_custom_call" | custom-call | tf_op jit(solution)/shard_map/pallas_call | solution.py:28
  108.9 2.9 %collective-permute-start.12 = (f32[384,128]{1,0:T(8,128)S(1)}, f32[384,128]{1,0:T(8,128)S(1)}, u32[]{:S(2)}, u32[]{:S(2)}) collective-permute-start(f32[384,128]{1,0:T(8,128)S(1)} %get-tuple-element.42), channel_id=1, source_target_pairs={{0,32},{16,48},{32,0},{48,16},{1,33},{17,49},{33,1},{49,17},{2,34}... | collective-permute-start | bytes 589832 | tf_op jit(solution)/shard_map/ppermute | solution.py:88
  111.8 1.8 %collective-permute-start.13 = (f32[384,128]{1,0:T(8,128)S(1)}, f32[384,128]{1,0:T(8,128)S(1)}, u32[]{:S(2)}, u32[]{:S(2)}) collective-permute-start(f32[384,128]{1,0:T(8,128)S(1)} %get-tuple-element.43), channel_id=1, source_target_pairs={{0,48},{16,0},{32,16},{48,32},{1,49},{17,1},{33,17},{49,33},{2,50}... | collective-permute-start | bytes 589832 | tf_op jit(solution)/shard_map/ppermute | solution.py:88
  113.8 2.1 %collective-permute-start.27 = (f32[256,128]{1,0:T(8,128)S(1)}, f32[256,128]{1,0:T(8,128)S(1)}, u32[]{:S(2)}, u32[]{:S(2)}) collective-permute-start(f32[256,128]{1,0:T(8,128)S(1)} %get-tuple-element.57), channel_id=1, source_target_pairs={{0,48},{16,0},{32,16},{48,32},{1,49},{17,1},{33,17},{49,33},{2,50}... | collective-permute-start | bytes 393224 | tf_op jit(solution)/shard_map/ppermute | solution.py:88
  118.8 2.6 %collective-permute-start.32 = (f32[128,128]{1,0:T(8,128)S(1)}, f32[128,128]{1,0:T(8,128)S(1)}, u32[]{:S(2)}, u32[]{:S(2)}) collective-permute-start(f32[128,128]{1,0:T(8,128)S(1)} %get-tuple-element.59), channel_id=1, source_target_pairs={{0,16},{16,32},{32,48},{48,0},{1,17},{17,33},{33,49},{49,1},{2,18}... | collective-permute-start | bytes 196616 | tf_op jit(solution)/shard_map/ppermute | solution.py:88
  124.8 2.1 %collective-permute-start.19 = (f32[128,128]{1,0:T(8,128)S(1)}, f32[128,128]{1,0:T(8,128)S(1)}, u32[]{:S(2)}, u32[]{:S(2)}) collective-permute-start(f32[128,128]{1,0:T(8,128)S(1)} %get-tuple-element.49), channel_id=1, source_target_pairs={{0,2},{2,4},{4,6},{6,0},{1,3},{3,5},{5,7},{7,1},{8,10},{10,12},{12... | collective-permute-start | bytes 196616 | tf_op jit(solution)/shard_map/ppermute | solution.py:117
  126.9 2.4 %collective-permute-start.20 = (f32[128,128]{1,0:T(8,128)S(1)}, f32[128,128]{1,0:T(8,128)S(1)}, u32[]{:S(2)}, u32[]{:S(2)}) collective-permute-start(f32[128,128]{1,0:T(8,128)S(1)} %get-tuple-element.50), channel_id=1, source_target_pairs={{0,4},{2,6},{4,0},{6,2},{1,5},{3,7},{5,1},{7,3},{8,12},{10,14},{12... | collective-permute-start | bytes 196616 | tf_op jit(solution)/shard_map/ppermute | solution.py:117
  132.7 2.4 %collective-permute-start.37 = (f32[128,128]{1,0:T(8,128)S(1)}, f32[128,128]{1,0:T(8,128)S(1)}, u32[]{:S(2)}, u32[]{:S(2)}) collective-permute-start(f32[128,128]{1,0:T(8,128)S(1)} %get-tuple-element.65), channel_id=1, source_target_pairs={{0,6},{2,0},{4,2},{6,4},{1,7},{3,1},{5,3},{7,5},{8,14},{10,8},{12,... | collective-permute-start | bytes 196616 | tf_op jit(solution)/shard_map/ppermute | solution.py:117
  135.1 2.0 %collective-permute-start.22 = (f32[64,128]{1,0:T(8,128)S(1)}, f32[64,128]{1,0:T(8,128)S(1)}, u32[]{:S(2)}, u32[]{:S(2)}) collective-permute-start(f32[64,128]{1,0:T(8,128)S(1)} %get-tuple-element.53), channel_id=1, source_target_pairs={{0,8},{8,0},{1,9},{9,1},{2,10},{10,2},{3,11},{11,3},{4,12},{12,4},... | collective-permute-start | bytes 98312 | tf_op jit(solution)/shard_map/ppermute | solution.py:125
  138.1 3.1 %collective-permute-start.38 = (f32[64,128]{1,0:T(8,128)S(1)}, f32[64,128]{1,0:T(8,128)S(1)}, u32[]{:S(2)}, u32[]{:S(2)}) collective-permute-start(f32[64,128]{1,0:T(8,128)S(1)} %get-tuple-element.67), channel_id=1, source_target_pairs={{0,8},{8,0},{1,9},{9,1},{2,10},{10,2},{3,11},{11,3},{4,12},{12,4},... | collective-permute-start | bytes 98312 | tf_op jit(solution)/shard_map/ppermute | solution.py:125
  141.3 1.8 %collective-permute-done.22.recv_a = f32[64,128]{1,0:T(8,128)S(1)} collective-permute-done((f32[64,128]{1,0:T(8,128)S(1)}, f32[64,128]{1,0:T(8,128)S(1)}, u32[]{:S(2)}, u32[]{:S(2)}) %collective-permute-start.22) | collective-permute-done | bytes 32800 | tf_op jit(solution)/shard_map/ppermute | solution.py:125
  143.0 3.0 %collective-permute-done.38.recv_b = f32[64,128]{1,0:T(8,128)S(1)} collective-permute-done((f32[64,128]{1,0:T(8,128)S(1)}, f32[64,128]{1,0:T(8,128)S(1)}, u32[]{:S(2)}, u32[]{:S(2)}) %collective-permute-start.38) | collective-permute-done | bytes 32800 | tf_op jit(solution)/shard_map/ppermute | solution.py:125
  (70 shorter events, 22.2 us)
Async XLA Ops:
  0.6 20.6 %all-to-all-start = ((f32[8,16,1792]{2,0,1:T(8,128)}), f32[8,16,1792]{2,0,1:T(8,128)S(1)}, u32[]{:S(2)}, u32[]{:S(2)}) async-start(f32[8,16,1792]{2,0,1:T(8,128)} %bitcast.21), calls=%async_computation | async-start | bytes 1835008 | tf_op jit(solution)/shard_map/all_to_all | solution.py:157
  21.2 14.7 %collective-permute-start.3 = (f32[64,1792]{1,0:T(8,128)S(1)}, f32[64,1792]{1,0:T(8,128)S(1)}, u32[]{:S(2)}, u32[]{:S(2)}) collective-permute-start(f32[64,1792]{1,0:T(8,128)S(1)} %bitcast.17), channel_id=1, source_target_pairs={{0,200},{64,0},{128,64},{192,128},{8,192},{72,8},{136,72},{200,136... | collective-permute-start | bytes 1376264 | tf_op jit(solution)/shard_map/ppermute | solution.py:175
  27.2 27.1 %all-to-all-start.1 = ((f32[8,16,1792]{2,0,1:T(8,128)}), f32[8,16,1792]{2,0,1:T(8,128)S(1)}, u32[]{:S(2)}, u32[]{:S(2)}) async-start(f32[8,16,1792]{2,0,1:T(8,128)} %bitcast.22), calls=%async_computation.1 | async-start | bytes 1835008 | tf_op jit(solution)/shard_map/all_to_all | solution.py:164
  33.8 14.8 %collective-permute-start.5 = (f32[64,1792]{1,0:T(8,128)S(1)}, f32[64,1792]{1,0:T(8,128)}, u32[]{:S(2)}, u32[]{:S(2)}) collective-permute-start(f32[64,1792]{1,0:T(8,128)S(1)} %bitcast.18), channel_id=1, source_target_pairs={{0,64},{64,128},{128,192},{192,8},{8,72},{72,136},{136,200},{200,0... | collective-permute-start | bytes 1376264 | tf_op jit(solution)/shard_map/ppermute | solution.py:176
  35.9 14.6 %collective-permute-start.7 = (f32[64,1792]{1,0:T(8,128)S(1)}, f32[64,1792]{1,0:T(8,128)}, u32[]{:S(2)}, u32[]{:S(2)}) collective-permute-start(f32[64,1792]{1,0:T(8,128)S(1)} %collective-permute-done.3.refs_2_), channel_id=1, source_target_pairs={{0,200},{64,0},{128,64},{192,128},{8,192},{72,8},{136,72},{200,136... | collective-permute-start | bytes 1376264 | tf_op jit(solution)/shard_map/ppermute | solution.py:175
  40.4 20.0 %collective-permute-start.4 = (f32[64,1792]{1,0:T(8,128)S(1)}, f32[64,1792]{1,0:T(8,128)}, u32[]{:S(2)}, u32[]{:S(2)}) collective-permute-start(f32[64,1792]{1,0:T(8,128)S(1)} %collective-permute-done.same.refs_1_), channel_id=1, source_target_pairs={{0,200},{64,0},{128,64},{192,128},{8,192},{72,8},{136,72},{200,136... | collective-permute-start | bytes 1376264 | tf_op jit(solution)/shard_map/ppermute | solution.py:175
  40.4 23.8 %collective-permute-start.6 = (f32[64,1792]{1,0:T(8,128)S(1)}, f32[64,1792]{1,0:T(8,128)}, u32[]{:S(2)}, u32[]{:S(2)}) collective-permute-start(f32[64,1792]{1,0:T(8,128)S(1)} %collective-permute-done.same.refs_1_), channel_id=1, source_target_pairs={{0,64},{64,128},{128,192},{192,8},{8,72},{72,136},{136,200},{200,0... | collective-permute-start | bytes 1376264 | tf_op jit(solution)/shard_map/ppermute | solution.py:176
  48.6 19.7 %collective-permute-start.9 = (f32[64,1792]{1,0:T(8,128)}, f32[64,1792]{1,0:T(8,128)}, u32[]{:S(2)}, u32[]{:S(2)}) collective-permute-start(f32[64,1792]{1,0:T(8,128)} %collective-permute-done.5.refs_4_), channel_id=1, source_target_pairs={{0,64},{64,128},{128,192},{192,8},{8,72},{72,136},{136,200},{200,0... | collective-permute-start | bytes 1376264 | tf_op jit(solution)/shard_map/ppermute | solution.py:176
  50.5 19.8 %collective-permute-start.8 = (f32[64,1792]{1,0:T(8,128)}, f32[64,1792]{1,0:T(8,128)S(1)}, u32[]{:S(2)}, u32[]{:S(2)}) collective-permute-start(f32[64,1792]{1,0:T(8,128)} %collective-permute-done.7.refs_0_), channel_id=1, source_target_pairs={{0,200},{64,0},{128,64},{192,128},{8,192},{72,8},{136,72},{200,136... | collective-permute-start | bytes 1376264 | tf_op jit(solution)/shard_map/ppermute | solution.py:175
  54.3 36.6 %collective-permute-start.2 = (f32[128,1792]{1,0:T(8,128)S(1)}, f32[128,1792]{1,0:T(8,128)S(1)}, u32[]{:S(2)}, u32[]{:S(2)}) collective-permute-start(f32[128,1792]{1,0:T(8,128)S(1)} %bitcast.15), channel_id=1, source_target_pairs={{0,1},{1,0},{2,3},{3,2},{4,5},{5,4},{6,7},{7,6},{8,9},{9,8},{10,11... | collective-permute-start | bytes 2752520 | tf_op jit(solution)/shard_map/ppermute | solution.py:185
  60.3 16.7 %collective-permute-start.14 = (f32[64,1792]{1,0:T(8,128)}, f32[64,1792]{1,0:T(8,128)S(1)}, u32[]{:S(2)}, u32[]{:S(2)}) collective-permute-start(f32[64,1792]{1,0:T(8,128)} %collective-permute-done.4.refs_3_), channel_id=1, source_target_pairs={{0,200},{64,0},{128,64},{192,128},{8,192},{72,8},{136,72},{200,136... | collective-permute-start | bytes 1376264 | tf_op jit(solution)/shard_map/ppermute | solution.py:175
  64.1 16.5 %collective-permute-start.15 = (f32[64,1792]{1,0:T(8,128)}, f32[64,1792]{1,0:T(8,128)S(1)}, u32[]{:S(2)}, u32[]{:S(2)}) collective-permute-start(f32[64,1792]{1,0:T(8,128)} %collective-permute-done.6.refs_5_), channel_id=1, source_target_pairs={{0,64},{64,128},{128,192},{192,8},{8,72},{72,136},{136,200},{200,0... | collective-permute-start | bytes 1376264 | tf_op jit(solution)/shard_map/ppermute | solution.py:176
  68.2 20.5 %collective-permute-start.10 = (f32[64,1792]{1,0:T(8,128)}, f32[64,1792]{1,0:T(8,128)S(1)}, u32[]{:S(2)}, u32[]{:S(2)}) collective-permute-start(f32[64,1792]{1,0:T(8,128)} %collective-permute-done.9.refs_2_), channel_id=1, source_target_pairs={{0,64},{64,128},{128,192},{192,8},{8,72},{72,136},{136,200},{200,0... | collective-permute-start | bytes 1376264 | tf_op jit(solution)/shard_map/ppermute | solution.py:176
  70.3 18.5 %collective-permute-start.1 = (f32[64,1792]{1,0:T(8,128)S(1)}, f32[64,1792]{1,0:T(8,128)S(1)}, u32[]{:S(2)}, u32[]{:S(2)}) collective-permute-start(f32[64,1792]{1,0:T(8,128)S(1)} %bitcast.19), channel_id=1, source_target_pairs={{0,1},{1,0},{2,3},{3,2},{4,5},{5,4},{6,7},{7,6},{8,9},{9,8},{10,11... | collective-permute-start | bytes 1376264 | tf_op jit(solution)/shard_map/ppermute | solution.py:163
  77.0 19.2 %collective-permute-start.23 = (f32[64,1792]{1,0:T(8,128)S(1)}, f32[64,1792]{1,0:T(8,128)S(1)}, u32[]{:S(2)}, u32[]{:S(2)}) collective-permute-start(f32[64,1792]{1,0:T(8,128)S(1)} %collective-permute-done.14.refs_1_), channel_id=1, source_target_pairs={{0,200},{64,0},{128,64},{192,128},{8,192},{72,8},{136,72},{200,136... | collective-permute-start | bytes 1376264 | tf_op jit(solution)/shard_map/ppermute | solution.py:175
  80.6 18.0 %collective-permute-start.24 = (f32[64,1792]{1,0:T(8,128)S(1)}, f32[64,1792]{1,0:T(8,128)S(1)}, u32[]{:S(2)}, u32[]{:S(2)}) collective-permute-start(f32[64,1792]{1,0:T(8,128)S(1)} %collective-permute-done.15.refs_3_), channel_id=1, source_target_pairs={{0,64},{64,128},{128,192},{192,8},{8,72},{72,136},{136,200},{200,0... | collective-permute-start | bytes 1376264 | tf_op jit(solution)/shard_map/ppermute | solution.py:176
  88.8 13.5 %collective-permute-start.28 = (f32[32,1792]{1,0:T(8,128)S(1)}, f32[32,1792]{1,0:T(8,128)S(1)}, u32[]{:S(2)}, u32[]{:S(2)}) collective-permute-start(f32[32,1792]{1,0:T(8,128)S(1)} %slice.16), channel_id=1, source_target_pairs={{0,200},{64,0},{128,64},{192,128},{8,192},{72,8},{136,72},{200,136... | collective-permute-start | bytes 688136 | tf_op jit(solution)/shard_map/ppermute | solution.py:175
  88.8 15.0 %collective-permute-start.29 = (f32[32,1792]{1,0:T(8,128)S(1)}, f32[32,1792]{1,0:T(8,128)S(1)}, u32[]{:S(2)}, u32[]{:S(2)}) collective-permute-start(f32[32,1792]{1,0:T(8,128)S(1)} %slice.17), channel_id=1, source_target_pairs={{0,64},{64,128},{128,192},{192,8},{8,72},{72,136},{136,200},{200,0... | collective-permute-start | bytes 688136 | tf_op jit(solution)/shard_map/ppermute | solution.py:176
  94.7 9.8 %collective-permute-start.16 = (f32[256,128]{1,0:T(8,128)S(1)}, f32[256,128]{1,0:T(8,128)S(1)}, u32[]{:S(2)}, u32[]{:S(2)}) collective-permute-start(f32[256,128]{1,0:T(8,128)S(1)} %get-tuple-element.45), channel_id=1, source_target_pairs={{0,16},{16,32},{32,48},{48,0},{1,17},{17,33},{33,49},{49,1},{2,18}... | collective-permute-start | bytes 393224 | tf_op jit(solution)/shard_map/ppermute | solution.py:88
  96.2 17.3 %collective-permute-start.30 = (f32[32,1792]{1,0:T(8,128)S(1)}, f32[32,1792]{1,0:T(8,128)S(1)}, u32[]{:S(2)}, u32[]{:S(2)}) collective-permute-start(f32[32,1792]{1,0:T(8,128)S(1)} %slice.18), channel_id=1, source_target_pairs={{0,200},{64,0},{128,64},{192,128},{8,192},{72,8},{136,72},{200,136... | collective-permute-start | bytes 688136 | tf_op jit(solution)/shard_map/ppermute | solution.py:175
  98.6 10.2 %collective-permute-start.17 = (f32[256,128]{1,0:T(8,128)S(1)}, f32[256,128]{1,0:T(8,128)S(1)}, u32[]{:S(2)}, u32[]{:S(2)}) collective-permute-start(f32[256,128]{1,0:T(8,128)S(1)} %get-tuple-element.46), channel_id=1, source_target_pairs={{0,32},{16,48},{32,0},{48,16},{1,33},{17,49},{33,1},{49,17},{2,34}... | collective-permute-start | bytes 393224 | tf_op jit(solution)/shard_map/ppermute | solution.py:88
  103.8 7.9 %collective-permute-start.25 = (f32[256,128]{1,0:T(8,128)S(1)}, f32[256,128]{1,0:T(8,128)S(1)}, u32[]{:S(2)}, u32[]{:S(2)}) collective-permute-start(f32[256,128]{1,0:T(8,128)S(1)} %get-tuple-element.55), channel_id=1, source_target_pairs={{0,16},{16,32},{32,48},{48,0},{1,17},{17,33},{33,49},{49,1},{2,18}... | collective-permute-start | bytes 393224 | tf_op jit(solution)/shard_map/ppermute | solution.py:88
  104.4 9.4 %collective-permute-start.31 = (f32[32,1792]{1,0:T(8,128)S(1)}, f32[32,1792]{1,0:T(8,128)S(1)}, u32[]{:S(2)}, u32[]{:S(2)}) collective-permute-start(f32[32,1792]{1,0:T(8,128)S(1)} %slice.19), channel_id=1, source_target_pairs={{0,64},{64,128},{128,192},{192,8},{8,72},{72,136},{136,200},{200,0... | collective-permute-start | bytes 688136 | tf_op jit(solution)/shard_map/ppermute | solution.py:176
  108.8 10.0 %collective-permute-start.11 = (f32[384,128]{1,0:T(8,128)S(1)}, f32[384,128]{1,0:T(8,128)S(1)}, u32[]{:S(2)}, u32[]{:S(2)}) collective-permute-start(f32[384,128]{1,0:T(8,128)S(1)} %get-tuple-element.41), channel_id=1, source_target_pairs={{0,16},{16,32},{32,48},{48,0},{1,17},{17,33},{33,49},{49,1},{2,18}... | collective-permute-start | bytes 589832 | tf_op jit(solution)/shard_map/ppermute | solution.py:88
  108.9 12.6 %collective-permute-start.12 = (f32[384,128]{1,0:T(8,128)S(1)}, f32[384,128]{1,0:T(8,128)S(1)}, u32[]{:S(2)}, u32[]{:S(2)}) collective-permute-start(f32[384,128]{1,0:T(8,128)S(1)} %get-tuple-element.42), channel_id=1, source_target_pairs={{0,32},{16,48},{32,0},{48,16},{1,33},{17,49},{33,1},{49,17},{2,34}... | collective-permute-start | bytes 589832 | tf_op jit(solution)/shard_map/ppermute | solution.py:88
  111.8 10.5 %collective-permute-start.13 = (f32[384,128]{1,0:T(8,128)S(1)}, f32[384,128]{1,0:T(8,128)S(1)}, u32[]{:S(2)}, u32[]{:S(2)}) collective-permute-start(f32[384,128]{1,0:T(8,128)S(1)} %get-tuple-element.43), channel_id=1, source_target_pairs={{0,48},{16,0},{32,16},{48,32},{1,49},{17,1},{33,17},{49,33},{2,50}... | collective-permute-start | bytes 589832 | tf_op jit(solution)/shard_map/ppermute | solution.py:88
  113.6 11.2 %collective-permute-start.26 = (f32[256,128]{1,0:T(8,128)S(1)}, f32[256,128]{1,0:T(8,128)S(1)}, u32[]{:S(2)}, u32[]{:S(2)}) collective-permute-start(f32[256,128]{1,0:T(8,128)S(1)} %get-tuple-element.56), channel_id=1, source_target_pairs={{0,32},{16,48},{32,0},{48,16},{1,33},{17,49},{33,1},{49,17},{2,34}... | collective-permute-start | bytes 393224 | tf_op jit(solution)/shard_map/ppermute | solution.py:88
  113.8 13.1 %collective-permute-start.27 = (f32[256,128]{1,0:T(8,128)S(1)}, f32[256,128]{1,0:T(8,128)S(1)}, u32[]{:S(2)}, u32[]{:S(2)}) collective-permute-start(f32[256,128]{1,0:T(8,128)S(1)} %get-tuple-element.57), channel_id=1, source_target_pairs={{0,48},{16,0},{32,16},{48,32},{1,49},{17,1},{33,17},{49,33},{2,50}... | collective-permute-start | bytes 393224 | tf_op jit(solution)/shard_map/ppermute | solution.py:88
  118.8 10.5 %collective-permute-start.32 = (f32[128,128]{1,0:T(8,128)S(1)}, f32[128,128]{1,0:T(8,128)S(1)}, u32[]{:S(2)}, u32[]{:S(2)}) collective-permute-start(f32[128,128]{1,0:T(8,128)S(1)} %get-tuple-element.59), channel_id=1, source_target_pairs={{0,16},{16,32},{32,48},{48,0},{1,17},{17,33},{33,49},{49,1},{2,18}... | collective-permute-start | bytes 196616 | tf_op jit(solution)/shard_map/ppermute | solution.py:88
  121.4 9.5 %collective-permute-start.33 = (f32[128,128]{1,0:T(8,128)S(1)}, f32[128,128]{1,0:T(8,128)S(1)}, u32[]{:S(2)}, u32[]{:S(2)}) collective-permute-start(f32[128,128]{1,0:T(8,128)S(1)} %get-tuple-element.60), channel_id=1, source_target_pairs={{0,32},{16,48},{32,0},{48,16},{1,33},{17,49},{33,1},{49,17},{2,34}... | collective-permute-start | bytes 196616 | tf_op jit(solution)/shard_map/ppermute | solution.py:88
  122.3 8.6 %collective-permute-start.34 = (f32[128,128]{1,0:T(8,128)S(1)}, f32[128,128]{1,0:T(8,128)S(1)}, u32[]{:S(2)}, u32[]{:S(2)}) collective-permute-start(f32[128,128]{1,0:T(8,128)S(1)} %get-tuple-element.61), channel_id=1, source_target_pairs={{0,48},{16,0},{32,16},{48,32},{1,49},{17,1},{33,17},{49,33},{2,50}... | collective-permute-start | bytes 196616 | tf_op jit(solution)/shard_map/ppermute | solution.py:88
  126.9 8.2 %collective-permute-start.20 = (f32[128,128]{1,0:T(8,128)S(1)}, f32[128,128]{1,0:T(8,128)S(1)}, u32[]{:S(2)}, u32[]{:S(2)}) collective-permute-start(f32[128,128]{1,0:T(8,128)S(1)} %get-tuple-element.50), channel_id=1, source_target_pairs={{0,4},{2,6},{4,0},{6,2},{1,5},{3,7},{5,1},{7,3},{8,12},{10,14},{12... | collective-permute-start | bytes 196616 | tf_op jit(solution)/shard_map/ppermute | solution.py:117
  (11 other events, 67.3 us)
